TPU v7x, 512 devices: a whole 4x4x16 slice. The times are simulated.
512 devices in a mesh: fsdp: 32 (over z, x_hi), pipe: 2 (over core), dp: 8 (over x_lo, y).
Axes of the slice: x: 4 (x_hi: 2, x_lo: 2; x = x_hi * 2 + x_lo), y: 4, z: 16, core: 2. Of those that a mesh axis runs over, the one named last changes fastest.
Arguments:
- video_tokens: bfloat16 [8, 4096, 2560], P('dp', 'fsdp'), may hold values from -6 to 6
- cached_out: bfloat16 [2, 8, 4096, 2560], P('pipe', 'dp', 'fsdp'), may hold values from -6 to 6
- fresh_mask: int32 [2, 8, 4096], P('pipe', 'dp', 'fsdp'), may hold values from 0 to 1, as said below
- timestep: int32 [8], P('dp'), may hold values from 0 to 49
- up_weight: bfloat16 [2, 7168, 2560], P('pipe', 'fsdp'), may hold values from -0.125 to 0.125
- down_weight: bfloat16 [2, 7168, 2560], P('pipe', 'fsdp'), may hold values from -0.0625 to 0.0625
- router_in: bfloat16 [2, 2560, 256], P('pipe', 'fsdp'), may hold values from -0.125 to 0.125
- router_bias: float32 [2, 50, 256], P('pipe'), may hold values from -6 to 6
- router_out: float32 [2, 256], P('pipe'), may hold values from -0.375 to 0.375
- out_cotangent: bfloat16 [8, 4096, 2560], P('dp', 'fsdp'), may hold values from -0.119628906 to 0.119628906
Outputs:
- blended: bfloat16 [2, 8, 4096, 2560], P('pipe', 'dp', 'fsdp')
- grad_router_in: float32 [2, 2560, 256], P('pipe', 'fsdp')
- grad_router_bias: float32 [2, 50, 256], P('pipe')
- grad_router_out: float32 [2, 256], P('pipe')
Inputs may be any that keep to these rules, and one draw needn't show every extreme that they name: `fresh_mask`: for each section and video, the 128 consecutive tokens of one index of fsdp hold 1 to 2 ones, and some index holds exactly 2.
All inputs are finite; a program needn't handle non-finite values.
Results may differ from a plain program's by a relative error of at most 0.023.
Values may be sent and summed in bfloat16 or wider, within the bound.
No kernel may reach another device: no remote copies, remote signals or barrier semaphores. Data moves between devices by JAX's collectives and lax.ppermute only.
A program may use at most 64 MiB of HBM per device.

v0:
```python
import jax
import jax.numpy as jnp
from jax import lax
from jax.sharding import Mesh
from jax.sharding import PartitionSpec as P

FRESH = 2
FSDP = ("fsdp_0", "fsdp_1")


layer_eps = 1e-06
gelu_scale = 0.7978845608028654
gelu_cubic = 0.044715


def laid_out(blocks, dim):
    lengths = list(blocks.shape[1:])
    lengths[dim] *= blocks.shape[0]
    return jnp.moveaxis(blocks, 0, dim).reshape(lengths)


def from_everyone(value, axis):
    copies = jnp.broadcast_to(value, (lax.axis_size(axis), *value.shape))
    return lax.all_to_all(copies, axis, split_axis=0, concat_axis=0, tiled=True)


def gathered_copies(value, axis, dim):
    return laid_out(from_everyone(value, axis), dim)


def whole_of(value, axes, dim):
    if not axes:
        return value
    nearer = lax.all_gather(value, axes[-1], axis=dim, tiled=True)
    return whole_of(nearer, axes[:-1], dim)


def cut_along(value, dim, count):
    before, after = (value.shape[:dim], value.shape[dim + 1 :])
    return jnp.moveaxis(value.reshape(*before, count, -1, *after), dim, 0)


def summed_on_arrival(value, axis, dim):
    blocks = cut_along(value, dim, lax.axis_size(axis))
    arrived = lax.all_to_all(blocks, axis, split_axis=0, concat_axis=0, tiled=True)
    return arrived.astype(jnp.float32).sum(axis=0)


def taken_together(value, axis):
    return from_everyone(value, axis).astype(jnp.float32).sum(axis=0)


def from_behind(block, axis, distance):
    devices = range(lax.axis_size(axis))
    route = [(i - distance, i) for i in devices if i - distance in devices]
    return lax.ppermute(block, axis, route)


def for_sending(value):
    return jax.tree.map(lambda a: a.astype(jnp.bfloat16) if a.dtype == jnp.float32 else a, value)


def gelu_tanh(values):
    inner_arg = gelu_scale * (values + gelu_cubic * values * values * values)
    return 0.5 * values * (1.0 + jnp.tanh(inner_arg))


def gelu_slope(values):
    inner_arg = gelu_scale * (values + gelu_cubic * values * values * values)
    tanh_val = jnp.tanh(inner_arg)
    return 0.5 * (1.0 + tanh_val) + 0.5 * values * (1.0 - tanh_val * tanh_val) * gelu_scale * (
        1.0 + 3.0 * gelu_cubic * values * values
    )


def normalize(inputs):
    values = inputs.astype(jnp.float32)
    center = values - jnp.mean(values, axis=1, keepdims=True)
    inv_std = lax.rsqrt(jnp.mean(center * center, axis=1, keepdims=True) + layer_eps)
    return (center * inv_std, inv_std)


def normalize_back(scaled, inv_std, grads):
    return inv_std * (
        grads
        - jnp.mean(grads, axis=1, keepdims=True)
        - scaled * jnp.mean(grads * scaled, axis=1, keepdims=True)
    )


def contract_last(left, right):
    return lax.dot_general(
        left, right, (((1,), (1,)), ((), ())), preferred_element_type=jnp.float32
    )


def contract_first(left, right):
    return lax.dot_general(
        left, right, (((0,), (0,)), ((), ())), preferred_element_type=jnp.float32
    )


def gather_gate(gate_grad):
    return gathered_copies(gate_grad, FSDP, 0)


def body(
    video_tokens,
    cached_out,
    fresh_mask,
    timestep,
    up_weight,
    down_weight,
    router_in,
    router_bias,
    router_out,
    out_cotangent,
):
    section_id = lax.axis_index("pipe")
    column_slot = lax.axis_index(FSDP)
    inputs_first = video_tokens[0]
    cached = cached_out[0, 0]
    mask_row = fresh_mask[0, 0]
    w_up = up_weight[0]
    w_down = down_weight[0]
    r_in = router_in[0]
    r_out = router_out[0]
    tok_rows = inputs_first.shape[0]
    shard_cols = r_in.shape[0]
    hot_step = (jnp.arange(router_bias.shape[1]) == timestep[0]).astype(jnp.float32)
    bias_row = jnp.dot(hot_step, router_bias[0])
    picked = jnp.argsort(1 - mask_row, stable=True)[:FRESH]
    live_rows = (jnp.arange(FRESH) < jnp.sum(mask_row)).astype(jnp.float32)

    def select(values):
        return jnp.take(values, picked, axis=0)

    def spread(values):
        return jnp.zeros((tok_rows, values.shape[1]), values.dtype).at[picked].add(values)

    def forward(inputs):
        rows_in = select(inputs)
        rows_cached = select(cached).astype(jnp.float32)
        scaled, inv_std = normalize(rows_in)
        normed = scaled.astype(jnp.bfloat16)
        row_count = normed.shape[0]
        gathered = whole_of(normed, FSDP, 0)
        pre_act = contract_last(gathered, w_up)
        hid_act = gelu_tanh(pre_act).astype(jnp.bfloat16)
        block_sum = summed_on_arrival(
            jnp.dot(hid_act, w_down, preferred_element_type=jnp.float32).astype(jnp.bfloat16),
            FSDP,
            0,
        )
        columns = lax.dynamic_slice_in_dim(gathered, column_slot * shard_cols, shard_cols, 1)
        router_part = jnp.dot(columns, r_in, preferred_element_type=jnp.float32)
        router_pre = (
            taken_together(router_part.astype(jnp.bfloat16), FSDP).astype(jnp.float32)
            + bias_row[None, :]
        )
        gate_all = jax.nn.sigmoid(jnp.dot(gelu_tanh(router_pre), r_out))
        gate_own = lax.dynamic_slice_in_dim(gate_all, column_slot * row_count, row_count, 0)
        fresh_out = rows_in.astype(jnp.float32) + block_sum
        delta_rows = live_rows[:, None] * gate_own[:, None] * (fresh_out - rows_cached)
        blended = (cached.astype(jnp.float32) + spread(delta_rows)).astype(jnp.bfloat16)
        stored = (
            scaled,
            inv_std,
            columns,
            pre_act,
            router_pre,
            gate_all,
            gate_own,
            fresh_out,
            rows_cached,
        )
        return (blended, stored)

    def local_grads(stored, cot_rows):
        gate_own = stored[6]
        fresh_out = stored[7]
        rows_cached = stored[8]
        gate_grad = jnp.sum(cot_rows * live_rows[:, None] * (fresh_out - rows_cached), axis=1)
        fresh_grad = cot_rows * (live_rows * gate_own)[:, None]
        return (gate_grad, fresh_grad)

    def router_grads(stored, gate_all_grad):
        columns = stored[2]
        router_pre = stored[4]
        gate_all = stored[5]
        logit_grad = gate_all_grad * gate_all * (1.0 - gate_all)
        out_grad = jnp.dot(logit_grad, gelu_tanh(router_pre))
        hidden_grad = logit_grad[:, None] * r_out[None, :] * gelu_slope(router_pre)
        hidden_b = hidden_grad.astype(jnp.bfloat16)
        in_grad = contract_first(columns, hidden_b)
        bias_grad = hot_step[:, None] * jnp.sum(hidden_grad, axis=0)[None, :]
        return (hidden_b, (in_grad, bias_grad, out_grad))

    blended_first, stored_first = forward(inputs_first)
    arriving = from_behind(blended_first, "pipe", 1)
    inputs_second = jnp.where(section_id == 1, arriving, inputs_first)
    blended_out, stored = forward(inputs_second)
    cot_second = select(out_cotangent[0]).astype(jnp.float32)
    gate_grad, fresh_grad = local_grads(stored, cot_second)
    hidden_b, grads_second = router_grads(stored, gather_gate(gate_grad))
    fresh_rows = gathered_copies(fresh_grad.astype(jnp.bfloat16), FSDP, 0)
    act_grad = contract_last(fresh_rows, w_down)
    pre_grad = (act_grad * gelu_slope(stored[3])).astype(jnp.bfloat16)
    row_count = fresh_grad.shape[0]
    total_rows = jnp.dot(pre_grad, w_up, preferred_element_type=jnp.float32)
    router_term = contract_last(hidden_b, r_in)
    current = lax.dynamic_slice_in_dim(total_rows, column_slot * shard_cols, shard_cols, 1)
    normed_grad = summed_on_arrival(
        lax.dynamic_update_slice_in_dim(
            total_rows, current + router_term, column_slot * shard_cols, 1
        ).astype(jnp.bfloat16),
        FSDP,
        0,
    )
    input_grad = fresh_grad + normalize_back(stored[0], stored[1], normed_grad)
    positions = picked.astype(jnp.float32)
    got_rows, got_positions = from_behind((input_grad, positions), "pipe", -1)
    returning = (
        jnp.zeros((tok_rows, input_grad.shape[1]), jnp.float32)
        .at[got_positions.astype(jnp.int32)]
        .add(got_rows)
    )
    gate_grad_first, unused_grad = local_grads(stored, select(returning))
    unused_hidden, grads_first = router_grads(stored, gather_gate(gate_grad_first))
    chosen = tuple(
        (
            jnp.where(section_id == 1, second_grad, first_grad)
            for second_grad, first_grad in zip(grads_second, grads_first)
        )
    )
    summed = jax.tree.map(
        lambda part: part.astype(jnp.float32),
        jax.tree.map(lambda part: taken_together(part, "dp"), for_sending(chosen)),
    )
    return (blended_out[None, None], summed[0][None], summed[1][None], summed[2][None])


def solution(mesh):
    torus = Mesh(
        mesh.devices.reshape(16, 2, mesh.shape["pipe"], mesh.shape["dp"]),
        ("fsdp_0", "fsdp_1", "pipe", "dp"),
    )
    return jax.shard_map(
        body,
        mesh=torus,
        in_specs=(
            P("dp", FSDP, None),
            P("pipe", "dp", FSDP, None),
            P("pipe", "dp", FSDP),
            P("dp"),
            P("pipe", FSDP, None),
            P("pipe", FSDP, None),
            P("pipe", FSDP, None),
            P("pipe", None, None),
            P("pipe", None),
            P("dp", FSDP, None),
        ),
        out_specs=(
            P("pipe", "dp", FSDP, None),
            P("pipe", FSDP, None),
            P("pipe", None, None),
            P("pipe", None),
        ),
        check_vma=False,
    )
```

profile of v0, /device:TPU:2, one launch (start us, length us, event | category | flops | bytes accessed | tf_op | source)
XLA Modules:
  0.0 396.6 jit_solution(14139143115911641954)
XLA Ops:
  2.2 2.5 sort.17
  4.8 1.8 gather_fusion.1
  7.0 5.9 %all-gather = bf16[2,2,2560]{2,1,0:T(2,128)(2,1)S(1)} all-gather(bf16[1,2,2560]{2,1,0:T(2,128)(2,1)S(1)} %fusion.120), channel_id=1, replica_groups=mesh['fsdp_0'=16,'fsdp_1'=2,'pipe'=2,'dp'=8] {'fsdp_1'}, dimensions={0}, use_global_device_ids=true | all-gather | bytes 30720 | tf_op jit(solution)/shard_map/all_gather | solution.py:34
  12.9 37.1 %all-gather.1 = bf16[16,4,2560]{2,1,0:T(4,128)(2,1)S(1)} all-gather(bf16[1,4,2560]{2,1,0:T(4,128)(2,1)S(1)} %reshape.185), channel_id=1, replica_groups=mesh['fsdp_0'=16,'fsdp_1'=2,'pipe'=2,'dp'=8] {'fsdp_0'}, dimensions={0}, use_global_device_ids=true | all-gather | bytes 348160 | tf_op jit(solution)/shard_map/all_gather | solution.py:34
  52.1 8.9 %all-to-all-start.1 = ((bf16[32,2,2560]{2,1,0:T(2,128)(2,1)}), bf16[32,2,2560]{2,1,0:T(2,128)(2,1)S(1)}, u32[]{:S(2)}, u32[]{:S(2)}) async-start(bf16[32,2,2560]{2,1,0:T(2,128)(2,1)} %reshape.105), calls=%async_computation.1 | async-start | bytes 655360 | tf_op jit(solution)/shard_map/all_to_all | solution.py:45
  61.2 19.0 %all-to-all-done.1 = bf16[32,2,2560]{2,1,0:T(2,128)(2,1)S(1)} async-done(((bf16[32,2,2560]{2,1,0:T(2,128)(2,1)}), bf16[32,2,2560]{2,1,0:T(2,128)(2,1)S(1)}, u32[]{:S(2)}, u32[]{:S(2)}) %all-to-all-start.1) | async-done | bytes 327712 | tf_op jit(solution)/shard_map/all_to_all | solution.py:45
  81.4 4.6 %all-to-all-start = ((bf16[32,64,256]{2,1,0:T(8,128)(2,1)}), bf16[32,64,256]{2,1,0:T(8,128)(2,1)S(1)}, u32[]{:S(2)}, u32[]{:S(2)}) async-start(bf16[32,64,256]{2,1,0:T(8,128)(2,1)} %broadcast_in_dim.84), calls=%async_computation | async-start | bytes 2097152 | tf_op jit(solution)/shard_map/all_to_all | solution.py:24
  86.6 1.8 gather_fusion.2
  93.4 38.3 %all-to-all-done = bf16[32,64,256]{2,1,0:T(8,128)(2,1)S(1)} async-done(((bf16[32,64,256]{2,1,0:T(8,128)(2,1)}), bf16[32,64,256]{2,1,0:T(8,128)(2,1)S(1)}, u32[]{:S(2)}, u32[]{:S(2)}) %all-to-all-start) | async-done | bytes 1048608 | tf_op jit(solution)/shard_map/all_to_all | solution.py:24
  135.7 2.2 collective-permute-start
  142.3 5.9 %all-gather.2 = bf16[2,2,2560]{2,1,0:T(2,128)(2,1)S(1)} all-gather(bf16[1,2,2560]{2,1,0:T(2,128)(2,1)S(1)} %fusion.119), channel_id=1, replica_groups=mesh['fsdp_0'=16,'fsdp_1'=2,'pipe'=2,'dp'=8] {'fsdp_1'}, dimensions={0}, use_global_device_ids=true | all-gather | bytes 30720 | tf_op jit(solution)/shard_map/all_gather | solution.py:34
  148.2 28.0 %all-gather.3 = bf16[16,4,2560]{2,1,0:T(4,128)(2,1)S(1)} all-gather(bf16[1,4,2560]{2,1,0:T(4,128)(2,1)S(1)} %reshape.189), channel_id=1, replica_groups=mesh['fsdp_0'=16,'fsdp_1'=2,'pipe'=2,'dp'=8] {'fsdp_0'}, dimensions={0}, use_global_device_ids=true | all-gather | bytes 348160 | tf_op jit(solution)/shard_map/all_gather | solution.py:34
  178.0 7.3 %all-to-all-start.3 = ((bf16[32,2,2560]{2,1,0:T(2,128)(2,1)}), bf16[32,2,2560]{2,1,0:T(2,128)(2,1)S(1)}, u32[]{:S(2)}, u32[]{:S(2)}) async-start(bf16[32,2,2560]{2,1,0:T(2,128)(2,1)} %reshape.106), calls=%async_computation.3 | async-start | bytes 655360 | tf_op jit(solution)/shard_map/all_to_all | solution.py:45
  185.5 18.8 %all-to-all-done.3 = bf16[32,2,2560]{2,1,0:T(2,128)(2,1)S(1)} async-done(((bf16[32,2,2560]{2,1,0:T(2,128)(2,1)}), bf16[32,2,2560]{2,1,0:T(2,128)(2,1)S(1)}, u32[]{:S(2)}, u32[]{:S(2)}) %all-to-all-start.3) | async-done | bytes 327712 | tf_op jit(solution)/shard_map/all_to_all | solution.py:45
  205.5 4.9 %all-to-all-start.2 = ((bf16[32,64,256]{2,1,0:T(8,128)(2,1)}), bf16[32,64,256]{2,1,0:T(8,128)(2,1)S(1)}, u32[]{:S(2)}, u32[]{:S(2)}) async-start(bf16[32,64,256]{2,1,0:T(8,128)(2,1)} %broadcast_in_dim.85), calls=%async_computation.2 | async-start | bytes 2097152 | tf_op jit(solution)/shard_map/all_to_all | solution.py:24
  210.4 1.9 gather_fusion.4
  214.8 43.1 %all-to-all-done.2 = bf16[32,64,256]{2,1,0:T(8,128)(2,1)S(1)} async-done(((bf16[32,64,256]{2,1,0:T(8,128)(2,1)}), bf16[32,64,256]{2,1,0:T(8,128)(2,1)S(1)}, u32[]{:S(2)}, u32[]{:S(2)}) %all-to-all-start.2) | async-done | bytes 1048608 | tf_op jit(solution)/shard_map/all_to_all | solution.py:24
  259.9 19.6 %all_to_all.58 = f32[32,1,2]{2,1,0:T(1,128)S(1)} all-to-all(f32[32,1,2]{2,1,0:T(1,128)S(1)} %broadcast_in_dim.87), channel_id=1, replica_groups=mesh['fsdp_0'=16,'fsdp_1'=2,'pipe'=2,'dp'=8] {'fsdp_0','fsdp_1'}, dimensions={0} | all-to-all | bytes 512 | tf_op jit(solution)/shard_map/all_to_all | solution.py:24
  280.4 3.9 all-to-all-start.5
  286.2 17.2 %all-to-all-done.5 = bf16[32,2,2560]{2,1,0:T(2,128)(2,1)S(1)} async-done(((bf16[32,2,2560]{2,1,0:T(2,128)(2,1)}), bf16[32,2,2560]{2,1,0:T(2,128)(2,1)S(1)}, u32[]{:S(2)}, u32[]{:S(2)}) %all-to-all-start.5) | async-done | bytes 327712 | tf_op jit(solution)/shard_map/all_to_all | solution.py:24
  307.1 5.0 %all-to-all-start.6 = ((bf16[32,2,2560]{2,1,0:T(2,128)(2,1)}), bf16[32,2,2560]{2,1,0:T(2,128)(2,1)S(1)}, u32[]{:S(2)}, u32[]{:S(2)}) async-start(bf16[32,2,2560]{2,1,0:T(2,128)(2,1)} %reshape.109), calls=%async_computation.6 | async-start | bytes 655360 | tf_op jit(solution)/shard_map/all_to_all | solution.py:45
  313.5 1.7 collective-permute-done.1
  316.6 14.7 %all-to-all-done.6 = bf16[32,2,2560]{2,1,0:T(2,128)(2,1)S(1)} async-done(((bf16[32,2,2560]{2,1,0:T(2,128)(2,1)}), bf16[32,2,2560]{2,1,0:T(2,128)(2,1)S(1)}, u32[]{:S(2)}, u32[]{:S(2)}) %all-to-all-start.6) | async-done | bytes 327712 | tf_op jit(solution)/shard_map/all_to_all | solution.py:45
  337.3 2.0 gather_fusion
  340.2 4.7 %all-to-all-start.7 = ((f32[32,1,2]{2,1,0:T(1,128)}), f32[32,1,2]{2,1,0:T(1,128)S(1)}, u32[]{:S(2)}, u32[]{:S(2)}) async-start(f32[32,1,2]{2,1,0:T(1,128)} %broadcast_in_dim.92), calls=%async_computation.7 | async-start | bytes 32768 | tf_op jit(solution)/shard_map/all_to_all | solution.py:24
  345.0 14.5 %all-to-all-done.7 = f32[32,1,2]{2,1,0:T(1,128)S(1)} async-done(((f32[32,1,2]{2,1,0:T(1,128)}), f32[32,1,2]{2,1,0:T(1,128)S(1)}, u32[]{:S(2)}, u32[]{:S(2)}) %all-to-all-start.7) | async-done | bytes 288 | tf_op jit(solution)/shard_map/all_to_all | solution.py:24
  362.4 5.9 %all-to-all-start.10 = ((bf16[8,2,128]{2,1,0:T(2,128)(2,1)}), bf16[8,2,128]{2,1,0:T(2,128)(2,1)S(1)}, u32[]{:S(2)}, u32[]{:S(2)}) async-start(bf16[8,2,128]{2,1,0:T(2,128)(2,1)} %reshape.233), calls=%async_computation.10 | async-start | bytes 8192 | tf_op jit(solution)/shard_map/all_to_all | solution.py:24
  368.4 4.6 %all-to-all-done.10 = bf16[8,2,128]{2,1,0:T(2,128)(2,1)S(1)} async-done(((bf16[8,2,128]{2,1,0:T(2,128)(2,1)}), bf16[8,2,128]{2,1,0:T(2,128)(2,1)S(1)}, u32[]{:S(2)}, u32[]{:S(2)}) %all-to-all-start.10) | async-done | bytes 4128 | tf_op jit(solution)/shard_map/all_to_all | solution.py:24
  373.7 4.8 %all-to-all-start.9 = ((bf16[8,50,256]{2,1,0:T(8,128)(2,1)}), bf16[8,50,256]{2,1,0:T(8,128)(2,1)S(1)}, u32[]{:S(2)}, u32[]{:S(2)}) async-start(bf16[8,50,256]{2,1,0:T(8,128)(2,1)} %broadcast_in_dim.95), calls=%async_computation.9 | async-start | bytes 458752 | tf_op jit(solution)/shard_map/all_to_all | solution.py:24
  379.5 4.7 %all-to-all-done.9 = bf16[8,50,256]{2,1,0:T(8,128)(2,1)S(1)} async-done(((bf16[8,50,256]{2,1,0:T(8,128)(2,1)}), bf16[8,50,256]{2,1,0:T(8,128)(2,1)S(1)}, u32[]{:S(2)}, u32[]{:S(2)}) %all-to-all-start.9) | async-done | bytes 204832 | tf_op jit(solution)/shard_map/all_to_all | solution.py:24
  384.9 4.8 %all-to-all-start.8 = ((bf16[8,80,256]{2,1,0:T(8,128)(2,1)}), bf16[8,80,256]{2,1,0:T(8,128)(2,1)S(1)}, u32[]{:S(2)}, u32[]{:S(2)}) async-start(bf16[8,80,256]{2,1,0:T(8,128)(2,1)} %broadcast_in_dim.93), calls=%async_computation.8 | async-start | bytes 655360 | tf_op jit(solution)/shard_map/all_to_all | solution.py:24
  392.0 3.9 all-to-all-done.8
  (159 shorter events, 50.7 us)
Async XLA Ops:
  0.6 49.5 %copy-start = (bf16[1,224,2560]{2,1,0:T(8,128)(2,1)S(1)}, bf16[1,224,2560]{2,1,0:T(8,128)(2,1)}, u32[]{:S(2)}) copy-start(bf16[1,224,2560]{2,1,0:T(8,128)(2,1)} %param.17) | copy-start | bytes 3440644
  0.6 49.5 %copy-start.1 = (bf16[1,224,2560]{2,1,0:T(8,128)(2,1)S(1)}, bf16[1,224,2560]{2,1,0:T(8,128)(2,1)}, u32[]{:S(2)}) copy-start(bf16[1,224,2560]{2,1,0:T(8,128)(2,1)} %param.16) | copy-start | bytes 3440644
  4.7 46.5 %copy-start.28 = (s32[2]{0:T(128)}, s32[2]{0:T(128)S(1)}, u32[]{:S(2)}) copy-start(s32[2]{0:T(128)S(1)} %get-tuple-element.30) | copy-start | bytes 28
  4.7 81.9 %copy-start.13 = (s32[1024]{0:T(1024)}, s32[1024]{0:T(1024)S(1)}, u32[]{:S(2)}) copy-start(s32[1024]{0:T(1024)S(1)} %pad_clamp_fusion) | copy-start | bytes 12292
  52.1 28.2 %all-to-all-start.1 = ((bf16[32,2,2560]{2,1,0:T(2,128)(2,1)}), bf16[32,2,2560]{2,1,0:T(2,128)(2,1)S(1)}, u32[]{:S(2)}, u32[]{:S(2)}) async-start(bf16[32,2,2560]{2,1,0:T(2,128)(2,1)} %reshape.105), calls=%async_computation.1 | async-start | bytes 655360 | tf_op jit(solution)/shard_map/all_to_all | solution.py:45
  81.4 50.3 %all-to-all-start = ((bf16[32,64,256]{2,1,0:T(8,128)(2,1)}), bf16[32,64,256]{2,1,0:T(8,128)(2,1)S(1)}, u32[]{:S(2)}, u32[]{:S(2)}) async-start(bf16[32,64,256]{2,1,0:T(8,128)(2,1)} %broadcast_in_dim.84), calls=%async_computation | async-start | bytes 2097152 | tf_op jit(solution)/shard_map/all_to_all | solution.py:24
  135.7 3.3 collective-permute-start
  137.9 38.4 %copy-start.2 = (bf16[1,224,2560]{2,1,0:T(8,128)(2,1)S(1)}, bf16[1,224,2560]{2,1,0:T(8,128)(2,1)}, u32[]{:S(2)}) copy-start(bf16[1,224,2560]{2,1,0:T(8,128)(2,1)} %param.16) | copy-start | bytes 3440644
  178.0 26.4 %all-to-all-start.3 = ((bf16[32,2,2560]{2,1,0:T(2,128)(2,1)}), bf16[32,2,2560]{2,1,0:T(2,128)(2,1)S(1)}, u32[]{:S(2)}, u32[]{:S(2)}) async-start(bf16[32,2,2560]{2,1,0:T(2,128)(2,1)} %reshape.106), calls=%async_computation.3 | async-start | bytes 655360 | tf_op jit(solution)/shard_map/all_to_all | solution.py:45
  205.5 52.6 %copy-start.20 = (f32[1,256]{1,0:T(1,128)S(1)}, f32[1,256]{1,0:T(1,128)}, u32[]{:S(2)}) copy-start(f32[1,256]{1,0:T(1,128)} %fusion.67) | copy-start | bytes 3076
  205.5 52.6 %copy-start.24 = (f32[1,256]{1,0:T(1,128)S(1)}, f32[1,256]{1,0:T(1,128)}, u32[]{:S(2)}) copy-start(f32[1,256]{1,0:T(1,128)} %param.20) | copy-start | bytes 3076
  205.5 52.4 %all-to-all-start.2 = ((bf16[32,64,256]{2,1,0:T(8,128)(2,1)}), bf16[32,64,256]{2,1,0:T(8,128)(2,1)S(1)}, u32[]{:S(2)}, u32[]{:S(2)}) async-start(bf16[32,64,256]{2,1,0:T(8,128)(2,1)} %broadcast_in_dim.85), calls=%async_computation.2 | async-start | bytes 2097152 | tf_op jit(solution)/shard_map/all_to_all | solution.py:24
  212.3 68.1 %copy-start.11 = (bf16[2,2560]{1,0:T(2,128)(2,1)}, bf16[2,2560]{1,0:T(2,128)(2,1)S(1)}, u32[]{:S(2)}) copy-start(bf16[2,2560]{1,0:T(2,128)(2,1)S(1)} %gather_fusion.4) | copy-start | bytes 30724
  258.1 28.2 %copy-start.7 = (f32[64,256]{1,0:T(8,128)}, f32[64,256]{1,0:T(8,128)S(1)}, u32[]{:S(2)}) copy-start(f32[64,256]{1,0:T(8,128)S(1)} %convert_reduce_fusion) | copy-start | bytes 196612
  258.2 45.2 %copy-start.29 = (f32[64]{0:T(128)}, f32[64]{0:T(128)S(1)}, u32[]{:S(2)}) copy-start(f32[64]{0:T(128)S(1)} %fusion.24) | copy-start | bytes 772
  280.4 23.0 %all-to-all-start.5 = ((bf16[32,2,2560]{2,1,0:T(2,128)(2,1)}), bf16[32,2,2560]{2,1,0:T(2,128)(2,1)S(1)}, u32[]{:S(2)}, u32[]{:S(2)}) async-start(bf16[32,2,2560]{2,1,0:T(2,128)(2,1)} %broadcast_in_dim.90), calls=%async_computation.5 | async-start | bytes 655360 | tf_op jit(solution)/shard_map/all_to_all | solution.py:24
  307.1 25.1 %copy-start.17 = (f32[2]{0:T(128)S(1)}, f32[2]{0:T(128)}, u32[]{:S(2)}) copy-start(f32[2]{0:T(128)} %copy-done.16) | copy-start | bytes 28
  307.1 25.1 %copy-start.19 = (f32[2]{0:T(128)S(1)}, f32[2]{0:T(128)}, u32[]{:S(2)}) copy-start(f32[2]{0:T(128)} %copy-done.18) | copy-start | bytes 28
  307.1 25.3 %copy-start.12 = (bf16[2,2560]{1,0:T(2,128)(2,1)S(1)}, bf16[2,2560]{1,0:T(2,128)(2,1)}, u32[]{:S(2)}) copy-start(bf16[2,2560]{1,0:T(2,128)(2,1)} %copy-done.11) | copy-start | bytes 30724
  307.1 26.7 %copy-start.8 = (f32[64,256]{1,0:T(8,128)S(1)}, f32[64,256]{1,0:T(8,128)}, u32[]{:S(2)}) copy-start(f32[64,256]{1,0:T(8,128)} %copy-done.7) | copy-start | bytes 196612
  307.1 26.7 %copy-start.22 = (f32[1,256]{1,0:T(1,128)S(1)}, f32[1,256]{1,0:T(1,128)}, u32[]{:S(2)}) copy-start(f32[1,256]{1,0:T(1,128)} %fusion.67) | copy-start | bytes 3076
  307.1 26.7 %copy-start.26 = (f32[1,256]{1,0:T(1,128)S(1)}, f32[1,256]{1,0:T(1,128)}, u32[]{:S(2)}) copy-start(f32[1,256]{1,0:T(1,128)} %param.20) | copy-start | bytes 3076
  307.1 26.7 %copy-start.27 = (f32[64]{0:T(128)S(1)}, f32[64]{0:T(128)}, u32[]{:S(2)}) copy-start(f32[64]{0:T(128)} %multiply_multiply_fusion.5) | copy-start | bytes 772
  307.1 24.2 %all-to-all-start.6 = ((bf16[32,2,2560]{2,1,0:T(2,128)(2,1)}), bf16[32,2,2560]{2,1,0:T(2,128)(2,1)S(1)}, u32[]{:S(2)}, u32[]{:S(2)}) async-start(bf16[32,2,2560]{2,1,0:T(2,128)(2,1)} %reshape.109), calls=%async_computation.6 | async-start | bytes 655360 | tf_op jit(solution)/shard_map/all_to_all | solution.py:45
  312.2 3.1 collective-permute-start.1
  316.6 22.7 %copy-start.23 = (f32[2]{0:T(128)S(1)}, f32[2]{0:T(128)}, u32[]{:S(2)}) copy-start(f32[2]{0:T(128)} %fusion.134) | copy-start | bytes 28
  316.6 43.7 %copy-start.30 = (f32[64]{0:T(128)S(1)}, f32[64]{0:T(128)}, u32[]{:S(2)}) copy-start(f32[64]{0:T(128)} %copy-done.29) | copy-start | bytes 772
  332.5 3.1 collective-permute-start.2
  340.2 19.3 %all-to-all-start.7 = ((f32[32,1,2]{2,1,0:T(1,128)}), f32[32,1,2]{2,1,0:T(1,128)S(1)}, u32[]{:S(2)}, u32[]{:S(2)}) async-start(f32[32,1,2]{2,1,0:T(1,128)} %broadcast_in_dim.92), calls=%async_computation.7 | async-start | bytes 32768 | tf_op jit(solution)/shard_map/all_to_all | solution.py:24
  362.4 10.6 %all-to-all-start.10 = ((bf16[8,2,128]{2,1,0:T(2,128)(2,1)}), bf16[8,2,128]{2,1,0:T(2,128)(2,1)S(1)}, u32[]{:S(2)}, u32[]{:S(2)}) async-start(bf16[8,2,128]{2,1,0:T(2,128)(2,1)} %reshape.233), calls=%async_computation.10 | async-start | bytes 8192 | tf_op jit(solution)/shard_map/all_to_all | solution.py:24
  373.7 10.5 %all-to-all-start.9 = ((bf16[8,50,256]{2,1,0:T(8,128)(2,1)}), bf16[8,50,256]{2,1,0:T(8,128)(2,1)S(1)}, u32[]{:S(2)}, u32[]{:S(2)}) async-start(bf16[8,50,256]{2,1,0:T(8,128)(2,1)} %broadcast_in_dim.95), calls=%async_computation.9 | async-start | bytes 458752 | tf_op jit(solution)/shard_map/all_to_all | solution.py:24
  384.9 11.0 %all-to-all-start.8 = ((bf16[8,80,256]{2,1,0:T(8,128)(2,1)}), bf16[8,80,256]{2,1,0:T(8,128)(2,1)S(1)}, u32[]{:S(2)}, u32[]{:S(2)}) async-start(bf16[8,80,256]{2,1,0:T(8,128)(2,1)} %broadcast_in_dim.93), calls=%async_computation.8 | async-start | bytes 655360 | tf_op jit(solution)/shard_map/all_to_all | solution.py:24
  (14 other events, 64.4 us)
where the time goes:
time: 398 us; the launch traced here: 397 us
  waiting for transfers between devices  182 us (46%)
  blocking collectives  96.5 us (24%)
  starting transfers between devices  59.6 us (15%)
  other arithmetic  25.7 us (6%)
  local copies, waits for them, and re-layouts  21.3 us (5%)
  matrix products  9.16 us (2%)
    all_to_all x7, waiting for transfers between devices, from_everyone(): return lax.all_to_all(copies, axis, split_axis=0, concat_axis=0, tiled=True)  126 us
    all_gather x4, blocking collectives, whole_of(): nearer = lax.all_gather(value, axes[-1], axis=dim, tiled=True)  76.9 us
    all_to_all x3, waiting for transfers between devices, summed_on_arrival(): lax.all_to_all(blocks, axis, split_axis=0, concat_axis=0, tiled=True)  52.6 us
    all_to_all x7, starting transfers between devices, from_everyone(): return lax.all_to_all(copies, axis, split_axis=0, concat_axis=0, tiled=True)  33.6 us
    all_to_all x3, starting transfers between devices, summed_on_arrival(): lax.all_to_all(blocks, axis, split_axis=0, concat_axis=0, tiled=True)  21.3 us
    all_to_all x1, blocking collectives, from_everyone(): return lax.all_to_all(copies, axis, split_axis=0, concat_axis=0, tiled=True)  19.6 us
    gather x5, local copies, waits for them, and re-layouts, select(): return jnp.take(values, picked, axis=0)  8.08 us
  transfers between devices with their start and end apart: 13, of which 13 were waited for; matrix products, arithmetic and copies ran while one was open for 5% of the time, Pallas kernels for 0%

commit v1 on v0

v1 whole, which is shorter than its diff:
```python
import jax
import jax.numpy as jnp
from jax import lax
from jax.sharding import Mesh
from jax.sharding import PartitionSpec as P


FSDP = ("fsdp_0", "fsdp_1")
PLANE = ("fsdp_1", "dp")


layer_eps = 1e-06
gelu_scale = 0.7978845608028654
gelu_cubic = 0.044715


def from_everyone(value, axis):
    copies = jnp.broadcast_to(value, (lax.axis_size(axis), *value.shape))
    arrived = lax.all_to_all(copies, axis, split_axis=0, concat_axis=0, tiled=True)
    return arrived.reshape(-1, value.shape[-1])


def summed_on_arrival(value, axis):
    blocks = value.reshape(lax.axis_size(axis), -1, value.shape[-1])
    arrived = lax.all_to_all(blocks, axis, split_axis=0, concat_axis=0, tiled=True)
    return arrived.astype(jnp.float32).sum(axis=0)


def gelu_both(values):
    inner_arg = gelu_scale * (values + gelu_cubic * values * values * values)
    tanh_val = jnp.tanh(inner_arg)
    half = 0.5 * (1.0 + tanh_val)
    slope = half + 0.5 * values * (1.0 - tanh_val * tanh_val) * gelu_scale * (
        1.0 + 3.0 * gelu_cubic * values * values
    )
    return (values * half, slope)


def normalize(inputs):
    values = inputs.astype(jnp.float32)
    center = values - jnp.mean(values, axis=1, keepdims=True)
    inv_std = lax.rsqrt(jnp.mean(center * center, axis=1, keepdims=True) + layer_eps)
    return (center * inv_std, inv_std)


def contract_last(left, right):
    return lax.dot_general(
        left, right, (((1,), (1,)), ((), ())), preferred_element_type=jnp.float32
    )


def contract_first(left, right):
    return lax.dot_general(
        left, right, (((0,), (0,)), ((), ())), preferred_element_type=jnp.float32
    )


def times(left, right):
    return jnp.dot(left, right, preferred_element_type=jnp.float32)


def fresh_positions(mask_row):
    rows = mask_row.shape[0]
    places = jnp.arange(rows)
    fresh = mask_row > 0
    first = jnp.min(jnp.where(fresh, places, rows))
    second = jnp.min(jnp.where(fresh & (places != first), places, rows))
    has_second = second < rows
    second = jnp.where(has_second, second, (first + 1) % rows)
    live = jnp.stack([jnp.float32(1.0), has_second.astype(jnp.float32)])
    return (first, second, live)


def rows_at(values, first, second):
    return jnp.concatenate(
        [lax.dynamic_slice_in_dim(values, first, 1), lax.dynamic_slice_in_dim(values, second, 1)]
    )


def body(
    video_tokens,
    cached_out,
    fresh_mask,
    timestep,
    up_weight,
    down_weight,
    router_in,
    router_bias,
    router_out,
    out_cotangent,
):
    second_section = lax.axis_index("pipe") == 1
    near = lax.axis_index("fsdp_1")
    along = lax.axis_index("fsdp_0")
    column_slot = lax.axis_index(FSDP)
    cached = cached_out[0, 0]
    w_up = up_weight[0]
    w_down = down_weight[0]
    r_in = router_in[0]
    r_out = router_out[0]
    features = cached.shape[1]
    hidden = r_in.shape[1]
    shard_cols = r_in.shape[0]
    near_count = lax.axis_size("fsdp_1")
    bias_row = lax.dynamic_slice_in_dim(router_bias[0], timestep[0], 1)

    swap = [(1, 3), (3, 1)]
    other_up = lax.ppermute(w_up, ("fsdp_1", "pipe"), swap)
    other_down = lax.ppermute(w_down, ("fsdp_1", "pipe"), swap)
    other_in = lax.ppermute(r_in, ("fsdp_1", "pipe"), swap)

    first, second, live = fresh_positions(fresh_mask[0, 0])
    live = live[:, None]
    positions = jnp.stack([first, second]).astype(jnp.float32)
    asked = lax.ppermute(positions, "pipe", [(1, 0)]).astype(jnp.int32)
    match = (asked[:, None] == positions.astype(jnp.int32)[None, :]).astype(jnp.float32)
    match = match * live[:, 0][None, :]

    rows_cached = rows_at(cached, first, second).astype(jnp.float32)
    cot_rows = rows_at(out_cotangent[0], first, second)
    scaled_first, _ = normalize(rows_at(video_tokens[0], first, second))
    rows_first = rows_at(video_tokens[0], first, second).astype(jnp.float32)
    sent_first = jnp.where(second_section, cot_rows, scaled_first.astype(jnp.bfloat16))

    def gate_of(router_pre):
        value, slope = gelu_both(router_pre)
        gate = jax.nn.sigmoid(jnp.sum(value * r_out[None, :], axis=1, keepdims=True))
        return (value, slope, gate)

    gathered = from_everyone(sent_first, FSDP)
    act_first, _ = gelu_both(contract_last(gathered, w_up))
    terms = times(act_first.astype(jnp.bfloat16), w_down)
    columns = lax.dynamic_slice_in_dim(gathered, column_slot * shard_cols, shard_cols, 1)
    sums_first = summed_on_arrival(
        jnp.concatenate([terms, times(columns, r_in)], axis=1).astype(jnp.bfloat16), FSDP
    )
    value_first, slope_first, gate_first = gate_of(sums_first[:, features:] + bias_row)
    change_first = rows_first + sums_first[:, :features] - rows_cached
    added_first = live * gate_first * change_first

    cached_asked = rows_at(cached, asked[0], asked[1]).astype(jnp.float32)

    def at_asked(values):
        return match[:, :1] * values[:1] + match[:, 1:] * values[1:]

    passed = jnp.concatenate([cached_asked + at_asked(added_first), at_asked(change_first)])
    passed = lax.ppermute(passed.astype(jnp.bfloat16), "pipe", [(0, 1)])
    rows_second = passed[:2]
    moved = passed[2:].astype(jnp.float32)

    scaled, inv_std = normalize(rows_second)
    tangent = inv_std * (
        moved
        - jnp.mean(moved, axis=1, keepdims=True)
        - scaled * jnp.mean(moved * scaled, axis=1, keepdims=True)
    )
    both = jnp.concatenate([scaled, tangent], axis=1).astype(jnp.bfloat16)
    both = from_everyone(both, "fsdp_0")
    group_rows = both.shape[0]
    normed_group = both[:, :features]
    stacked = jnp.concatenate([normed_group, both[:, features:]])
    up_pair = jnp.concatenate([w_up, other_up])
    down_pair = jnp.concatenate([w_down, other_down])
    in_pair = jnp.where(
        near == 0, jnp.concatenate([r_in, other_in]), jnp.concatenate([other_in, r_in])
    )
    by_near = gathered.reshape(-1, near_count, 2, features)
    group_first = lax.dynamic_index_in_dim(by_near, near, 1, keepdims=False)
    group_first = group_first.reshape(group_rows, features)
    act_grad = contract_last(group_first, down_pair)
    pre_both = contract_last(stacked, up_pair)
    act, act_slope = gelu_both(pre_both[:group_rows])
    terms = times(act.astype(jnp.bfloat16), down_pair)
    slope_terms = jnp.sum(act_grad * act_slope * pre_both[group_rows:], axis=1, keepdims=True)
    pair_cols = near_count * shard_cols
    routed = times(
        lax.dynamic_slice_in_dim(stacked, along * pair_cols, pair_cols, 1), in_pair
    )
    sums = summed_on_arrival(
        jnp.concatenate(
            [
                terms,
                routed[:group_rows],
                routed[group_rows:],
                jnp.broadcast_to(slope_terms, (group_rows, 128)),
            ],
            axis=1,
        ).astype(jnp.bfloat16),
        "fsdp_0",
    )
    value, slope, gate = gate_of(sums[:, features : features + hidden] + bias_row)
    change = rows_second.astype(jnp.float32) + sums[:, :features] - rows_cached
    added = live * gate * change
    cot = cot_rows.astype(jnp.float32)
    gate_grad = live * jnp.sum(cot * change, axis=1, keepdims=True)
    logit_grad = gate_grad * gate * (1.0 - gate)
    routed_tangent = sums[:, features + hidden : features + 2 * hidden]
    input_grad = live * gate * (
        jnp.sum(cot * moved, axis=1, keepdims=True) + sums[:, features + 2 * hidden :][:, :1]
    ) + logit_grad * jnp.sum(r_out[None, :] * slope * routed_tangent, axis=1, keepdims=True)

    returned = lax.ppermute(input_grad[:, 0], "pipe", [(1, 0)])
    gate_grad_first = jnp.sum(match * returned[:, None], axis=0)[:, None]
    logit_grad_first = gate_grad_first * gate_first * (1.0 - gate_first)

    logit_own = jnp.where(second_section, logit_grad, logit_grad_first)
    slope_own = jnp.where(second_section, slope, slope_first)
    value_own = jnp.where(second_section, value, value_first)
    late = jnp.concatenate([logit_own * r_out[None, :] * slope_own, logit_own * value_own], axis=1)
    late = from_everyone(late.astype(jnp.bfloat16), "fsdp_0")
    normed_own = jnp.where(second_section, normed_group, group_first)
    pair_columns = lax.dynamic_slice_in_dim(normed_own, along * pair_cols, pair_cols, 1)
    in_grad = contract_first(pair_columns, late[:, :hidden])
    totals = jnp.sum(late.astype(jnp.float32), axis=0).reshape(2, hidden)
    step_row = jnp.broadcast_to(timestep[0].astype(jnp.float32), (1, hidden))
    dp_count = lax.axis_size("dp")
    extra = jnp.concatenate([totals, step_row])
    message = jnp.concatenate(
        [
            in_grad.reshape(near_count, shard_cols, hidden),
            jnp.broadcast_to(extra, (near_count, *extra.shape)),
        ],
        axis=1,
    ).astype(jnp.bfloat16)
    message = jnp.broadcast_to(message[:, None], (near_count, dp_count, *message.shape[1:]))
    arrived = lax.all_to_all(
        message.reshape(-1, *message.shape[2:]), PLANE, split_axis=0, concat_axis=0, tiled=True
    ).astype(jnp.float32)
    summed_in = jnp.sum(arrived[:, :shard_cols], axis=0)
    bias_parts = arrived[:, shard_cols]
    summed_out = jnp.sum(arrived[:, shard_cols + 1], axis=0)
    steps = jnp.arange(router_bias.shape[1]).astype(jnp.float32)
    is_step = steps[:, None] == arrived[:, shard_cols + 2, 0][None, :]
    summed_bias = jnp.sum(jnp.where(is_step[:, :, None], bias_parts[None], 0.0), axis=1)

    new_rows = rows_cached + jnp.where(second_section, added, added_first)
    new_rows = new_rows.astype(jnp.bfloat16)
    blended = lax.dynamic_update_slice_in_dim(cached, new_rows[:1], first, 0)
    blended = lax.dynamic_update_slice_in_dim(blended, new_rows[1:], second, 0)
    return (blended[None, None], summed_in[None], summed_bias[None], summed_out[None])


def solution(mesh):
    torus = Mesh(
        mesh.devices.reshape(16, 2, mesh.shape["pipe"], mesh.shape["dp"]),
        ("fsdp_0", "fsdp_1", "pipe", "dp"),
    )
    return jax.shard_map(
        body,
        mesh=torus,
        in_specs=(
            P("dp", FSDP, None),
            P("pipe", "dp", FSDP, None),
            P("pipe", "dp", FSDP),
            P("dp"),
            P("pipe", FSDP, None),
            P("pipe", FSDP, None),
            P("pipe", FSDP, None),
            P("pipe", None, None),
            P("pipe", None),
            P("dp", FSDP, None),
        ),
        out_specs=(
            P("pipe", "dp", FSDP, None),
            P("pipe", FSDP, None),
            P("pipe", None, None),
            P("pipe", None),
        ),
        check_vma=False,
    )
```

time: 398 us -> 203 us (0.51)
  the two profiles are of different devices: /device:TPU:2 before, /device:TPU:32 now
where the time goes in v1:
time: 203 us; the launch traced here: 202 us
  waiting for transfers between devices  93 us (46%)
  starting transfers between devices  48.8 us (24%)
  blocking collectives  20 us (10%)
  local copies, waits for them, and re-layouts  14.4 us (7%)
  between operations  9.49 us (5%)
  other arithmetic  9.03 us (4%)
  matrix products  7.37 us (4%)
    all_to_all x3, waiting for transfers between devices, from_everyone(): lax.all_to_all(copies, axis, split_axis=0, concat_axis=0, tiled=True)  50.8 us
    all_to_all x3, starting transfers between devices, from_everyone(): lax.all_to_all(copies, axis, split_axis=0, concat_axis=0, tiled=True)  29.3 us
    all_to_all x1, blocking collectives, summed_on_arrival(): lax.all_to_all(blocks, axis, split_axis=0, concat_axis=0, tiled=True)  20 us
    ppermute x1, waiting for transfers between devices, body(): returned = lax.ppermute(input_grad[:, 0], 'pipe', [(1, 0)])  16.1 us
    all_to_all x1, waiting for transfers between devices, summed_on_arrival(): lax.all_to_all(blocks, axis, split_axis=0, concat_axis=0, tiled=True)  14.4 us
    all_to_all x1, waiting for transfers between devices, body(): lax.all_to_all(message.reshape(-1, *message.shape[2:]), PLANE, split_axis...  9.83 us
    all_to_all x1, starting transfers between devices, summed_on_arrival(): lax.all_to_all(blocks, axis, split_axis=0, concat_axis=0, tiled=True)  6.35 us
    all_to_all x1, starting transfers between devices, body(): lax.all_to_all(message.reshape(-1, *message.shape[2:]), PLANE, split_axis...  5.26 us
  transfers between devices with their start and end apart: 11, of which 8 were waited for; matrix products, arithmetic and copies ran while one was open for 4% of the time, Pallas kernels for 0%

profile of v1, /device:TPU:32, one launch (start us, length us, event | category | flops | bytes accessed | tf_op | source)
XLA Modules:
  0.0 202.1 jit_solution(1560905913301682241)
XLA Ops:
  0.7 2.1 %copy.112 = bf16[1,1,128,2560]{3,2,1,0:T(8,128)(2,1)} copy(bf16[1,1,128,2560]{3,2,1,0:T(8,128)(2,1)} %param.11) | data formatting | bytes 1310720
  2.7 1.3 fusion.75
  4.7 1.9 fusion.76
  9.9 0.9 dynamic-slice_bitcast_fusion.1
  11.2 0.9 broadcast_in_dim.89
  12.1 17.9 %all-to-all-start = ((bf16[32,2,2560]{2,1,0:T(2,128)(2,1)}), bf16[32,2,2560]{2,1,0:T(2,128)(2,1)S(1)}, u32[]{:S(2)}, u32[]{:S(2)}) async-start(bf16[32,2,2560]{2,1,0:T(2,128)(2,1)} %broadcast_in_dim.89), calls=%async_computation | async-start | bytes 655360 | tf_op jit(solution)/shard_map/all_to_all | solution.py:19
  30.1 23.1 %all-to-all-done = bf16[32,2,2560]{2,1,0:T(2,128)(2,1)S(1)} async-done(((bf16[32,2,2560]{2,1,0:T(2,128)(2,1)}), bf16[32,2,2560]{2,1,0:T(2,128)(2,1)S(1)}, u32[]{:S(2)}, u32[]{:S(2)}) %all-to-all-start) | async-done | bytes 327712 | tf_op jit(solution)/shard_map/all_to_all | solution.py:19
  54.5 1.1 copy.89
  55.6 6.3 %all-to-all-start.1 = ((bf16[32,2,2816]{2,1,0:T(2,128)(2,1)}), bf16[32,2,2816]{2,1,0:T(2,128)(2,1)S(1)}, u32[]{:S(2)}, u32[]{:S(2)}) async-start(bf16[32,2,2816]{2,1,0:T(2,128)(2,1)} %copy.89), calls=%async_computation.1 | async-start | bytes 720896 | tf_op jit(solution)/shard_map/all_to_all | solution.py:25
  62.6 1.3 collective-permute-start
  64.7 1.0 collective-permute-done
  70.2 0.9 dynamic-slice_bitcast_fusion.5
  71.1 14.4 %all-to-all-done.1 = bf16[32,2,2816]{2,1,0:T(2,128)(2,1)S(1)} async-done(((bf16[32,2,2816]{2,1,0:T(2,128)(2,1)}), bf16[32,2,2816]{2,1,0:T(2,128)(2,1)S(1)}, u32[]{:S(2)}, u32[]{:S(2)}) %all-to-all-start.1) | async-done | bytes 360480 | tf_op jit(solution)/shard_map/all_to_all | solution.py:25
  86.4 1.3 collective-permute-start.1
  89.3 0.9 broadcast_in_dim.90
  90.1 6.3 %all-to-all-start.2 = ((bf16[16,2,5120]{2,1,0:T(2,128)(2,1)}), bf16[16,2,5120]{2,1,0:T(2,128)(2,1)S(1)}, u32[]{:S(2)}, u32[]{:S(2)}) async-start(bf16[16,2,5120]{2,1,0:T(2,128)(2,1)} %broadcast_in_dim.90), calls=%async_computation.2 | async-start | bytes 655360 | tf_op jit(solution)/shard_map/all_to_all | solution.py:19
  97.1 1.7 collective-permute-start.2
  98.8 1.7 collective-permute-start.3
  100.7 16.3 %all-to-all-done.2 = bf16[16,2,5120]{2,1,0:T(2,128)(2,1)S(1)} async-done(((bf16[16,2,5120]{2,1,0:T(2,128)(2,1)}), bf16[16,2,5120]{2,1,0:T(2,128)(2,1)S(1)}, u32[]{:S(2)}, u32[]{:S(2)}) %all-to-all-start.2) | async-done | bytes 327712 | tf_op jit(solution)/shard_map/all_to_all | solution.py:19
  117.4 2.0 %fusion = f32[64,448]{1,0:T(8,128)S(1)} fusion(bf16[224,2560]{1,0:T(8,128)(2,1)} %collective-permute-done.2, bf16[224,2560]{1,0:T(8,128)(2,1)S(1)} %bitcast.78, bf16[32,2560]{1,0:T(8,128)(2,1)S(1)} %get-tuple-element.55, bf16[32,2560]{1,0:T(8,128)(2,1)S(1)} %get-tuple-element.54), kind=kOutput, calls=%fused_computation.2 | convolution fusion | flops 152043520 | bytes 2736128 | tf_op jit(solution)/shard_map/dot_general | solution.py:47
  119.5 1.7 convolution_convert_fusion.1
  121.3 2.1 %fusion.8 = bf16[32]{0:T(256)(128)(2,1)S(1)} fusion(bf16[32,2560]{1,0:T(8,128)(2,1)S(1)} %reshape.334, bf16[224,2560]{1,0:T(8,128)(2,1)} %collective-permute-done.3, bf16[224,2560]{1,0:T(8,128)(2,1)S(1)} %bitcast.81, f32[64,448]{1,0:T(8,128)S(1)} %fusion), kind=kOutput, calls=%fused_computation.15 | convolution fusion | flops 78274528 | bytes 2572352 | tf_op jit(solution)/shard_map/dot_general | solution.py:47
  123.8 20.0 %all_to_all.30 = bf16[16,2,3200]{2,1,0:T(2,128)(2,1)S(1)} all-to-all(bf16[16,2,3200]{2,1,0:T(2,128)(2,1)S(1)} %pad_maximum_fusion.12), channel_id=1, replica_groups=mesh['fsdp_0'=16,'fsdp_1'=2,'pipe'=2,'dp'=8] {'fsdp_0'}, dimensions={0} | all-to-all | bytes 409600 | tf_op jit(solution)/shard_map/all_to_all | solution.py:25
  144.9 1.3 collective-permute-start.5
  146.2 16.1 %collective-permute-done.5 = f32[2]{0:T(128)S(1)} collective-permute-done((f32[2]{0:T(128)S(1)}, f32[2]{0:T(128)S(1)}, u32[]{:S(2)}, u32[]{:S(2)}) %collective-permute-start.5) | collective-permute-done | bytes 40 | tf_op jit(solution)/shard_map/ppermute | solution.py:202
  163.3 5.0 %all-to-all-start.4 = ((bf16[16,2,512]{2,1,0:T(2,128)(2,1)}), bf16[16,2,512]{2,1,0:T(2,128)(2,1)S(1)}, u32[]{:S(2)}, u32[]{:S(2)}) async-start(bf16[16,2,512]{2,1,0:T(2,128)(2,1)} %broadcast_in_dim.96), calls=%async_computation.4 | async-start | bytes 65536 | tf_op jit(solution)/shard_map/all_to_all | solution.py:19
  168.4 11.4 %all-to-all-done.4 = bf16[16,2,512]{2,1,0:T(2,128)(2,1)S(1)} async-done(((bf16[16,2,512]{2,1,0:T(2,128)(2,1)}), bf16[16,2,512]{2,1,0:T(2,128)(2,1)S(1)}, u32[]{:S(2)}, u32[]{:S(2)}) %all-to-all-start.4) | async-done | bytes 32800 | tf_op jit(solution)/shard_map/all_to_all | solution.py:19
  180.4 1.1 copy.98
  181.5 5.3 %all-to-all-start.5 = ((bf16[16,83,256]{2,1,0:T(8,128)(2,1)}), bf16[16,83,256]{2,1,0:T(8,128)(2,1)S(1)}, u32[]{:S(2)}, u32[]{:S(2)}) async-start(bf16[16,83,256]{2,1,0:T(8,128)(2,1)} %copy.98), calls=%async_computation.5 | async-start | bytes 1441792 | tf_op jit(solution)/shard_map/all_to_all | solution.py:226
  186.8 1.4 dynamic_update_slice.8
  188.2 1.4 dynamic_update_slice.9
  189.6 9.8 %all-to-all-done.5 = bf16[16,83,256]{2,1,0:T(8,128)(2,1)S(1)} async-done(((bf16[16,83,256]{2,1,0:T(8,128)(2,1)}), bf16[16,83,256]{2,1,0:T(8,128)(2,1)S(1)}, u32[]{:S(2)}, u32[]{:S(2)}) %all-to-all-start.5) | async-done | bytes 679968 | tf_op jit(solution)/shard_map/all_to_all | solution.py:226
  (97 shorter events, 12.5 us)
Async XLA Ops:
  0.6 64.0 %copy-start = (f32[1,50,256]{2,0,1:T(1,128)S(1)}, f32[1,50,256]{2,0,1:T(1,128)}, u32[]{:S(2)}) copy-start(f32[1,50,256]{2,0,1:T(1,128)} %param.17) | copy-start | bytes 153604
  0.6 52.8 %copy-start.1 = (bf16[1,224,2560]{2,1,0:T(8,128)(2,1)S(1)}, bf16[1,224,2560]{2,1,0:T(8,128)(2,1)}, u32[]{:S(2)}) copy-start(bf16[1,224,2560]{2,1,0:T(8,128)(2,1)} %param.14) | copy-start | bytes 3440644
  12.1 41.8 %copy-start.3 = (bf16[1,80,256]{2,1,0:T(8,128)(2,1)S(1)}, bf16[1,80,256]{2,1,0:T(8,128)(2,1)}, u32[]{:S(2)}) copy-start(bf16[1,80,256]{2,1,0:T(8,128)(2,1)} %param.16) | copy-start | bytes 122884
  12.1 41.9 %copy-start.2 = (bf16[1,224,2560]{2,1,0:T(8,128)(2,1)S(1)}, bf16[1,224,2560]{2,1,0:T(8,128)(2,1)}, u32[]{:S(2)}) copy-start(bf16[1,224,2560]{2,1,0:T(8,128)(2,1)} %param.15) | copy-start | bytes 3440644
  12.1 41.1 %all-to-all-start = ((bf16[32,2,2560]{2,1,0:T(2,128)(2,1)}), bf16[32,2,2560]{2,1,0:T(2,128)(2,1)S(1)}, u32[]{:S(2)}, u32[]{:S(2)}) async-start(bf16[32,2,2560]{2,1,0:T(2,128)(2,1)} %broadcast_in_dim.89), calls=%async_computation | async-start | bytes 655360 | tf_op jit(solution)/shard_map/all_to_all | solution.py:19
  54.4 31.5 %copy-start.4 = (f32[1,256]{1,0:T(1,128)S(1)}, f32[1,256]{1,0:T(1,128)}, u32[]{:S(2)}) copy-start(f32[1,256]{1,0:T(1,128)} %param.18) | copy-start | bytes 3076
  55.6 30.0 %all-to-all-start.1 = ((bf16[32,2,2816]{2,1,0:T(2,128)(2,1)}), bf16[32,2,2816]{2,1,0:T(2,128)(2,1)S(1)}, u32[]{:S(2)}, u32[]{:S(2)}) async-start(bf16[32,2,2816]{2,1,0:T(2,128)(2,1)} %copy.89), calls=%async_computation.1 | async-start | bytes 720896 | tf_op jit(solution)/shard_map/all_to_all | solution.py:25
  62.6 3.0 %collective-permute-start = (f32[2]{0:T(128)S(1)}, f32[2]{0:T(128)S(1)}, u32[]{:S(2)}, u32[]{:S(2)}) collective-permute-start(f32[2]{0:T(128)S(1)} %get-tuple-element.35), channel_id=1, source_target_pairs={{8,0},{9,1},{10,2},{11,3},{12,4},{13,5},{14,6},{15,7},{24,16},{25,... | collective-permute-start | bytes 32 | tf_op jit(solution)/shard_map/ppermute | solution.py:115
  86.4 2.1 %collective-permute-start.1 = (bf16[4,2560]{1,0:T(4,128)(2,1)S(1)}, bf16[4,2560]{1,0:T(4,128)(2,1)S(1)}, u32[]{:S(2)}, u32[]{:S(2)}) collective-permute-start(bf16[4,2560]{1,0:T(4,128)(2,1)S(1)} %pad_maximum_fusion.14), channel_id=1, source_target_pairs={{0,8},{1,9},{2,10},{3,11},{4,12},{5,13},{6,14},{7,15},{16,24},{17,... | collective-permute-start | bytes 61448 | tf_op jit(solution)/shard_map/ppermute | solution.py:147
  90.1 26.8 %all-to-all-start.2 = ((bf16[16,2,5120]{2,1,0:T(2,128)(2,1)}), bf16[16,2,5120]{2,1,0:T(2,128)(2,1)S(1)}, u32[]{:S(2)}, u32[]{:S(2)}) async-start(bf16[16,2,5120]{2,1,0:T(2,128)(2,1)} %broadcast_in_dim.90), calls=%async_computation.2 | async-start | bytes 655360 | tf_op jit(solution)/shard_map/all_to_all | solution.py:19
  96.5 20.7 %collective-permute-start.4 = (bf16[80,256]{1,0:T(8,128)(2,1)S(1)}, bf16[80,256]{1,0:T(8,128)(2,1)S(1)}, u32[]{:S(2)}, u32[]{:S(2)}) collective-permute-start(bf16[80,256]{1,0:T(8,128)(2,1)S(1)} %bitcast.84), channel_id=1, source_target_pairs={{8,24},{24,8},{9,25},{25,9},{10,26},{26,10},{11,27},{27,11},{12,28... | collective-permute-start | bytes 122888 | tf_op jit(solution)/shard_map/ppermute | solution.py:110
  97.1 20.3 %collective-permute-start.2 = (bf16[224,2560]{1,0:T(8,128)(2,1)S(1)}, bf16[224,2560]{1,0:T(8,128)(2,1)}, u32[]{:S(2)}, u32[]{:S(2)}) collective-permute-start(bf16[224,2560]{1,0:T(8,128)(2,1)S(1)} %bitcast.77), channel_id=1, source_target_pairs={{8,24},{24,8},{9,25},{25,9},{10,26},{26,10},{11,27},{27,11},{12,28... | collective-permute-start | bytes 3440648 | tf_op jit(solution)/shard_map/ppermute | solution.py:108
  98.8 20.6 %collective-permute-start.3 = (bf16[224,2560]{1,0:T(8,128)(2,1)S(1)}, bf16[224,2560]{1,0:T(8,128)(2,1)}, u32[]{:S(2)}, u32[]{:S(2)}) collective-permute-start(bf16[224,2560]{1,0:T(8,128)(2,1)S(1)} %bitcast.79), channel_id=1, source_target_pairs={{8,24},{24,8},{9,25},{25,9},{10,26},{26,10},{11,27},{27,11},{12,28... | collective-permute-start | bytes 3440648 | tf_op jit(solution)/shard_map/ppermute | solution.py:109
  144.9 17.4 %collective-permute-start.5 = (f32[2]{0:T(128)S(1)}, f32[2]{0:T(128)S(1)}, u32[]{:S(2)}, u32[]{:S(2)}) collective-permute-start(f32[2]{0:T(128)S(1)} %fusion.74), channel_id=1, source_target_pairs={{8,0},{9,1},{10,2},{11,3},{12,4},{13,5},{14,6},{15,7},{24,16},{25,... | collective-permute-start | bytes 32 | tf_op jit(solution)/shard_map/ppermute | solution.py:202
  163.3 16.5 %all-to-all-start.4 = ((bf16[16,2,512]{2,1,0:T(2,128)(2,1)}), bf16[16,2,512]{2,1,0:T(2,128)(2,1)S(1)}, u32[]{:S(2)}, u32[]{:S(2)}) async-start(bf16[16,2,512]{2,1,0:T(2,128)(2,1)} %broadcast_in_dim.96), calls=%async_computation.4 | async-start | bytes 65536 | tf_op jit(solution)/shard_map/all_to_all | solution.py:19
  181.5 18.0 %all-to-all-start.5 = ((bf16[16,83,256]{2,1,0:T(8,128)(2,1)}), bf16[16,83,256]{2,1,0:T(8,128)(2,1)S(1)}, u32[]{:S(2)}, u32[]{:S(2)}) async-start(bf16[16,83,256]{2,1,0:T(8,128)(2,1)} %copy.98), calls=%async_computation.5 | async-start | bytes 1441792 | tf_op jit(solution)/shard_map/all_to_all | solution.py:226

commit v2 on v1

v2 whole, which is shorter than its diff:
```python
import jax
import jax.numpy as jnp
from jax import lax
from jax.sharding import Mesh
from jax.sharding import PartitionSpec as P

FRESH = 2
FSDP = ("fsdp_0", "fsdp_1")
PLANE = ("fsdp_1", "dp")


layer_eps = 1e-06
gelu_scale = 0.7978845608028654
gelu_cubic = 0.044715


def from_everyone(value, axis):
    copies = jnp.broadcast_to(value, (lax.axis_size(axis), *value.shape))
    arrived = lax.all_to_all(copies, axis, split_axis=0, concat_axis=0, tiled=True)
    return arrived.reshape(-1, value.shape[-1])


def summed_on_arrival(value, axis):
    blocks = value.reshape(lax.axis_size(axis), -1, value.shape[-1])
    arrived = lax.all_to_all(blocks, axis, split_axis=0, concat_axis=0, tiled=True)
    return arrived.astype(jnp.float32).sum(axis=0)


def gelu_both(values):
    inner_arg = gelu_scale * (values + gelu_cubic * values * values * values)
    tanh_val = jnp.tanh(inner_arg)
    half = 0.5 * (1.0 + tanh_val)
    slope = half + 0.5 * values * (1.0 - tanh_val * tanh_val) * gelu_scale * (
        1.0 + 3.0 * gelu_cubic * values * values
    )
    return (values * half, slope)


def normalize(inputs):
    values = inputs.astype(jnp.float32)
    center = values - jnp.mean(values, axis=1, keepdims=True)
    inv_std = lax.rsqrt(jnp.mean(center * center, axis=1, keepdims=True) + layer_eps)
    return (center * inv_std, inv_std)


def contract_last(left, right):
    return lax.dot_general(
        left, right, (((1,), (1,)), ((), ())), preferred_element_type=jnp.float32
    )


def contract_first(left, right):
    return lax.dot_general(
        left, right, (((0,), (0,)), ((), ())), preferred_element_type=jnp.float32
    )


def times(left, right):
    return jnp.dot(left, right, preferred_element_type=jnp.float32)


def pick_fresh(mask_row):
    rows = mask_row.shape[0]
    fresh = (mask_row > 0).astype(jnp.float32)
    before = (jnp.arange(rows)[:, None] <= jnp.arange(rows)[None, :]).astype(jnp.float32)
    rank = jnp.sum(before * fresh[:, None], axis=0)
    wanted = jnp.arange(1, FRESH + 1).astype(jnp.float32)
    return jnp.where(rank[None, :] == wanted[:, None], fresh[None, :], 0.0)


def rows_at(picked, values):
    return times(picked.astype(jnp.bfloat16), values)


def body(
    video_tokens,
    cached_out,
    fresh_mask,
    timestep,
    up_weight,
    down_weight,
    router_in,
    router_bias,
    router_out,
    out_cotangent,
):
    second_section = lax.axis_index("pipe") == 1
    near = lax.axis_index("fsdp_1")
    along = lax.axis_index("fsdp_0")
    column_slot = lax.axis_index(FSDP)
    cached = cached_out[0, 0]
    w_up = up_weight[0]
    w_down = down_weight[0]
    r_in = router_in[0]
    r_out = router_out[0]
    features = cached.shape[1]
    hidden = r_in.shape[1]
    shard_cols = r_in.shape[0]
    near_count = lax.axis_size("fsdp_1")
    along_count = lax.axis_size("fsdp_0")
    group_rows = along_count * FRESH
    pair_cols = near_count * shard_cols
    bias_row = lax.dynamic_slice_in_dim(router_bias[0], timestep[0], 1)

    cached_before = lax.ppermute(cached, "pipe", [(0, 1)])
    picked = pick_fresh(fresh_mask[0, 0])
    live = jnp.sum(picked, axis=1, keepdims=True)

    def gate_of(router_pre):
        value, slope = gelu_both(router_pre)
        gate = jax.nn.sigmoid(jnp.sum(value * r_out[None, :], axis=1, keepdims=True))
        return (value, slope, gate)

    def columns_of(rows):
        return lax.dynamic_slice_in_dim(rows, along * pair_cols, pair_cols, 1)

    def first_part():
        rows_first = rows_at(picked, video_tokens[0])
        rows_cached = rows_at(picked, cached)
        scaled_first, _ = normalize(rows_first)
        gathered = from_everyone(scaled_first.astype(jnp.bfloat16), FSDP)
        act_first, _ = gelu_both(contract_last(gathered, w_up))
        terms = times(act_first.astype(jnp.bfloat16), w_down)
        columns = lax.dynamic_slice_in_dim(gathered, column_slot * shard_cols, shard_cols, 1)
        sums_first = summed_on_arrival(
            jnp.concatenate([terms, times(columns, r_in)], axis=1).astype(jnp.bfloat16), FSDP
        )
        by_near = gathered.reshape(along_count, near_count, FRESH, features)
        group_first = lax.dynamic_index_in_dim(by_near, near, 1, keepdims=False)
        columns_first = columns_of(group_first.reshape(group_rows, features))
        value_first, slope_first, gate_first = gate_of(sums_first[:, features:] + bias_row)
        change_first = rows_first + sums_first[:, :features] - rows_cached
        added_first = live * gate_first * change_first
        nothing = (
            jnp.zeros_like(w_up),
            jnp.zeros_like(w_down),
            jnp.zeros_like(r_in),
            jnp.zeros((group_rows, near_count * w_down.shape[0]), jnp.float32),
        )
        passing = jnp.concatenate([added_first, change_first, picked], axis=1)
        state = (value_first, slope_first, gate_first, rows_cached, columns_first)
        return (passing, state, rows_cached, nothing)

    def second_waits():
        swap = [(1, 3), (3, 1)]
        cot_rows = rows_at(picked, out_cotangent[0])
        group = from_everyone(cot_rows.astype(jnp.bfloat16), "fsdp_0")
        other_up = lax.ppermute(w_up, ("fsdp_1", "pipe"), swap)
        other_down = lax.ppermute(w_down, ("fsdp_1", "pipe"), swap)
        other_in = lax.ppermute(r_in, ("fsdp_1", "pipe"), swap)
        act_grad = jnp.concatenate(
            [contract_last(group, w_down), contract_last(group, other_down)], axis=1
        )
        row = jnp.zeros((FRESH, hidden), jnp.float32)
        state = (
            row,
            row,
            row[:, :1],
            rows_at(picked, cached),
            jnp.zeros((group_rows, pair_cols), jnp.bfloat16),
        )
        passing = jnp.zeros((FRESH, 2 * features + picked.shape[1]), jnp.float32)
        return (passing, state, cot_rows, (other_up, other_down, other_in, act_grad))

    passing, state, cot, others = lax.cond(second_section, second_waits, first_part)
    passed = lax.ppermute(passing, "pipe", [(0, 1)])

    def second_part():
        other_up, other_down, other_in, act_grad = others
        rows_cached = state[3]
        match = contract_last(picked, passed[:, 2 * features :])

        def at_match(values):
            return match[:, :1] * values[:1] + match[:, 1:] * values[1:]

        rows_second = rows_at(picked, cached_before) + at_match(passed[:, :features])
        rows_second = rows_second.astype(jnp.bfloat16).astype(jnp.float32)
        moved = at_match(passed[:, features : 2 * features])
        scaled, inv_std = normalize(rows_second)
        tangent = inv_std * (
            moved
            - jnp.mean(moved, axis=1, keepdims=True)
            - scaled * jnp.mean(moved * scaled, axis=1, keepdims=True)
        )
        both = jnp.concatenate([scaled, tangent], axis=1).astype(jnp.bfloat16)
        both = from_everyone(both, "fsdp_0")
        normed_group = both[:, :features]
        stacked = jnp.concatenate([normed_group, both[:, features:]])
        pre_both = jnp.concatenate(
            [contract_last(stacked, w_up), contract_last(stacked, other_up)], axis=1
        )
        act, act_slope = gelu_both(pre_both[:group_rows])
        act = act.astype(jnp.bfloat16)
        own_units = w_down.shape[0]
        terms = times(act[:, :own_units], w_down) + times(act[:, own_units:], other_down)
        slope_terms = jnp.sum(act_grad * act_slope * pre_both[group_rows:], axis=1, keepdims=True)
        in_pair = jnp.where(
            near == 0, jnp.concatenate([r_in, other_in]), jnp.concatenate([other_in, r_in])
        )
        columns = columns_of(stacked)
        routed = times(columns, in_pair)
        sums = summed_on_arrival(
            jnp.concatenate(
                [
                    terms,
                    routed[:group_rows],
                    routed[group_rows:],
                    jnp.broadcast_to(slope_terms, (group_rows, 128)),
                ],
                axis=1,
            ).astype(jnp.bfloat16),
            "fsdp_0",
        )
        value, slope, gate = gate_of(sums[:, features : features + hidden] + bias_row)
        change = rows_second + sums[:, :features] - rows_cached
        gate_grad = live * jnp.sum(cot * change, axis=1, keepdims=True)
        logit_grad = gate_grad * gate * (1.0 - gate)
        routed_tangent = sums[:, features + hidden : features + 2 * hidden]
        input_grad = live * gate * (
            jnp.sum(cot * moved, axis=1, keepdims=True) + sums[:, features + 2 * hidden :][:, :1]
        ) + logit_grad * jnp.sum(r_out[None, :] * slope * routed_tangent, axis=1, keepdims=True)
        returning = jnp.sum(match * input_grad, axis=0)
        return (
            returning,
            rows_cached + live * gate * change,
            value,
            slope,
            logit_grad,
            columns[:group_rows],
        )

    def first_waits():
        value_first, slope_first, gate_first, rows_cached, columns_first = state
        return (
            jnp.zeros((FRESH,), jnp.float32),
            rows_cached + passing[:, :features],
            value_first,
            slope_first,
            gate_first * (1.0 - gate_first),
            columns_first,
        )

    returning, new_rows, value, slope, logit_grad, pair_columns = lax.cond(
        second_section, second_part, first_waits
    )

    returned = lax.ppermute(returning, "pipe", [(1, 0)])[:, None]
    logit_grad = jnp.where(second_section, logit_grad, live * returned * logit_grad)
    late = jnp.concatenate([logit_grad * r_out[None, :] * slope, logit_grad * value], axis=1)
    late = from_everyone(late.astype(jnp.bfloat16), "fsdp_0")
    in_grad = contract_first(pair_columns, late[:, :hidden])
    totals = jnp.sum(late.astype(jnp.float32), axis=0).reshape(2, hidden)
    step_row = jnp.broadcast_to(timestep[0].astype(jnp.float32), (1, hidden))
    dp_count = lax.axis_size("dp")
    extra = jnp.concatenate([totals, step_row])
    message = jnp.concatenate(
        [
            in_grad.reshape(near_count, shard_cols, hidden),
            jnp.broadcast_to(extra, (near_count, *extra.shape)),
        ],
        axis=1,
    ).astype(jnp.bfloat16)
    message = jnp.broadcast_to(message[:, None], (near_count, dp_count, *message.shape[1:]))
    arrived = lax.all_to_all(
        message.reshape(-1, *message.shape[2:]), PLANE, split_axis=0, concat_axis=0, tiled=True
    ).astype(jnp.float32)
    summed_in = jnp.sum(arrived[:, :shard_cols], axis=0)
    bias_parts = arrived[:, shard_cols]
    summed_out = jnp.sum(arrived[:, shard_cols + 1], axis=0)
    steps = jnp.arange(router_bias.shape[1]).astype(jnp.float32)
    is_step = steps[:, None] == arrived[:, shard_cols + 2, 0][None, :]
    summed_bias = jnp.sum(jnp.where(is_step[:, :, None], bias_parts[None], 0.0), axis=1)

    new_rows = new_rows.astype(jnp.bfloat16)
    blended = cached
    for row in range(FRESH):
        blended = jnp.where(picked[row][:, None] > 0, new_rows[row][None, :], blended)
    return (blended[None, None], summed_in[None], summed_bias[None], summed_out[None])


def solution(mesh):
    torus = Mesh(
        mesh.devices.reshape(16, 2, mesh.shape["pipe"], mesh.shape["dp"]),
        ("fsdp_0", "fsdp_1", "pipe", "dp"),
    )
    return jax.shard_map(
        body,
        mesh=torus,
        in_specs=(
            P("dp", FSDP, None),
            P("pipe", "dp", FSDP, None),
            P("pipe", "dp", FSDP),
            P("dp"),
            P("pipe", FSDP, None),
            P("pipe", FSDP, None),
            P("pipe", FSDP, None),
            P("pipe", None, None),
            P("pipe", None),
            P("dp", FSDP, None),
        ),
        out_specs=(
            P("pipe", "dp", FSDP, None),
            P("pipe", FSDP, None),
            P("pipe", None, None),
            P("pipe", None),
        ),
        check_vma=False,
    )
```

time: 203 us -> 175 us (0.86)
  blocking collectives: 20 us -> 0 us
  waiting for transfers between devices: 93 us -> 113 us
  between operations: 9.49 us -> 1.46 us
  starting transfers between devices: 48.8 us -> 41.2 us
  local copies, waits for them, and re-layouts: 14.4 us -> 7.9 us
  matrix products: 7.37 us -> 3.15 us
    ppermute x6 -> x3, waiting for transfers between devices: 17.9 us -> 51.8 us  [the longest x1 51 us: body(): returned = lax.ppermute(returning, 'pipe', [(1, 0)])[:, None]]
    all_to_all x1 -> x0, blocking collectives: 20 us -> none  [summed_on_arrival(): lax.all_to_all(blocks, axis, split_axis=0, concat_axis=0, tiled=True)]
    all_to_all x3 -> x2, waiting for transfers between devices: 50.8 us -> 30.9 us  [from_everyone(): lax.all_to_all(copies, axis, split_axis=0, concat_axis=0, tiled=True)]
    all_to_all x3 -> x2, starting transfers between devices: 29.3 us -> 22.8 us  [from_everyone(): lax.all_to_all(copies, axis, split_axis=0, concat_axis=0, tiled=True)]
    dot_general x3 -> x0, matrix products: 4.66 us -> none  [contract_last(): lax.dot_general(left, right, (((1,), (1,)), ((), ())), preferred_element_...]
    all_to_all x1, waiting for transfers between devices: 14.4 us -> 18.4 us  [summed_on_arrival(): lax.all_to_all(blocks, axis, split_axis=0, concat_axis=0, tiled=True)]
    reduce_min x2 -> x0, other arithmetic: 3.23 us -> none  [the longest x1 1.94 us: fresh_positions(): second = jnp.min(jnp.where(fresh & (places != first), places, rows))]
    dynamic_update_slice x2 -> x0, local copies, waits for them, and re-layouts: 2.87 us -> none  [the longest x1 1.44 us: body(): blended = lax.dynamic_update_slice_in_dim(cached, new_rows[:1], first, 0)]
  transfers between devices with their start and end apart: 11 -> 7, of which waited for: 8 -> 6; matrix products, arithmetic and copies ran while one was open for 4% -> 7% of each run, Pallas kernels for 0% -> 0%
where the time goes in v2:
time: 175 us; the launch traced here: 174 us
  waiting for transfers between devices  113 us (65%)
  starting transfers between devices  41.2 us (24%)
  local copies, waits for them, and re-layouts  7.9 us (5%)
  other arithmetic  7.59 us (4%)
  matrix products  3.15 us (2%)
    ppermute x1, waiting for transfers between devices, body(): returned = lax.ppermute(returning, 'pipe', [(1, 0)])[:, None]  51 us
    all_to_all x2, waiting for transfers between devices, from_everyone(): lax.all_to_all(copies, axis, split_axis=0, concat_axis=0, tiled=True)  30.9 us
    all_to_all x2, starting transfers between devices, from_everyone(): lax.all_to_all(copies, axis, split_axis=0, concat_axis=0, tiled=True)  22.8 us
    all_to_all x1, waiting for transfers between devices, summed_on_arrival(): lax.all_to_all(blocks, axis, split_axis=0, concat_axis=0, tiled=True)  18.4 us
    all_to_all x1, waiting for transfers between devices, body(): lax.all_to_all(message.reshape(-1, *message.shape[2:]), PLANE, split_axis...  11.7 us
    all_to_all x1, starting transfers between devices, summed_on_arrival(): lax.all_to_all(blocks, axis, split_axis=0, concat_axis=0, tiled=True)  6.73 us
    all_to_all x1, starting transfers between devices, body(): lax.all_to_all(message.reshape(-1, *message.shape[2:]), PLANE, split_axis...  6.31 us
  transfers between devices with their start and end apart: 7, of which 6 were waited for; matrix products, arithmetic and copies ran while one was open for 7% of the time, Pallas kernels for 0%

profile of v2, /device:TPU:32, one launch (start us, length us, event | category | flops | bytes accessed | tf_op | source)
XLA Modules:
  0.0 174.2 jit_solution(6339637496140275956)
XLA Ops:
  0.6 2.7 %collective-permute-start.4 = (bf16[128,2560]{1,0:T(8,128)(2,1)}, bf16[128,2560]{1,0:T(8,128)(2,1)}, u32[]{:S(2)}, u32[]{:S(2)}) collective-permute-start(bf16[128,2560]{1,0:T(8,128)(2,1)} %bitcast.78), channel_id=1, source_target_pairs={{0,8},{1,9},{2,10},{3,11},{4,12},{5,13},{6,14},{7,15},{16,24},{17,... | collective-permute-start | bytes 1966088 | tf_op jit(solution)/shard_map/ppermute | solution.py:105
  4.0 0.7 fusion.77
  5.0 72.3 %conditional.2 = (f32[2,5248]{1,0:T(2,128)S(1)}, f32[2,256]{1,0:T(2,128)S(1)}, f32[2,256]{1,0:T(2,128)S(1)}, f32[2,1]{0,1:T(1,128)}, f32[2,2560]{1,0:T(2,128)S(1...) conditional(s32[]{:T(128)} %convert_element_type.95, ...), branch_computations={%region_2.7_spmd, %region_7.8_spmd} | conditional | flops 153511936 | bytes 24574534 | solution.py:165
  5.1 1.6 fusion.85
  6.9 0.9 broadcast_in_dim.79
  7.8 17.8 %all-to-all-start.3 = ((bf16[32,2,2560]{2,1,0:T(2,128)(2,1)}), bf16[32,2,2560]{2,1,0:T(2,128)(2,1)S(1)}, u32[]{:S(2)}, u32[]{:S(2)}) async-start(bf16[32,2,2560]{2,1,0:T(2,128)(2,1)} %broadcast_in_dim.79), calls=%async_computation.3 | async-start | bytes 655360 | tf_op jit(solution)/shard_map/cond/branch_0_fun/all_to_all | solution.py:19
  25.7 19.5 %all-to-all-done.3 = bf16[32,2,2560]{2,1,0:T(2,128)(2,1)S(1)} async-done(((bf16[32,2,2560]{2,1,0:T(2,128)(2,1)}), bf16[32,2,2560]{2,1,0:T(2,128)(2,1)S(1)}, u32[]{:S(2)}, u32[]{:S(2)}) %all-to-all-start.3) | async-done | bytes 327712 | tf_op jit(solution)/shard_map/cond/branch_0_fun/all_to_all | solution.py:19
  45.6 1.0 convolution_convert_fusion
  46.8 1.1 pad_maximum_fusion
  47.8 6.7 %all-to-all-start.4 = ((bf16[32,2,2816]{2,1,0:T(2,128)(2,1)}), bf16[32,2,2816]{2,1,0:T(2,128)(2,1)S(1)}, u32[]{:S(2)}, u32[]{:S(2)}) async-start(bf16[32,2,2816]{2,1,0:T(2,128)(2,1)} %pad_maximum_fusion), calls=%async_computation.4 | async-start | bytes 720896 | tf_op jit(solution)/shard_map/cond/branch_0_fun/all_to_all | solution.py:25
  54.8 18.4 %all-to-all-done.4 = bf16[32,2,2816]{2,1,0:T(2,128)(2,1)S(1)} async-done(((bf16[32,2,2816]{2,1,0:T(2,128)(2,1)}), bf16[32,2,2816]{2,1,0:T(2,128)(2,1)S(1)}, u32[]{:S(2)}, u32[]{:S(2)}) %all-to-all-start.4) | async-done | bytes 360480 | tf_op jit(solution)/shard_map/cond/branch_0_fun/all_to_all | solution.py:25
  74.5 1.1 broadcast.258
  75.5 1.1 broadcast.258.clone
  76.7 0.6 broadcast.259
  77.3 1.3 collective-permute-start.3
  78.6 0.8 collective-permute-done.3
  79.4 0.7 conditional.3
  79.4 0.7 copy.151
  80.1 1.3 collective-permute-start.5
  81.4 51.0 %collective-permute-done.5 = f32[2]{0:T(128)S(1)} collective-permute-done((f32[2]{0:T(128)S(1)}, f32[2]{0:T(128)S(1)}, u32[]{:S(2)}, u32[]{:S(2)}) %collective-permute-start.5) | collective-permute-done | bytes 40 | tf_op jit(solution)/shard_map/ppermute | solution.py:247
  132.3 0.7 fusion.76
  133.0 0.8 multiply_convert_fusion.4
  133.8 0.6 broadcast_in_dim.142
  134.4 5.0 %all-to-all-start.5 = ((bf16[16,2,512]{2,1,0:T(2,128)(2,1)}), bf16[16,2,512]{2,1,0:T(2,128)(2,1)S(1)}, u32[]{:S(2)}, u32[]{:S(2)}) async-start(bf16[16,2,512]{2,1,0:T(2,128)(2,1)} %broadcast_in_dim.142), calls=%async_computation.5 | async-start | bytes 65536 | tf_op jit(solution)/shard_map/all_to_all | solution.py:19
  139.5 11.3 %all-to-all-done.5 = bf16[16,2,512]{2,1,0:T(2,128)(2,1)S(1)} async-done(((bf16[16,2,512]{2,1,0:T(2,128)(2,1)}), bf16[16,2,512]{2,1,0:T(2,128)(2,1)S(1)}, u32[]{:S(2)}, u32[]{:S(2)}) %all-to-all-start.5) | async-done | bytes 32800 | tf_op jit(solution)/shard_map/all_to_all | solution.py:19
  151.4 1.1 copy.115
  152.5 6.3 %all-to-all-start.6 = ((bf16[16,83,256]{2,1,0:T(8,128)(2,1)}), bf16[16,83,256]{2,1,0:T(8,128)(2,1)S(1)}, u32[]{:S(2)}, u32[]{:S(2)}) async-start(bf16[16,83,256]{2,1,0:T(8,128)(2,1)} %copy.115), calls=%async_computation.6 | async-start | bytes 1441792 | tf_op jit(solution)/shard_map/all_to_all | solution.py:264
  158.8 1.0 select_select_fusion
  159.8 11.7 %all-to-all-done.6 = bf16[16,83,256]{2,1,0:T(8,128)(2,1)S(1)} async-done(((bf16[16,83,256]{2,1,0:T(8,128)(2,1)}), bf16[16,83,256]{2,1,0:T(8,128)(2,1)S(1)}, u32[]{:S(2)}, u32[]{:S(2)}) %all-to-all-start.6) | async-done | bytes 679968 | tf_op jit(solution)/shard_map/all_to_all | solution.py:264
  171.8 0.7 slice_reduce_fusion.6
  172.5 0.6 slice_reduce_fusion.7
  173.5 0.7 copy.116
  (59 shorter events, 3.9 us)
Async XLA Ops:
  0.6 4.4 %copy-start = (f32[1,50,256]{2,0,1:T(1,128)S(1)}, f32[1,50,256]{2,0,1:T(1,128)}, u32[]{:S(2)}) copy-start(f32[1,50,256]{2,0,1:T(1,128)} %param.21) | copy-start | bytes 153604
  0.6 78.8 %collective-permute-start.4 = (bf16[128,2560]{1,0:T(8,128)(2,1)}, bf16[128,2560]{1,0:T(8,128)(2,1)}, u32[]{:S(2)}, u32[]{:S(2)}) collective-permute-start(bf16[128,2560]{1,0:T(8,128)(2,1)} %bitcast.78), channel_id=1, source_target_pairs={{0,8},{1,9},{2,10},{3,11},{4,12},{5,13},{6,14},{7,15},{16,24},{17,... | collective-permute-start | bytes 1966088 | tf_op jit(solution)/shard_map/ppermute | solution.py:105
  5.0 40.3 %copy-start.8 = (bf16[80,256]{1,0:T(8,128)(2,1)S(1)}, bf16[80,256]{1,0:T(8,128)(2,1)}, u32[]{:S(2)}) copy-start(bf16[80,256]{1,0:T(8,128)(2,1)} %get-tuple-element.96) | copy-start | bytes 122884 | tf_op jit(solution)/shard_map/cond
  5.0 40.5 %copy-start.1 = (bf16[224,2560]{1,0:T(8,128)(2,1)S(1)}, bf16[224,2560]{1,0:T(8,128)(2,1)}, u32[]{:S(2)}) copy-start(bf16[224,2560]{1,0:T(8,128)(2,1)} %get-tuple-element.94) | copy-start | bytes 3440644 | tf_op jit(solution)/shard_map/cond
  5.0 40.5 %copy-start.6 = (bf16[224,2560]{1,0:T(8,128)(2,1)S(1)}, bf16[224,2560]{1,0:T(8,128)(2,1)}, u32[]{:S(2)}) copy-start(bf16[224,2560]{1,0:T(8,128)(2,1)} %get-tuple-element.93) | copy-start | bytes 3440644 | tf_op jit(solution)/shard_map/cond
  7.8 37.4 %all-to-all-start.3 = ((bf16[32,2,2560]{2,1,0:T(2,128)(2,1)}), bf16[32,2,2560]{2,1,0:T(2,128)(2,1)S(1)}, u32[]{:S(2)}, u32[]{:S(2)}) async-start(bf16[32,2,2560]{2,1,0:T(2,128)(2,1)} %broadcast_in_dim.79), calls=%async_computation.3 | async-start | bytes 655360 | tf_op jit(solution)/shard_map/cond/branch_0_fun/all_to_all | solution.py:19
  46.7 26.8 %copy-start.11 = (f32[1,256]{1,0:T(1,128)S(1)}, f32[1,256]{1,0:T(1,128)}, u32[]{:S(2)}) copy-start(f32[1,256]{1,0:T(1,128)} %get-tuple-element.98) | copy-start | bytes 3076 | tf_op jit(solution)/shard_map/cond
  46.7 27.5 %copy-start.5 = (bf16[128,2560]{1,0:T(8,128)(2,1)S(1)}, bf16[128,2560]{1,0:T(8,128)(2,1)}, u32[]{:S(2)}) copy-start(bf16[128,2560]{1,0:T(8,128)(2,1)} %get-tuple-element.99) | copy-start | bytes 1966084 | tf_op jit(solution)/shard_map/cond
  47.8 25.4 %all-to-all-start.4 = ((bf16[32,2,2816]{2,1,0:T(2,128)(2,1)}), bf16[32,2,2816]{2,1,0:T(2,128)(2,1)S(1)}, u32[]{:S(2)}, u32[]{:S(2)}) async-start(bf16[32,2,2816]{2,1,0:T(2,128)(2,1)} %pad_maximum_fusion), calls=%async_computation.4 | async-start | bytes 720896 | tf_op jit(solution)/shard_map/cond/branch_0_fun/all_to_all | solution.py:25
  77.3 2.1 %collective-permute-start.3 = (f32[2,5248]{1,0:T(2,128)S(1)}, f32[2,5248]{1,0:T(2,128)S(1)}, u32[]{:S(2)}, u32[]{:S(2)}) collective-permute-start(f32[2,5248]{1,0:T(2,128)S(1)} %get-tuple-element.154), channel_id=1, source_target_pairs={{0,8},{1,9},{2,10},{3,11},{4,12},{5,13},{6,14},{7,15},{16,24},{17,... | collective-permute-start | bytes 125960 | tf_op jit(solution)/shard_map/ppermute | solution.py:166
  80.1 52.2 %collective-permute-start.5 = (f32[2]{0:T(128)S(1)}, f32[2]{0:T(128)S(1)}, u32[]{:S(2)}, u32[]{:S(2)}) collective-permute-start(f32[2]{0:T(128)S(1)} %get-tuple-element.170), channel_id=1, source_target_pairs={{8,0},{9,1},{10,2},{11,3},{12,4},{13,5},{14,6},{15,7},{24,16},{25,... | collective-permute-start | bytes 32 | tf_op jit(solution)/shard_map/ppermute | solution.py:247
  134.4 16.5 %all-to-all-start.5 = ((bf16[16,2,512]{2,1,0:T(2,128)(2,1)}), bf16[16,2,512]{2,1,0:T(2,128)(2,1)S(1)}, u32[]{:S(2)}, u32[]{:S(2)}) async-start(bf16[16,2,512]{2,1,0:T(2,128)(2,1)} %broadcast_in_dim.142), calls=%async_computation.5 | async-start | bytes 65536 | tf_op jit(solution)/shard_map/all_to_all | solution.py:19
  151.4 7.4 %copy-start.4 = (bf16[1,1,128,2560]{3,2,1,0:T(8,128)(2,1)S(1)}, bf16[1,1,128,2560]{3,2,1,0:T(8,128)(2,1)}, u32[]{:S(2)}) copy-start(bf16[1,1,128,2560]{3,2,1,0:T(8,128)(2,1)} %param.15) | copy-start | bytes 1966084
  152.5 19.0 %all-to-all-start.6 = ((bf16[16,83,256]{2,1,0:T(8,128)(2,1)}), bf16[16,83,256]{2,1,0:T(8,128)(2,1)S(1)}, u32[]{:S(2)}, u32[]{:S(2)}) async-start(bf16[16,83,256]{2,1,0:T(8,128)(2,1)} %copy.115), calls=%async_computation.6 | async-start | bytes 1441792 | tf_op jit(solution)/shard_map/all_to_all | solution.py:264

commit v3 on v2

--- a/solution.py
+++ b/solution.py
@@ -1,6 +1,7 @@
 import jax
 import jax.numpy as jnp
 from jax import lax
+from jax.experimental import pallas as pl
 from jax.sharding import Mesh
 from jax.sharding import PartitionSpec as P
 
@@ -57,6 +58,14 @@
 
 def times(left, right):
     return jnp.dot(left, right, preferred_element_type=jnp.float32)
+
+
+def unset(*arrays):
+    return pl.pallas_call(
+        lambda *refs: None,
+        out_shape=[jax.ShapeDtypeStruct(shape, dtype) for shape, dtype in arrays],
+        out_specs=[pl.BlockSpec(memory_space=pl.ANY)] * len(arrays),
+    )()
 
 
 def pick_fresh(mask_row):
@@ -99,6 +108,8 @@
     near_count = lax.axis_size("fsdp_1")
     along_count = lax.axis_size("fsdp_0")
     group_rows = along_count * FRESH
+    dp_count = lax.axis_size("dp")
+    plane_count = near_count * dp_count
     pair_cols = near_count * shard_cols
     bias_row = lax.dynamic_slice_in_dim(router_bias[0], timestep[0], 1)
 
@@ -114,51 +125,57 @@
     def columns_of(rows):
         return lax.dynamic_slice_in_dim(rows, along * pair_cols, pair_cols, 1)
 
+    def from_next(value, section):
+        place = lambda x_hi, dp: (x_hi * 2 + section) * dp_count + dp
+        route = [
+            (place(x_hi, dp), place(1 - x_hi, dp ^ (dp_count // 2)))
+            for x_hi in range(near_count)
+            for dp in range(dp_count)
+        ]
+        return lax.ppermute(value, ("fsdp_1", "pipe", "dp"), route)
+
     def first_part():
         rows_first = rows_at(picked, video_tokens[0])
         rows_cached = rows_at(picked, cached)
         scaled_first, _ = normalize(rows_first)
-        gathered = from_everyone(scaled_first.astype(jnp.bfloat16), FSDP)
-        act_first, _ = gelu_both(contract_last(gathered, w_up))
-        terms = times(act_first.astype(jnp.bfloat16), w_down)
-        columns = lax.dynamic_slice_in_dim(gathered, column_slot * shard_cols, shard_cols, 1)
-        sums_first = summed_on_arrival(
-            jnp.concatenate([terms, times(columns, r_in)], axis=1).astype(jnp.bfloat16), FSDP
-        )
-        by_near = gathered.reshape(along_count, near_count, FRESH, features)
-        group_first = lax.dynamic_index_in_dim(by_near, near, 1, keepdims=False)
-        columns_first = columns_of(group_first.reshape(group_rows, features))
+        own = from_everyone(scaled_first.astype(jnp.bfloat16), "fsdp_0")
+        other = from_next(own, 0)
+
+        def partial_sums(rows):
+            act_first, _ = gelu_both(contract_last(rows, w_up))
+            terms = times(act_first.astype(jnp.bfloat16), w_down)
+            columns = lax.dynamic_slice_in_dim(rows, column_slot * shard_cols, shard_cols, 1)
+            return jnp.concatenate([terms, times(columns, r_in)], axis=1)
+
+        returned = from_next(partial_sums(other).astype(jnp.bfloat16), 0)
+        sums_first = (partial_sums(own) + returned.astype(jnp.float32)).astype(jnp.bfloat16)
+        sums_first = summed_on_arrival(sums_first, "fsdp_0")
+        columns_first = columns_of(own)
         value_first, slope_first, gate_first = gate_of(sums_first[:, features:] + bias_row)
         change_first = rows_first + sums_first[:, :features] - rows_cached
         added_first = live * gate_first * change_first
-        nothing = (
-            jnp.zeros_like(w_up),
-            jnp.zeros_like(w_down),
-            jnp.zeros_like(r_in),
-            jnp.zeros((group_rows, near_count * w_down.shape[0]), jnp.float32),
+        nothing = unset(
+            (w_up.shape, w_up.dtype),
+            (w_down.shape, w_down.dtype),
+            (r_in.shape, r_in.dtype),
+            ((group_rows, near_count * w_down.shape[0]), jnp.float32),
         )
         passing = jnp.concatenate([added_first, change_first, picked], axis=1)
         state = (value_first, slope_first, gate_first, rows_cached, columns_first)
-        return (passing, state, rows_cached, nothing)
+        return (passing, state, rows_cached, tuple(nothing))
 
     def second_waits():
-        swap = [(1, 3), (3, 1)]
         cot_rows = rows_at(picked, out_cotangent[0])
         group = from_everyone(cot_rows.astype(jnp.bfloat16), "fsdp_0")
-        other_up = lax.ppermute(w_up, ("fsdp_1", "pipe"), swap)
-        other_down = lax.ppermute(w_down, ("fsdp_1", "pipe"), swap)
-        other_in = lax.ppermute(r_in, ("fsdp_1", "pipe"), swap)
+        other_up = from_next(w_up, 1)
+        other_down = from_next(w_down, 1)
+        other_in = from_next(r_in, 1)
         act_grad = jnp.concatenate(
             [contract_last(group, w_down), contract_last(group, other_down)], axis=1
         )
         row = jnp.zeros((FRESH, hidden), jnp.float32)
-        state = (
-            row,
-            row,
-            row[:, :1],
-            rows_at(picked, cached),
-            jnp.zeros((group_rows, pair_cols), jnp.bfloat16),
-        )
+        (columns,) = unset(((group_rows, pair_cols), jnp.bfloat16))
+        state = (row, row, row[:, :1], rows_at(picked, cached), columns)
         passing = jnp.zeros((FRESH, 2 * features + picked.shape[1]), jnp.float32)
         return (passing, state, cot_rows, (other_up, other_down, other_in, act_grad))
 
@@ -199,18 +216,16 @@
         )
         columns = columns_of(stacked)
         routed = times(columns, in_pair)
-        sums = summed_on_arrival(
-            jnp.concatenate(
-                [
-                    terms,
-                    routed[:group_rows],
-                    routed[group_rows:],
-                    jnp.broadcast_to(slope_terms, (group_rows, 128)),
-                ],
-                axis=1,
-            ).astype(jnp.bfloat16),
-            "fsdp_0",
-        )
+        sums = jnp.concatenate(
+            [
+                terms,
+                routed[:group_rows],
+                routed[group_rows:],
+                jnp.broadcast_to(slope_terms, (group_rows, 128)),
+            ],
+            axis=1,
+        ).astype(jnp.bfloat16)
+        sums = summed_on_arrival(sums, "fsdp_0")
         value, slope, gate = gate_of(sums[:, features : features + hidden] + bias_row)
         change = rows_second + sums[:, :features] - rows_cached
         gate_grad = live * jnp.sum(cot * change, axis=1, keepdims=True)
@@ -248,28 +263,27 @@
     logit_grad = jnp.where(second_section, logit_grad, live * returned * logit_grad)
     late = jnp.concatenate([logit_grad * r_out[None, :] * slope, logit_grad * value], axis=1)
     late = from_everyone(late.astype(jnp.bfloat16), "fsdp_0")
-    in_grad = contract_first(pair_columns, late[:, :hidden])
-    totals = jnp.sum(late.astype(jnp.float32), axis=0).reshape(2, hidden)
+    out_row = jnp.sum(late[:, hidden:].astype(jnp.float32), axis=0, keepdims=True)
     step_row = jnp.broadcast_to(timestep[0].astype(jnp.float32), (1, hidden))
-    dp_count = lax.axis_size("dp")
-    extra = jnp.concatenate([totals, step_row])
+    hidden_part = jnp.concatenate(
+        [late[:, :hidden], out_row.astype(jnp.bfloat16), step_row.astype(jnp.bfloat16)]
+    )
+    shards = jnp.moveaxis(pair_columns.reshape(group_rows, near_count, shard_cols), 1, 0)
+    shards = jnp.pad(shards, ((0, 0), (0, 2), (0, 128 - shard_cols)))
     message = jnp.concatenate(
-        [
-            in_grad.reshape(near_count, shard_cols, hidden),
-            jnp.broadcast_to(extra, (near_count, *extra.shape)),
-        ],
-        axis=1,
-    ).astype(jnp.bfloat16)
+        [jnp.broadcast_to(hidden_part, (near_count, *hidden_part.shape)), shards], axis=2
+    )
     message = jnp.broadcast_to(message[:, None], (near_count, dp_count, *message.shape[1:]))
     arrived = lax.all_to_all(
-        message.reshape(-1, *message.shape[2:]), PLANE, split_axis=0, concat_axis=0, tiled=True
-    ).astype(jnp.float32)
-    summed_in = jnp.sum(arrived[:, :shard_cols], axis=0)
-    bias_parts = arrived[:, shard_cols]
-    summed_out = jnp.sum(arrived[:, shard_cols + 1], axis=0)
-    steps = jnp.arange(router_bias.shape[1]).astype(jnp.float32)
-    is_step = steps[:, None] == arrived[:, shard_cols + 2, 0][None, :]
-    summed_bias = jnp.sum(jnp.where(is_step[:, :, None], bias_parts[None], 0.0), axis=1)
+        message.reshape(plane_count, *message.shape[2:]), PLANE, 0, 0, tiled=True
+    )
+    plane_rows = arrived[:, :group_rows].reshape(plane_count * group_rows, -1)
+    hidden_rows = plane_rows[:, :hidden]
+    summed_in = contract_first(plane_rows[:, hidden : hidden + shard_cols], hidden_rows)
+    steps = jnp.arange(router_bias.shape[1]).astype(jnp.bfloat16)
+    is_step = (steps[:, None] == arrived[:, group_rows + 1, 0][None, :]).astype(jnp.bfloat16)
+    summed_bias = times(jnp.repeat(is_step, group_rows, axis=1), hidden_rows)
+    summed_out = jnp.sum(arrived[:, group_rows, :hidden].astype(jnp.float32), axis=0)
 
     new_rows = new_rows.astype(jnp.bfloat16)
     blended = cached

time: 175 us -> 173 us (0.989)
  waiting for transfers between devices: 113 us -> 103 us
  starting transfers between devices: 41.2 us -> 50.5 us
  matrix products: 3.15 us -> 6.45 us
  local copies, waits for them, and re-layouts: 7.9 us -> 5.13 us
  other arithmetic: 7.59 us -> 5.47 us
    ppermute x0 -> x2, starting transfers between devices: none -> 10.7 us  [from_next(): return lax.ppermute(value, ('fsdp_1', 'pipe', 'dp'), route)]
    all_to_all x1, waiting for transfers between devices: 18.4 us -> 12.8 us  [summed_on_arrival(): lax.all_to_all(blocks, axis, split_axis=0, concat_axis=0, tiled=True)]
    all_to_all x2, waiting for transfers between devices: 30.9 us -> 25.5 us  [from_everyone(): lax.all_to_all(copies, axis, split_axis=0, concat_axis=0, tiled=True)]
    ppermute x0 -> x2, waiting for transfers between devices: none -> 4.17 us  [from_next(): return lax.ppermute(value, ('fsdp_1', 'pipe', 'dp'), route)]
    another operation x5 -> x1, local copies, waits for them, and re-layouts: 2.82 us -> 0.01 us
    dot_general x4 -> x7, matrix products: 2.95 us -> 5.61 us  [times(): return jnp.dot(left, right, preferred_element_type=jnp.float32)]
    all_to_all x2, starting transfers between devices: 22.8 us -> 20.2 us  [from_everyone(): lax.all_to_all(copies, axis, split_axis=0, concat_axis=0, tiled=True)]
    all_to_all x1, waiting for transfers between devices: 11.7 us -> 9.26 us  [body(): lax.all_to_all(message.reshape(plane_count, *message.shape[2:]), PLANE, 0...]
  transfers between devices with their start and end apart: 7 -> 9, of which waited for: 6 -> 8; matrix products, arithmetic and copies ran while one was open for 7% -> 6% of each run, Pallas kernels for 0% -> 0%
where the time goes in v3:
time: 173 us; the launch traced here: 172 us
  waiting for transfers between devices  103 us (60%)
  starting transfers between devices  50.5 us (29%)
  matrix products  6.45 us (4%)
  other arithmetic  5.47 us (3%)
  local copies, waits for them, and re-layouts  5.13 us (3%)
    ppermute x1, waiting for transfers between devices, body(): returned = lax.ppermute(returning, 'pipe', [(1, 0)])[:, None]  50.6 us
    all_to_all x2, waiting for transfers between devices, from_everyone(): lax.all_to_all(copies, axis, split_axis=0, concat_axis=0, tiled=True)  25.5 us
    all_to_all x2, starting transfers between devices, from_everyone(): lax.all_to_all(copies, axis, split_axis=0, concat_axis=0, tiled=True)  20.2 us
    all_to_all x1, waiting for transfers between devices, summed_on_arrival(): lax.all_to_all(blocks, axis, split_axis=0, concat_axis=0, tiled=True)  12.8 us
    ppermute x2, starting transfers between devices, from_next(): return lax.ppermute(value, ('fsdp_1', 'pipe', 'dp'), route)  10.7 us
    all_to_all x1, waiting for transfers between devices, body(): lax.all_to_all(message.reshape(plane_count, *message.shape[2:]), PLANE, 0...  9.26 us
    all_to_all x1, starting transfers between devices, summed_on_arrival(): lax.all_to_all(blocks, axis, split_axis=0, concat_axis=0, tiled=True)  7.87 us
    all_to_all x1, starting transfers between devices, body(): lax.all_to_all(message.reshape(plane_count, *message.shape[2:]), PLANE, 0...  6.32 us
  transfers between devices with their start and end apart: 9, of which 8 were waited for; matrix products, arithmetic and copies ran while one was open for 6% of the time, Pallas kernels for 0%

profile of v3, /device:TPU:32, one launch (start us, length us, event | category | flops | bytes accessed | tf_op | source)
XLA Modules:
  0.0 172.2 jit_solution(1472264390509391798)
XLA Ops:
  0.6 2.7 %collective-permute-start.6 = (bf16[128,2560]{1,0:T(8,128)(2,1)}, bf16[128,2560]{1,0:T(8,128)(2,1)}, u32[]{:S(2)}, u32[]{:S(2)}) collective-permute-start(bf16[128,2560]{1,0:T(8,128)(2,1)} %bitcast.86), channel_id=1, source_target_pairs={{0,8},{1,9},{2,10},{3,11},{4,12},{5,13},{6,14},{7,15},{16,24},{17,... | collective-permute-start | bytes 1966088 | tf_op jit(solution)/shard_map/ppermute | solution.py:116
  4.0 0.7 fusion.101
  5.0 73.5 %conditional.2 = (f32[2,5248]{1,0:T(2,128)S(1)}, f32[2,256]{1,0:T(2,128)S(1)}, f32[2,256]{1,0:T(2,128)S(1)}, f32[2,1]{0,1:T(1,128)}, f32[2,2560]{1,0:T(2,128)S(1...) conditional(s32[]{:T(128)} %convert_element_type.117, ...), branch_computations={%region_2.7_spmd, %region_7.8_spmd} | conditional | flops 153241600 | bytes 23714412 | solution.py:182
  5.0 1.5 fusion.109
  6.8 0.8 broadcast_in_dim.63
  7.6 15.2 %all-to-all-start.3 = ((bf16[16,2,2560]{2,1,0:T(2,128)(2,1)}), bf16[16,2,2560]{2,1,0:T(2,128)(2,1)S(1)}, u32[]{:S(2)}, u32[]{:S(2)}) async-start(bf16[16,2,2560]{2,1,0:T(2,128)(2,1)} %broadcast_in_dim.63), calls=%async_computation.3 | async-start | bytes 327680 | tf_op jit(solution)/shard_map/cond/branch_0_fun/all_to_all | solution.py:20
  22.8 14.3 %all-to-all-done.3 = bf16[16,2,2560]{2,1,0:T(2,128)(2,1)S(1)} async-done(((bf16[16,2,2560]{2,1,0:T(2,128)(2,1)}), bf16[16,2,2560]{2,1,0:T(2,128)(2,1)S(1)}, u32[]{:S(2)}, u32[]{:S(2)}) %all-to-all-start.3) | async-done | bytes 163872 | tf_op jit(solution)/shard_map/cond/branch_0_fun/all_to_all | solution.py:20
  37.2 5.6 %collective-permute-start.3 = (bf16[32,2560]{1,0:T(8,128)(2,1)S(1)}, bf16[32,2560]{1,0:T(8,128)(2,1)S(1)}, u32[]{:S(2)}, u32[]{:S(2)}) collective-permute-start(bf16[32,2560]{1,0:T(8,128)(2,1)S(1)} %reshape.216), channel_id=1, source_target_pairs={{0,20},{1,21},{2,22},{3,23},{4,16},{5,17},{6,18},{7,19},{16,4},{17... | collective-permute-start | bytes 491528 | tf_op jit(solution)/shard_map/cond/branch_0_fun/ppermute | solution.py:135
  42.8 2.3 %fusion.17 = f32[32,2560]{1,0:T(8,128)S(1)} fusion(bf16[224,2560]{1,0:T(8,128)(2,1)S(1)} %copy-done.1, bf16[32,2560]{1,0:T(8,128)(2,1)S(1)} %reshape.216, bf16[224,2560]{1,0:T(8,128)(2,1)} %get-tuple-element.91), kind=kOutput, calls=%fused_computation.27 | convolution fusion | flops 73464832 | bytes 2785280 | tf_op jit(solution)/shard_map/cond/branch_0_fun/dot_general | solution.py:60
  45.1 0.9 collective-permute-done.3
  46.0 1.0 convolution_convert_fusion
  47.3 5.1 %collective-permute-start.4 = (bf16[32,2816]{1,0:T(8,128)(2,1)S(1)}, bf16[32,2816]{1,0:T(8,128)(2,1)S(1)}, u32[]{:S(2)}, u32[]{:S(2)}) collective-permute-start(bf16[32,2816]{1,0:T(8,128)(2,1)S(1)} %pad_maximum_fusion), channel_id=1, source_target_pairs={{0,20},{1,21},{2,22},{3,23},{4,16},{5,17},{6,18},{7,19},{16,4},{17... | collective-permute-start | bytes 540680 | tf_op jit(solution)/shard_map/cond/branch_0_fun/ppermute | solution.py:135
  52.6 3.3 %collective-permute-done.4 = bf16[32,2816]{1,0:T(8,128)(2,1)S(1)} collective-permute-done((bf16[32,2816]{1,0:T(8,128)(2,1)S(1)}, bf16[32,2816]{1,0:T(8,128)(2,1)S(1)}, u32[]{:S(2)}, u32[]{:S(2)}) %collective-permute-start.4) | collective-permute-done | bytes 180256 | tf_op jit(solution)/shard_map/cond/branch_0_fun/ppermute | solution.py:135
  55.9 0.7 reshape.217
  56.6 7.9 %all-to-all-start.4 = ((bf16[16,2,2816]{2,1,0:T(2,128)(2,1)}), bf16[16,2,2816]{2,1,0:T(2,128)(2,1)S(1)}, u32[]{:S(2)}, u32[]{:S(2)}) async-start(bf16[16,2,2816]{2,1,0:T(2,128)(2,1)} %reshape.217), calls=%async_computation.4 | async-start | bytes 360448 | tf_op jit(solution)/shard_map/cond/branch_0_fun/all_to_all | solution.py:26
  64.6 12.8 %all-to-all-done.4 = bf16[16,2,2816]{2,1,0:T(2,128)(2,1)S(1)} async-done(((bf16[16,2,2816]{2,1,0:T(2,128)(2,1)}), bf16[16,2,2816]{2,1,0:T(2,128)(2,1)S(1)}, u32[]{:S(2)}, u32[]{:S(2)}) %all-to-all-start.4) | async-done | bytes 180256 | tf_op jit(solution)/shard_map/cond/branch_0_fun/all_to_all | solution.py:26
  78.5 1.3 collective-permute-start.5
  79.9 0.7 collective-permute-done.5
  80.7 0.7 conditional.3
  80.7 0.7 copy.106
  81.4 1.3 collective-permute-start.7
  82.6 50.6 %collective-permute-done.7 = f32[2]{0:T(128)S(1)} collective-permute-done((f32[2]{0:T(128)S(1)}, f32[2]{0:T(128)S(1)}, u32[]{:S(2)}, u32[]{:S(2)}) %collective-permute-start.7) | collective-permute-done | bytes 40 | tf_op jit(solution)/shard_map/ppermute | solution.py:262
  133.3 0.7 fusion.100
  133.9 0.8 multiply_convert_fusion.4
  135.3 5.0 %all-to-all-start.5 = ((bf16[16,2,512]{2,1,0:T(2,128)(2,1)}), bf16[16,2,512]{2,1,0:T(2,128)(2,1)S(1)}, u32[]{:S(2)}, u32[]{:S(2)}) async-start(bf16[16,2,512]{2,1,0:T(2,128)(2,1)} %broadcast_in_dim.125), calls=%async_computation.5 | async-start | bytes 65536 | tf_op jit(solution)/shard_map/all_to_all | solution.py:20
  140.5 11.3 %all-to-all-done.5 = bf16[16,2,512]{2,1,0:T(2,128)(2,1)S(1)} async-done(((bf16[16,2,512]{2,1,0:T(2,128)(2,1)}), bf16[16,2,512]{2,1,0:T(2,128)(2,1)S(1)}, u32[]{:S(2)}, u32[]{:S(2)}) %all-to-all-start.5) | async-done | bytes 32800 | tf_op jit(solution)/shard_map/all_to_all | solution.py:20
  152.1 0.9 copy.74
  152.9 6.3 %all-to-all-start.6 = ((bf16[16,34,384]{2,1,0:T(8,128)(2,1)}), bf16[16,34,384]{2,1,0:T(8,128)(2,1)S(1)}, u32[]{:S(2)}, u32[]{:S(2)}) async-start(bf16[16,34,384]{2,1,0:T(8,128)(2,1)} %copy.74), calls=%async_computation.6 | async-start | bytes 983040 | tf_op jit(solution)/shard_map/all_to_all | solution.py:277
  159.3 1.0 select_select_fusion
  160.3 9.3 %all-to-all-done.6 = bf16[16,34,384]{2,1,0:T(8,128)(2,1)S(1)} async-done(((bf16[16,34,384]{2,1,0:T(8,128)(2,1)}), bf16[16,34,384]{2,1,0:T(8,128)(2,1)S(1)}, u32[]{:S(2)}, u32[]{:S(2)}) %all-to-all-start.6) | async-done | bytes 417824 | tf_op jit(solution)/shard_map/all_to_all | solution.py:277
  169.6 0.8 convolution_bitcast_fusion
  170.9 0.7 copy.75
  (59 shorter events, 4.6 us)
Async XLA Ops:
  0.6 4.4 %copy-start = (f32[1,50,256]{2,0,1:T(1,128)S(1)}, f32[1,50,256]{2,0,1:T(1,128)}, u32[]{:S(2)}) copy-start(f32[1,50,256]{2,0,1:T(1,128)} %param.21) | copy-start | bytes 153604
  0.6 80.0 %collective-permute-start.6 = (bf16[128,2560]{1,0:T(8,128)(2,1)}, bf16[128,2560]{1,0:T(8,128)(2,1)}, u32[]{:S(2)}, u32[]{:S(2)}) collective-permute-start(bf16[128,2560]{1,0:T(8,128)(2,1)} %bitcast.86), channel_id=1, source_target_pairs={{0,8},{1,9},{2,10},{3,11},{4,12},{5,13},{6,14},{7,15},{16,24},{17,... | collective-permute-start | bytes 1966088 | tf_op jit(solution)/shard_map/ppermute | solution.py:116
  5.0 37.7 %copy-start.1 = (bf16[224,2560]{1,0:T(8,128)(2,1)S(1)}, bf16[224,2560]{1,0:T(8,128)(2,1)}, u32[]{:S(2)}) copy-start(bf16[224,2560]{1,0:T(8,128)(2,1)} %get-tuple-element.92) | copy-start | bytes 3440644 | tf_op jit(solution)/shard_map/cond
  7.6 29.5 %all-to-all-start.3 = ((bf16[16,2,2560]{2,1,0:T(2,128)(2,1)}), bf16[16,2,2560]{2,1,0:T(2,128)(2,1)S(1)}, u32[]{:S(2)}, u32[]{:S(2)}) async-start(bf16[16,2,2560]{2,1,0:T(2,128)(2,1)} %broadcast_in_dim.63), calls=%async_computation.3 | async-start | bytes 327680 | tf_op jit(solution)/shard_map/cond/branch_0_fun/all_to_all | solution.py:20
  37.2 8.9 %collective-permute-start.3 = (bf16[32,2560]{1,0:T(8,128)(2,1)S(1)}, bf16[32,2560]{1,0:T(8,128)(2,1)S(1)}, u32[]{:S(2)}, u32[]{:S(2)}) collective-permute-start(bf16[32,2560]{1,0:T(8,128)(2,1)S(1)} %reshape.216), channel_id=1, source_target_pairs={{0,20},{1,21},{2,22},{3,23},{4,16},{5,17},{6,18},{7,19},{16,4},{17... | collective-permute-start | bytes 491528 | tf_op jit(solution)/shard_map/cond/branch_0_fun/ppermute | solution.py:135
  42.8 3.3 %copy-start.4 = (bf16[224,2560]{1,0:T(8,128)(2,1)S(1)}, bf16[224,2560]{1,0:T(8,128)(2,1)}, u32[]{:S(2)}) copy-start(bf16[224,2560]{1,0:T(8,128)(2,1)} %get-tuple-element.91) | copy-start | bytes 3440644 | tf_op jit(solution)/shard_map/cond
  45.1 1.9 %copy-start.8 = (bf16[80,256]{1,0:T(8,128)(2,1)S(1)}, bf16[80,256]{1,0:T(8,128)(2,1)}, u32[]{:S(2)}) copy-start(bf16[80,256]{1,0:T(8,128)(2,1)} %get-tuple-element.94) | copy-start | bytes 122884 | tf_op jit(solution)/shard_map/cond
  47.0 30.6 %copy-start.11 = (f32[1,256]{1,0:T(1,128)S(1)}, f32[1,256]{1,0:T(1,128)}, u32[]{:S(2)}) copy-start(f32[1,256]{1,0:T(1,128)} %get-tuple-element.96) | copy-start | bytes 3076 | tf_op jit(solution)/shard_map/cond
  47.0 31.3 %copy-start.7 = (bf16[128,2560]{1,0:T(8,128)(2,1)S(1)}, bf16[128,2560]{1,0:T(8,128)(2,1)}, u32[]{:S(2)}) copy-start(bf16[128,2560]{1,0:T(8,128)(2,1)} %get-tuple-element.97) | copy-start | bytes 1966084 | tf_op jit(solution)/shard_map/cond
  47.3 8.6 %collective-permute-start.4 = (bf16[32,2816]{1,0:T(8,128)(2,1)S(1)}, bf16[32,2816]{1,0:T(8,128)(2,1)S(1)}, u32[]{:S(2)}, u32[]{:S(2)}) collective-permute-start(bf16[32,2816]{1,0:T(8,128)(2,1)S(1)} %pad_maximum_fusion), channel_id=1, source_target_pairs={{0,20},{1,21},{2,22},{3,23},{4,16},{5,17},{6,18},{7,19},{16,4},{17... | collective-permute-start | bytes 540680 | tf_op jit(solution)/shard_map/cond/branch_0_fun/ppermute | solution.py:135
  56.6 20.8 %all-to-all-start.4 = ((bf16[16,2,2816]{2,1,0:T(2,128)(2,1)}), bf16[16,2,2816]{2,1,0:T(2,128)(2,1)S(1)}, u32[]{:S(2)}, u32[]{:S(2)}) async-start(bf16[16,2,2816]{2,1,0:T(2,128)(2,1)} %reshape.217), calls=%async_computation.4 | async-start | bytes 360448 | tf_op jit(solution)/shard_map/cond/branch_0_fun/all_to_all | solution.py:26
  78.5 2.2 %collective-permute-start.5 = (f32[2,5248]{1,0:T(2,128)S(1)}, f32[2,5248]{1,0:T(2,128)S(1)}, u32[]{:S(2)}, u32[]{:S(2)}) collective-permute-start(f32[2,5248]{1,0:T(2,128)S(1)} %get-tuple-element.155), channel_id=1, source_target_pairs={{0,8},{1,9},{2,10},{3,11},{4,12},{5,13},{6,14},{7,15},{16,24},{17,... | collective-permute-start | bytes 125960 | tf_op jit(solution)/shard_map/ppermute | solution.py:183
  81.4 51.9 %collective-permute-start.7 = (f32[2]{0:T(128)S(1)}, f32[2]{0:T(128)S(1)}, u32[]{:S(2)}, u32[]{:S(2)}) collective-permute-start(f32[2]{0:T(128)S(1)} %get-tuple-element.170), channel_id=1, source_target_pairs={{8,0},{9,1},{10,2},{11,3},{12,4},{13,5},{14,6},{15,7},{24,16},{25,... | collective-permute-start | bytes 32 | tf_op jit(solution)/shard_map/ppermute | solution.py:262
  135.3 16.5 %all-to-all-start.5 = ((bf16[16,2,512]{2,1,0:T(2,128)(2,1)}), bf16[16,2,512]{2,1,0:T(2,128)(2,1)S(1)}, u32[]{:S(2)}, u32[]{:S(2)}) async-start(bf16[16,2,512]{2,1,0:T(2,128)(2,1)} %broadcast_in_dim.125), calls=%async_computation.5 | async-start | bytes 65536 | tf_op jit(solution)/shard_map/all_to_all | solution.py:20
  152.0 7.3 %copy-start.6 = (bf16[1,1,128,2560]{3,2,1,0:T(8,128)(2,1)S(1)}, bf16[1,1,128,2560]{3,2,1,0:T(8,128)(2,1)}, u32[]{:S(2)}) copy-start(bf16[1,1,128,2560]{3,2,1,0:T(8,128)(2,1)} %param.15) | copy-start | bytes 1966084
  152.9 16.6 %all-to-all-start.6 = ((bf16[16,34,384]{2,1,0:T(8,128)(2,1)}), bf16[16,34,384]{2,1,0:T(8,128)(2,1)S(1)}, u32[]{:S(2)}, u32[]{:S(2)}) async-start(bf16[16,34,384]{2,1,0:T(8,128)(2,1)} %copy.74), calls=%async_computation.6 | async-start | bytes 983040 | tf_op jit(solution)/shard_map/all_to_all | solution.py:277

commit v4 on v3

--- a/solution.py
+++ b/solution.py
@@ -4,6 +4,7 @@
 from jax.experimental import pallas as pl
 from jax.sharding import Mesh
 from jax.sharding import PartitionSpec as P
+
 
 FRESH = 2
 FSDP = ("fsdp_0", "fsdp_1")
@@ -96,7 +97,6 @@
     second_section = lax.axis_index("pipe") == 1
     near = lax.axis_index("fsdp_1")
     along = lax.axis_index("fsdp_0")
-    column_slot = lax.axis_index(FSDP)
     cached = cached_out[0, 0]
     w_up = up_weight[0]
     w_down = down_weight[0]
@@ -134,23 +134,36 @@
         ]
         return lax.ppermute(value, ("fsdp_1", "pipe", "dp"), route)
 
+    def other_shards(section):
+        swapped = []
+        for value in (w_up, w_down, r_in):
+            swapped.append(from_next(value, section))
+        return tuple(swapped)
+
+    def paired_in(other_in):
+        return jnp.where(
+            near == 0, jnp.concatenate([r_in, other_in]), jnp.concatenate([other_in, r_in])
+        )
+
+    def up_both(rows, other_up):
+        return jnp.concatenate([contract_last(rows, w_up), contract_last(rows, other_up)], axis=1)
+
+    def down_both(act, other_down):
+        act = act.astype(jnp.bfloat16)
+        own_units = w_down.shape[0]
+        return times(act[:, :own_units], w_down) + times(act[:, own_units:], other_down)
+
     def first_part():
+        other_up, other_down, other_in = other_shards(0)
         rows_first = rows_at(picked, video_tokens[0])
         rows_cached = rows_at(picked, cached)
         scaled_first, _ = normalize(rows_first)
         own = from_everyone(scaled_first.astype(jnp.bfloat16), "fsdp_0")
-        other = from_next(own, 0)
-
-        def partial_sums(rows):
-            act_first, _ = gelu_both(contract_last(rows, w_up))
-            terms = times(act_first.astype(jnp.bfloat16), w_down)
-            columns = lax.dynamic_slice_in_dim(rows, column_slot * shard_cols, shard_cols, 1)
-            return jnp.concatenate([terms, times(columns, r_in)], axis=1)
-
-        returned = from_next(partial_sums(other).astype(jnp.bfloat16), 0)
-        sums_first = (partial_sums(own) + returned.astype(jnp.float32)).astype(jnp.bfloat16)
-        sums_first = summed_on_arrival(sums_first, "fsdp_0")
+        act_first, _ = gelu_both(up_both(own, other_up))
         columns_first = columns_of(own)
+        routed = times(columns_first, paired_in(other_in))
+        sums_first = jnp.concatenate([down_both(act_first, other_down), routed], axis=1)
+        sums_first = summed_on_arrival(sums_first.astype(jnp.bfloat16), "fsdp_0")
         value_first, slope_first, gate_first = gate_of(sums_first[:, features:] + bias_row)
         change_first = rows_first + sums_first[:, :features] - rows_cached
         added_first = live * gate_first * change_first
@@ -167,9 +180,7 @@
     def second_waits():
         cot_rows = rows_at(picked, out_cotangent[0])
         group = from_everyone(cot_rows.astype(jnp.bfloat16), "fsdp_0")
-        other_up = from_next(w_up, 1)
-        other_down = from_next(w_down, 1)
-        other_in = from_next(r_in, 1)
+        other_up, other_down, other_in = other_shards(1)
         act_grad = jnp.concatenate(
             [contract_last(group, w_down), contract_last(group, other_down)], axis=1
         )
@@ -181,6 +192,7 @@
 
     passing, state, cot, others = lax.cond(second_section, second_waits, first_part)
     passed = lax.ppermute(passing, "pipe", [(0, 1)])
+    cached_asked = rows_at(picked, cached_before)
 
     def second_part():
         other_up, other_down, other_in, act_grad = others
@@ -190,7 +202,7 @@
         def at_match(values):
             return match[:, :1] * values[:1] + match[:, 1:] * values[1:]
 
-        rows_second = rows_at(picked, cached_before) + at_match(passed[:, :features])
+        rows_second = cached_asked + at_match(passed[:, :features])
         rows_second = rows_second.astype(jnp.bfloat16).astype(jnp.float32)
         moved = at_match(passed[:, features : 2 * features])
         scaled, inv_std = normalize(rows_second)
@@ -203,19 +215,12 @@
         both = from_everyone(both, "fsdp_0")
         normed_group = both[:, :features]
         stacked = jnp.concatenate([normed_group, both[:, features:]])
-        pre_both = jnp.concatenate(
-            [contract_last(stacked, w_up), contract_last(stacked, other_up)], axis=1
-        )
+        pre_both = up_both(stacked, other_up)
         act, act_slope = gelu_both(pre_both[:group_rows])
-        act = act.astype(jnp.bfloat16)
-        own_units = w_down.shape[0]
-        terms = times(act[:, :own_units], w_down) + times(act[:, own_units:], other_down)
+        terms = down_both(act, other_down)
         slope_terms = jnp.sum(act_grad * act_slope * pre_both[group_rows:], axis=1, keepdims=True)
-        in_pair = jnp.where(
-            near == 0, jnp.concatenate([r_in, other_in]), jnp.concatenate([other_in, r_in])
-        )
         columns = columns_of(stacked)
-        routed = times(columns, in_pair)
+        routed = times(columns, paired_in(other_in))
         sums = jnp.concatenate(
             [
                 terms,

time: 173 us -> 191 us (1.10)
  waiting for transfers between devices: 103 us -> 115 us
  starting transfers between devices: 50.5 us -> 54.8 us
    ppermute x2 -> x3, waiting for transfers between devices: 4.17 us -> 30.2 us  [from_next(): return lax.ppermute(value, ('fsdp_1', 'pipe', 'dp'), route)]
    all_to_all x2, waiting for transfers between devices: 25.5 us -> 13.8 us  [from_everyone(): lax.all_to_all(copies, axis, split_axis=0, concat_axis=0, tiled=True)]
    all_to_all x1, starting transfers between devices: 7.87 us -> 12 us  [summed_on_arrival(): lax.all_to_all(blocks, axis, split_axis=0, concat_axis=0, tiled=True)]
    dot_general x0 -> x2, matrix products: none -> 3.34 us  [contract_last(): lax.dot_general(left, right, (((1,), (1,)), ((), ())), preferred_element_...]
    ppermute x2 -> x3, starting transfers between devices: 10.7 us -> 11.7 us  [from_next(): return lax.ppermute(value, ('fsdp_1', 'pipe', 'dp'), route)]
  transfers between devices with their start and end apart: 9 -> 10, of which waited for: 8 -> 6; matrix products, arithmetic and copies ran while one was open for 6% -> 7% of each run, Pallas kernels for 0% -> 0%
where the time goes in v4:
time: 191 us; the launch traced here: 190 us
  waiting for transfers between devices  115 us (60%)
  starting transfers between devices  54.8 us (29%)
  matrix products  8.12 us (4%)
  other arithmetic  6.39 us (3%)
  local copies, waits for them, and re-layouts  4.49 us (2%)
    ppermute x1, waiting for transfers between devices, body(): returned = lax.ppermute(returning, 'pipe', [(1, 0)])[:, None]  48.8 us
    ppermute x3, waiting for transfers between devices, from_next(): return lax.ppermute(value, ('fsdp_1', 'pipe', 'dp'), route)  30.2 us
    all_to_all x2, starting transfers between devices, from_everyone(): lax.all_to_all(copies, axis, split_axis=0, concat_axis=0, tiled=True)  20.2 us
    all_to_all x2, waiting for transfers between devices, from_everyone(): lax.all_to_all(copies, axis, split_axis=0, concat_axis=0, tiled=True)  13.8 us
    all_to_all x1, waiting for transfers between devices, summed_on_arrival(): lax.all_to_all(blocks, axis, split_axis=0, concat_axis=0, tiled=True)  12.9 us
    all_to_all x1, starting transfers between devices, summed_on_arrival(): lax.all_to_all(blocks, axis, split_axis=0, concat_axis=0, tiled=True)  12 us
    ppermute x3, starting transfers between devices, from_next(): return lax.ppermute(value, ('fsdp_1', 'pipe', 'dp'), route)  11.7 us
    all_to_all x1, waiting for transfers between devices, body(): lax.all_to_all(message.reshape(plane_count, *message.shape[2:]), PLANE, 0...  9.26 us
  transfers between devices with their start and end apart: 10, of which 6 were waited for; matrix products, arithmetic and copies ran while one was open for 7% of the time, Pallas kernels for 0%

profile of v4, /device:TPU:32, one launch (start us, length us, event | category | flops | bytes accessed | tf_op | source)
XLA Modules:
  0.0 190.4 jit_solution(17619296063785627909)
XLA Ops:
  0.6 2.7 %collective-permute-start.7 = (bf16[128,2560]{1,0:T(8,128)(2,1)}, bf16[128,2560]{1,0:T(8,128)(2,1)}, u32[]{:S(2)}, u32[]{:S(2)}) collective-permute-start(bf16[128,2560]{1,0:T(8,128)(2,1)} %bitcast.82), channel_id=1, source_target_pairs={{0,8},{1,9},{2,10},{3,11},{4,12},{5,13},{6,14},{7,15},{16,24},{17,... | collective-permute-start | bytes 1966088 | tf_op jit(solution)/shard_map/ppermute | solution.py:116
  4.0 0.7 fusion.82
  5.0 93.7 %conditional.2 = (f32[2,5248]{1,0:T(2,128)S(1)}, f32[2,256]{1,0:T(2,128)S(1)}, f32[2,256]{1,0:T(2,128)S(1)}, f32[2,1]{0,1:T(1,128)}, f32[2,2560]{1,0:T(2,128)S(1...) conditional(s32[]{:T(128)} %convert_element_type.109, ...), branch_computations={%region_2.7_spmd, %region_7.8_spmd} | conditional | flops 153346048 | bytes 26833460 | solution.py:193
  5.0 1.5 fusion.91
  6.9 0.8 broadcast_in_dim.63
  7.6 15.2 %all-to-all-start = ((bf16[16,2,2560]{2,1,0:T(2,128)(2,1)}), bf16[16,2,2560]{2,1,0:T(2,128)(2,1)S(1)}, u32[]{:S(2)}, u32[]{:S(2)}) async-start(bf16[16,2,2560]{2,1,0:T(2,128)(2,1)} %broadcast_in_dim.63), calls=%async_computation | async-start | bytes 327680 | tf_op jit(solution)/shard_map/cond/branch_0_fun/all_to_all | solution.py:21
  22.8 4.7 %collective-permute-start = (bf16[224,2560]{1,0:T(8,128)(2,1)}, bf16[224,2560]{1,0:T(8,128)(2,1)}, u32[]{:S(2)}, u32[]{:S(2)}) collective-permute-start(bf16[224,2560]{1,0:T(8,128)(2,1)} %get-tuple-element.91), channel_id=1, source_target_pairs={{0,20},{1,21},{2,22},{3,23},{4,16},{5,17},{6,18},{7,19},{16,4},{17... | collective-permute-start | bytes 3440648 | tf_op jit(solution)/shard_map/cond/branch_0_fun/ppermute | solution.py:135
  27.5 2.4 %collective-permute-start.1 = (bf16[224,2560]{1,0:T(8,128)(2,1)S(1)}, bf16[224,2560]{1,0:T(8,128)(2,1)S(1)}, u32[]{:S(2)}, u32[]{:S(2)}) collective-permute-start(bf16[224,2560]{1,0:T(8,128)(2,1)S(1)} %copy-done.1), channel_id=1, source_target_pairs={{0,20},{1,21},{2,22},{3,23},{4,16},{5,17},{6,18},{7,19},{16,4},{17... | collective-permute-start | bytes 3440648 | tf_op jit(solution)/shard_map/cond/branch_0_fun/ppermute | solution.py:135
  29.9 4.7 %collective-permute-start.2 = (bf16[80,256]{1,0:T(8,128)(2,1)S(1)}, bf16[80,256]{1,0:T(8,128)(2,1)S(1)}, u32[]{:S(2)}, u32[]{:S(2)}) collective-permute-start(bf16[80,256]{1,0:T(8,128)(2,1)S(1)} %copy-done.9), channel_id=1, source_target_pairs={{0,20},{1,21},{2,22},{3,23},{4,16},{5,17},{6,18},{7,19},{16,4},{17... | collective-permute-start | bytes 122888 | tf_op jit(solution)/shard_map/cond/branch_0_fun/ppermute | solution.py:135
  34.6 2.5 %all-to-all-done = bf16[16,2,2560]{2,1,0:T(2,128)(2,1)S(1)} async-done(((bf16[16,2,2560]{2,1,0:T(2,128)(2,1)}), bf16[16,2,2560]{2,1,0:T(2,128)(2,1)S(1)}, u32[]{:S(2)}, u32[]{:S(2)}) %all-to-all-start) | async-done | bytes 163872 | tf_op jit(solution)/shard_map/cond/branch_0_fun/all_to_all | solution.py:21
  37.3 30.2 %collective-permute-done.2 = bf16[80,256]{1,0:T(8,128)(2,1)S(1)} collective-permute-done((bf16[80,256]{1,0:T(8,128)(2,1)S(1)}, bf16[80,256]{1,0:T(8,128)(2,1)S(1)}, u32[]{:S(2)}, u32[]{:S(2)}) %collective-permute-start.2) | collective-permute-done | bytes 40992 | tf_op jit(solution)/shard_map/cond/branch_0_fun/ppermute | solution.py:135
  67.6 1.7 fusion.97
  69.3 1.7 fusion.98
  71.9 0.8 pad_maximum_fusion
  72.7 12.0 %all-to-all-start.1 = ((bf16[16,2,2816]{2,1,0:T(2,128)(2,1)}), bf16[16,2,2816]{2,1,0:T(2,128)(2,1)S(1)}, u32[]{:S(2)}, u32[]{:S(2)}) async-start(bf16[16,2,2816]{2,1,0:T(2,128)(2,1)} %pad_maximum_fusion), calls=%async_computation.1 | async-start | bytes 360448 | tf_op jit(solution)/shard_map/cond/branch_0_fun/all_to_all | solution.py:27
  84.7 12.9 %all-to-all-done.1 = bf16[16,2,2816]{2,1,0:T(2,128)(2,1)S(1)} async-done(((bf16[16,2,2816]{2,1,0:T(2,128)(2,1)}), bf16[16,2,2816]{2,1,0:T(2,128)(2,1)S(1)}, u32[]{:S(2)}, u32[]{:S(2)}) %all-to-all-start.1) | async-done | bytes 180256 | tf_op jit(solution)/shard_map/cond/branch_0_fun/all_to_all | solution.py:27
  98.8 1.3 collective-permute-start.6
  100.2 1.3 fusion.83
  101.4 0.7 conditional.3
  101.4 0.7 copy.115
  102.1 1.3 collective-permute-start.8
  103.4 48.8 %collective-permute-done.8 = f32[2]{0:T(128)S(1)} collective-permute-done((f32[2]{0:T(128)S(1)}, f32[2]{0:T(128)S(1)}, u32[]{:S(2)}, u32[]{:S(2)}) %collective-permute-start.8) | collective-permute-done | bytes 40 | tf_op jit(solution)/shard_map/ppermute | solution.py:267
  152.2 0.7 fusion.81
  152.9 0.8 multiply_convert_fusion.4
  154.3 5.0 %all-to-all-start.5 = ((bf16[16,2,512]{2,1,0:T(2,128)(2,1)}), bf16[16,2,512]{2,1,0:T(2,128)(2,1)S(1)}, u32[]{:S(2)}, u32[]{:S(2)}) async-start(bf16[16,2,512]{2,1,0:T(2,128)(2,1)} %broadcast_in_dim.125), calls=%async_computation.5 | async-start | bytes 65536 | tf_op jit(solution)/shard_map/all_to_all | solution.py:21
  159.5 11.3 %all-to-all-done.5 = bf16[16,2,512]{2,1,0:T(2,128)(2,1)S(1)} async-done(((bf16[16,2,512]{2,1,0:T(2,128)(2,1)}), bf16[16,2,512]{2,1,0:T(2,128)(2,1)S(1)}, u32[]{:S(2)}, u32[]{:S(2)}) %all-to-all-start.5) | async-done | bytes 32800 | tf_op jit(solution)/shard_map/all_to_all | solution.py:21
  171.0 0.9 copy.83
  171.9 5.5 %all-to-all-start.6 = ((bf16[16,34,384]{2,1,0:T(8,128)(2,1)}), bf16[16,34,384]{2,1,0:T(8,128)(2,1)S(1)}, u32[]{:S(2)}, u32[]{:S(2)}) async-start(bf16[16,34,384]{2,1,0:T(8,128)(2,1)} %copy.83), calls=%async_computation.6 | async-start | bytes 983040 | tf_op jit(solution)/shard_map/all_to_all | solution.py:282
  177.4 1.0 select_select_fusion
  178.4 9.3 %all-to-all-done.6 = bf16[16,34,384]{2,1,0:T(8,128)(2,1)S(1)} async-done(((bf16[16,34,384]{2,1,0:T(8,128)(2,1)}), bf16[16,34,384]{2,1,0:T(8,128)(2,1)S(1)}, u32[]{:S(2)}, u32[]{:S(2)}) %all-to-all-start.6) | async-done | bytes 417824 | tf_op jit(solution)/shard_map/all_to_all | solution.py:282
  187.7 0.8 convolution_bitcast_fusion
  189.1 0.7 copy.84
  (62 shorter events, 5.2 us)
Async XLA Ops:
  0.6 4.4 %copy-start = (f32[1,50,256]{2,0,1:T(1,128)S(1)}, f32[1,50,256]{2,0,1:T(1,128)}, u32[]{:S(2)}) copy-start(f32[1,50,256]{2,0,1:T(1,128)} %param.21) | copy-start | bytes 153604
  0.6 99.5 %collective-permute-start.7 = (bf16[128,2560]{1,0:T(8,128)(2,1)}, bf16[128,2560]{1,0:T(8,128)(2,1)}, u32[]{:S(2)}, u32[]{:S(2)}) collective-permute-start(bf16[128,2560]{1,0:T(8,128)(2,1)} %bitcast.82), channel_id=1, source_target_pairs={{0,8},{1,9},{2,10},{3,11},{4,12},{5,13},{6,14},{7,15},{16,24},{17,... | collective-permute-start | bytes 1966088 | tf_op jit(solution)/shard_map/ppermute | solution.py:116
  5.0 22.5 %copy-start.1 = (bf16[224,2560]{1,0:T(8,128)(2,1)S(1)}, bf16[224,2560]{1,0:T(8,128)(2,1)}, u32[]{:S(2)}) copy-start(bf16[224,2560]{1,0:T(8,128)(2,1)} %get-tuple-element.92) | copy-start | bytes 3440644 | tf_op jit(solution)/shard_map/cond
  5.0 24.9 %copy-start.9 = (bf16[80,256]{1,0:T(8,128)(2,1)S(1)}, bf16[80,256]{1,0:T(8,128)(2,1)}, u32[]{:S(2)}) copy-start(bf16[80,256]{1,0:T(8,128)(2,1)} %get-tuple-element.95) | copy-start | bytes 122884 | tf_op jit(solution)/shard_map/cond
  7.6 29.5 %all-to-all-start = ((bf16[16,2,2560]{2,1,0:T(2,128)(2,1)}), bf16[16,2,2560]{2,1,0:T(2,128)(2,1)S(1)}, u32[]{:S(2)}, u32[]{:S(2)}) async-start(bf16[16,2,2560]{2,1,0:T(2,128)(2,1)} %broadcast_in_dim.63), calls=%async_computation | async-start | bytes 327680 | tf_op jit(solution)/shard_map/cond/branch_0_fun/all_to_all | solution.py:21
  22.8 46.5 %collective-permute-start = (bf16[224,2560]{1,0:T(8,128)(2,1)}, bf16[224,2560]{1,0:T(8,128)(2,1)}, u32[]{:S(2)}, u32[]{:S(2)}) collective-permute-start(bf16[224,2560]{1,0:T(8,128)(2,1)} %get-tuple-element.91), channel_id=1, source_target_pairs={{0,20},{1,21},{2,22},{3,23},{4,16},{5,17},{6,18},{7,19},{16,4},{17... | collective-permute-start | bytes 3440648 | tf_op jit(solution)/shard_map/cond/branch_0_fun/ppermute | solution.py:135
  27.5 43.9 %collective-permute-start.1 = (bf16[224,2560]{1,0:T(8,128)(2,1)S(1)}, bf16[224,2560]{1,0:T(8,128)(2,1)S(1)}, u32[]{:S(2)}, u32[]{:S(2)}) collective-permute-start(bf16[224,2560]{1,0:T(8,128)(2,1)S(1)} %copy-done.1), channel_id=1, source_target_pairs={{0,20},{1,21},{2,22},{3,23},{4,16},{5,17},{6,18},{7,19},{16,4},{17... | collective-permute-start | bytes 3440648 | tf_op jit(solution)/shard_map/cond/branch_0_fun/ppermute | solution.py:135
  29.9 37.5 %collective-permute-start.2 = (bf16[80,256]{1,0:T(8,128)(2,1)S(1)}, bf16[80,256]{1,0:T(8,128)(2,1)S(1)}, u32[]{:S(2)}, u32[]{:S(2)}) collective-permute-start(bf16[80,256]{1,0:T(8,128)(2,1)S(1)} %copy-done.9), channel_id=1, source_target_pairs={{0,20},{1,21},{2,22},{3,23},{4,16},{5,17},{6,18},{7,19},{16,4},{17... | collective-permute-start | bytes 122888 | tf_op jit(solution)/shard_map/cond/branch_0_fun/ppermute | solution.py:135
  71.4 26.4 %copy-start.7 = (f32[1,256]{1,0:T(1,128)S(1)}, f32[1,256]{1,0:T(1,128)}, u32[]{:S(2)}) copy-start(f32[1,256]{1,0:T(1,128)} %get-tuple-element.97) | copy-start | bytes 3076 | tf_op jit(solution)/shard_map/cond
  71.4 27.1 %copy-start.5 = (bf16[128,2560]{1,0:T(8,128)(2,1)S(1)}, bf16[128,2560]{1,0:T(8,128)(2,1)}, u32[]{:S(2)}) copy-start(bf16[128,2560]{1,0:T(8,128)(2,1)} %get-tuple-element.98) | copy-start | bytes 1966084 | tf_op jit(solution)/shard_map/cond
  72.7 24.9 %all-to-all-start.1 = ((bf16[16,2,2816]{2,1,0:T(2,128)(2,1)}), bf16[16,2,2816]{2,1,0:T(2,128)(2,1)S(1)}, u32[]{:S(2)}, u32[]{:S(2)}) async-start(bf16[16,2,2816]{2,1,0:T(2,128)(2,1)} %pad_maximum_fusion), calls=%async_computation.1 | async-start | bytes 360448 | tf_op jit(solution)/shard_map/cond/branch_0_fun/all_to_all | solution.py:27
  98.8 2.7 %collective-permute-start.6 = (f32[2,5248]{1,0:T(2,128)S(1)}, f32[2,5248]{1,0:T(2,128)S(1)}, u32[]{:S(2)}, u32[]{:S(2)}) collective-permute-start(f32[2,5248]{1,0:T(2,128)S(1)} %get-tuple-element.155), channel_id=1, source_target_pairs={{0,8},{1,9},{2,10},{3,11},{4,12},{5,13},{6,14},{7,15},{16,24},{17,... | collective-permute-start | bytes 125960 | tf_op jit(solution)/shard_map/ppermute | solution.py:194
  102.1 50.1 %collective-permute-start.8 = (f32[2]{0:T(128)S(1)}, f32[2]{0:T(128)S(1)}, u32[]{:S(2)}, u32[]{:S(2)}) collective-permute-start(f32[2]{0:T(128)S(1)} %get-tuple-element.170), channel_id=1, source_target_pairs={{8,0},{9,1},{10,2},{11,3},{12,4},{13,5},{14,6},{15,7},{24,16},{25,... | collective-permute-start | bytes 32 | tf_op jit(solution)/shard_map/ppermute | solution.py:267
  154.3 16.5 %all-to-all-start.5 = ((bf16[16,2,512]{2,1,0:T(2,128)(2,1)}), bf16[16,2,512]{2,1,0:T(2,128)(2,1)S(1)}, u32[]{:S(2)}, u32[]{:S(2)}) async-start(bf16[16,2,512]{2,1,0:T(2,128)(2,1)} %broadcast_in_dim.125), calls=%async_computation.5 | async-start | bytes 65536 | tf_op jit(solution)/shard_map/all_to_all | solution.py:21
  171.0 6.5 %copy-start.4 = (bf16[1,1,128,2560]{3,2,1,0:T(8,128)(2,1)S(1)}, bf16[1,1,128,2560]{3,2,1,0:T(8,128)(2,1)}, u32[]{:S(2)}) copy-start(bf16[1,1,128,2560]{3,2,1,0:T(8,128)(2,1)} %param.15) | copy-start | bytes 1966084
  171.9 15.8 %all-to-all-start.6 = ((bf16[16,34,384]{2,1,0:T(8,128)(2,1)}), bf16[16,34,384]{2,1,0:T(8,128)(2,1)S(1)}, u32[]{:S(2)}, u32[]{:S(2)}) async-start(bf16[16,34,384]{2,1,0:T(8,128)(2,1)} %copy.83), calls=%async_computation.6 | async-start | bytes 983040 | tf_op jit(solution)/shard_map/all_to_all | solution.py:282

commit v5 on v4

--- a/solution.py
+++ b/solution.py
@@ -59,6 +59,11 @@
 
 def times(left, right):
     return jnp.dot(left, right, preferred_element_type=jnp.float32)
+
+
+def two_parts(values):
+    upper = lax.reduce_precision(values, exponent_bits=8, mantissa_bits=7)
+    return [upper, values - upper]
 
 
 def unset(*arrays):
@@ -134,6 +139,15 @@
         ]
         return lax.ppermute(value, ("fsdp_1", "pipe", "dp"), route)
 
+    def halves_from_next(value):
+        half = value.shape[0] // 2
+        far = lax.axis_index("dp") // (dp_count // 2)
+        wanted = lax.dynamic_slice_in_dim(value, (1 - far) * half, half)
+        got = from_next(wanted, 1)
+        route = [(dp_count + dp, dp_count + (dp ^ (dp_count // 2))) for dp in range(dp_count)]
+        shared = lax.ppermute(got, ("pipe", "dp"), route)
+        return jnp.concatenate([got, shared])
+
     def other_shards(section):
         swapped = []
         for value in (w_up, w_down, r_in):
@@ -170,8 +184,9 @@
         nothing = unset(
             (w_up.shape, w_up.dtype),
             (w_down.shape, w_down.dtype),
-            (r_in.shape, r_in.dtype),
+            ((features, hidden), r_in.dtype),
             ((group_rows, near_count * w_down.shape[0]), jnp.float32),
+            ((group_rows, features), jnp.bfloat16),
         )
         passing = jnp.concatenate([added_first, change_first, picked], axis=1)
         state = (value_first, slope_first, gate_first, rows_cached, columns_first)
@@ -179,8 +194,18 @@
 
     def second_waits():
         cot_rows = rows_at(picked, out_cotangent[0])
-        group = from_everyone(cot_rows.astype(jnp.bfloat16), "fsdp_0")
-        other_up, other_down, other_in = other_shards(1)
+        piece = shard_cols // dp_count
+        own_piece = lax.dynamic_slice_in_dim(r_in, lax.axis_index("dp") * piece, piece)
+        sent = jnp.concatenate([cot_rows.astype(jnp.bfloat16), own_piece.reshape(1, features)])
+        sent = from_everyone(sent, "fsdp_0")
+        sent = sent.reshape(along_count, FRESH + 1, features)
+        group = sent[:, :FRESH].reshape(group_rows, features)
+        pieces = sent[:, FRESH].reshape(along_count * piece, hidden)
+        other_up = halves_from_next(w_up)
+        other_down = halves_from_next(w_down)
+        whole_in = from_everyone(pieces, PLANE)
+        whole_in = whole_in.reshape(near_count, dp_count, along_count, piece, hidden)
+        whole_in = whole_in.transpose(2, 0, 1, 3, 4).reshape(features, hidden)
         act_grad = jnp.concatenate(
             [contract_last(group, w_down), contract_last(group, other_down)], axis=1
         )
@@ -188,14 +213,14 @@
         (columns,) = unset(((group_rows, pair_cols), jnp.bfloat16))
         state = (row, row, row[:, :1], rows_at(picked, cached), columns)
         passing = jnp.zeros((FRESH, 2 * features + picked.shape[1]), jnp.float32)
-        return (passing, state, cot_rows, (other_up, other_down, other_in, act_grad))
+        return (passing, state, cot_rows, (other_up, other_down, whole_in, act_grad, group))
 
     passing, state, cot, others = lax.cond(second_section, second_waits, first_part)
     passed = lax.ppermute(passing, "pipe", [(0, 1)])
     cached_asked = rows_at(picked, cached_before)
 
     def second_part():
-        other_up, other_down, other_in, act_grad = others
+        other_up, other_down, whole_in, act_grad, cot_group = others
         rows_cached = state[3]
         match = contract_last(picked, passed[:, 2 * features :])
 
@@ -211,67 +236,76 @@
             - jnp.mean(moved, axis=1, keepdims=True)
             - scaled * jnp.mean(moved * scaled, axis=1, keepdims=True)
         )
-        both = jnp.concatenate([scaled, tangent], axis=1).astype(jnp.bfloat16)
+        standing = jnp.sum(cot * (rows_second - rows_cached), axis=1, keepdims=True)
+        moving = jnp.sum(cot * moved, axis=1, keepdims=True)
+        numbers = jnp.concatenate(
+            [live, match, *two_parts(standing), *two_parts(moving)], axis=1
+        )
+        numbers = jnp.pad(numbers, ((0, 0), (0, 128 - numbers.shape[1])))
+        both = jnp.concatenate([scaled, tangent, numbers], axis=1).astype(jnp.bfloat16)
         both = from_everyone(both, "fsdp_0")
-        normed_group = both[:, :features]
-        stacked = jnp.concatenate([normed_group, both[:, features:]])
+        stacked = jnp.concatenate([both[:, :features], both[:, features : 2 * features]])
+        numbers = both[:, 2 * features :].astype(jnp.float32)
         pre_both = up_both(stacked, other_up)
         act, act_slope = gelu_both(pre_both[:group_rows])
         terms = down_both(act, other_down)
-        slope_terms = jnp.sum(act_grad * act_slope * pre_both[group_rows:], axis=1, keepdims=True)
-        columns = columns_of(stacked)
-        routed = times(columns, paired_in(other_in))
-        sums = jnp.concatenate(
-            [
-                terms,
-                routed[:group_rows],
-                routed[group_rows:],
-                jnp.broadcast_to(slope_terms, (group_rows, 128)),
-            ],
-            axis=1,
-        ).astype(jnp.bfloat16)
-        sums = summed_on_arrival(sums, "fsdp_0")
-        value, slope, gate = gate_of(sums[:, features : features + hidden] + bias_row)
+        block_parts = jnp.sum(terms * cot_group.astype(jnp.float32), axis=1)
+        slope_parts = jnp.sum(act_grad * act_slope * pre_both[group_rows:], axis=1)
+        parts = jnp.pad(jnp.stack([block_parts, slope_parts]), ((0, 0), (0, 128 - group_rows)))
+        parts = jnp.broadcast_to(parts.astype(jnp.bfloat16), (along_count, *parts.shape))
+        terms = terms.astype(jnp.bfloat16).reshape(along_count, FRESH, features)
+        sums = summed_on_arrival(jnp.concatenate([terms, parts], axis=2), "fsdp_0")
+
+        routed = times(stacked, whole_in)
+        value, slope, gate = gate_of(routed[:group_rows] + bias_row)
+        pull = r_out[None, :] * slope
+        pull_tangent = jnp.sum(pull * routed[group_rows:], axis=1, keepdims=True)
+        gate_own = lax.dynamic_slice_in_dim(gate, along * FRESH, FRESH)
         change = rows_second + sums[:, :features] - rows_cached
-        gate_grad = live * jnp.sum(cot * change, axis=1, keepdims=True)
+        live_group = numbers[:, :1]
+        block_dot = sums[0, features : features + group_rows][:, None]
+        slope_dot = sums[1, features : features + group_rows][:, None]
+        gate_grad = live_group * (numbers[:, 3:4] + numbers[:, 4:5] + block_dot)
         logit_grad = gate_grad * gate * (1.0 - gate)
-        routed_tangent = sums[:, features + hidden : features + 2 * hidden]
-        input_grad = live * gate * (
-            jnp.sum(cot * moved, axis=1, keepdims=True) + sums[:, features + 2 * hidden :][:, :1]
-        ) + logit_grad * jnp.sum(r_out[None, :] * slope * routed_tangent, axis=1, keepdims=True)
-        returning = jnp.sum(match * input_grad, axis=0)
+        input_grad = live_group * gate * (
+            numbers[:, 5:6] + numbers[:, 6:7] + slope_dot
+        ) + logit_grad * pull_tangent
+        returning = (numbers[:, 1:3] * input_grad).reshape(along_count, FRESH, FRESH)
         return (
-            returning,
-            rows_cached + live * gate * change,
+            jnp.sum(returning, axis=1).reshape(group_rows),
+            rows_cached + live * gate_own * change,
             value,
-            slope,
-            logit_grad,
-            columns[:group_rows],
+            pull,
+            logit_grad[:, 0],
+            columns_of(stacked)[:group_rows],
         )
 
     def first_waits():
         value_first, slope_first, gate_first, rows_cached, columns_first = state
+        factor = live * gate_first * (1.0 - gate_first)
+        factors = jnp.pad(jnp.concatenate(two_parts(factor), axis=1), ((0, 0), (0, 126)))
+        rows = jnp.concatenate([r_out[None, :] * slope_first, value_first, factors], axis=1)
+        rows = from_everyone(rows.astype(jnp.bfloat16), "fsdp_0").astype(jnp.float32)
         return (
-            jnp.zeros((FRESH,), jnp.float32),
+            jnp.zeros((group_rows,), jnp.float32),
             rows_cached + passing[:, :features],
-            value_first,
-            slope_first,
-            gate_first * (1.0 - gate_first),
+            rows[:, hidden : 2 * hidden],
+            rows[:, :hidden],
+            rows[:, 2 * hidden] + rows[:, 2 * hidden + 1],
             columns_first,
         )
 
-    returning, new_rows, value, slope, logit_grad, pair_columns = lax.cond(
+    returning, new_rows, value, pull, logit_grad, pair_columns = lax.cond(
         second_section, second_part, first_waits
     )
 
-    returned = lax.ppermute(returning, "pipe", [(1, 0)])[:, None]
-    logit_grad = jnp.where(second_section, logit_grad, live * returned * logit_grad)
-    late = jnp.concatenate([logit_grad * r_out[None, :] * slope, logit_grad * value], axis=1)
-    late = from_everyone(late.astype(jnp.bfloat16), "fsdp_0")
-    out_row = jnp.sum(late[:, hidden:].astype(jnp.float32), axis=0, keepdims=True)
+    returned = lax.ppermute(returning, "pipe", [(1, 0)])
+    logit_grad = (jnp.where(second_section, 1.0, returned) * logit_grad)[:, None]
+    hidden_rows = (logit_grad * pull).astype(jnp.bfloat16)
+    out_row = jnp.sum(logit_grad * value, axis=0, keepdims=True)
     step_row = jnp.broadcast_to(timestep[0].astype(jnp.float32), (1, hidden))
     hidden_part = jnp.concatenate(
-        [late[:, :hidden], out_row.astype(jnp.bfloat16), step_row.astype(jnp.bfloat16)]
+        [hidden_rows, out_row.astype(jnp.bfloat16), step_row.astype(jnp.bfloat16)]
     )
     shards = jnp.moveaxis(pair_columns.reshape(group_rows, near_count, shard_cols), 1, 0)
     shards = jnp.pad(shards, ((0, 0), (0, 2), (0, 128 - shard_cols)))

time: 191 us -> 172 us (0.901)
  waiting for transfers between devices: 115 us -> 94.7 us
  starting transfers between devices: 54.8 us -> 57.3 us
    ppermute x1, waiting for transfers between devices: 48.8 us -> 26.7 us  [body(): returned = lax.ppermute(returning, 'pipe', [(1, 0)])]
    all_to_all x1, starting transfers between devices: 5.52 us -> 7.71 us  [body(): lax.all_to_all(message.reshape(plane_count, *message.shape[2:]), PLANE, 0...]
where the time goes in v5:
time: 172 us; the launch traced here: 171 us
  waiting for transfers between devices  94.7 us (55%)
  starting transfers between devices  57.3 us (33%)
  matrix products  8.13 us (5%)
  other arithmetic  5.43 us (3%)
  local copies, waits for them, and re-layouts  4.02 us (2%)
    ppermute x3, waiting for transfers between devices, from_next(): return lax.ppermute(value, ('fsdp_1', 'pipe', 'dp'), route)  31.3 us
    ppermute x1, waiting for transfers between devices, body(): returned = lax.ppermute(returning, 'pipe', [(1, 0)])  26.7 us
    all_to_all x2, starting transfers between devices, from_everyone(): lax.all_to_all(copies, axis, split_axis=0, concat_axis=0, tiled=True)  20.5 us
    all_to_all x2, waiting for transfers between devices, from_everyone(): lax.all_to_all(copies, axis, split_axis=0, concat_axis=0, tiled=True)  13.4 us
    all_to_all x1, waiting for transfers between devices, summed_on_arrival(): lax.all_to_all(blocks, axis, split_axis=0, concat_axis=0, tiled=True)  12.9 us
    all_to_all x1, starting transfers between devices, summed_on_arrival(): lax.all_to_all(blocks, axis, split_axis=0, concat_axis=0, tiled=True)  12 us
    ppermute x3, starting transfers between devices, from_next(): return lax.ppermute(value, ('fsdp_1', 'pipe', 'dp'), route)  11.7 us
    all_to_all x1, waiting for transfers between devices, body(): lax.all_to_all(message.reshape(plane_count, *message.shape[2:]), PLANE, 0...  10.5 us
  transfers between devices with their start and end apart: 10, of which 6 were waited for; matrix products, arithmetic and copies ran while one was open for 7% of the time, Pallas kernels for 0%

profile of v5, /device:TPU:32, one launch (start us, length us, event | category | flops | bytes accessed | tf_op | source)
XLA Modules:
  0.0 171.2 jit_solution(9653039240013063648)
XLA Ops:
  0.6 2.7 %collective-permute-start.8 = (bf16[128,2560]{1,0:T(8,128)(2,1)}, bf16[128,2560]{1,0:T(8,128)(2,1)}, u32[]{:S(2)}, u32[]{:S(2)}) collective-permute-start(bf16[128,2560]{1,0:T(8,128)(2,1)} %bitcast.142), channel_id=1, source_target_pairs={{0,8},{1,9},{2,10},{3,11},{4,12},{5,13},{6,14},{7,15},{16,24},{17,... | collective-permute-start | bytes 1966088 | tf_op jit(solution)/shard_map/ppermute | solution.py:121
  4.0 0.7 fusion.97
  5.0 92.7 %conditional.2 = (f32[2,5248]{1,0:T(2,128)S(1)}, f32[2,256]{1,0:T(2,128)S(1)}, f32[2,256]{1,0:T(2,128)S(1)}, f32[2,1]{0,1:T(1,128)S(1)}, f32[2,2560]{1,0:T(2,128...) conditional(s32[]{:T(128)} %convert_element_type.133, ...), branch_computations={%region_2.7_spmd, %region_7.8_spmd} | conditional | flops 153346048 | bytes 51374876 | solution.py:218
  5.0 1.5 fusion.109
  6.9 0.8 broadcast_in_dim.63
  7.6 15.2 %all-to-all-start.1 = ((bf16[16,2,2560]{2,1,0:T(2,128)(2,1)}), bf16[16,2,2560]{2,1,0:T(2,128)(2,1)S(1)}, u32[]{:S(2)}, u32[]{:S(2)}) async-start(bf16[16,2,2560]{2,1,0:T(2,128)(2,1)} %broadcast_in_dim.63), calls=%async_computation.1 | async-start | bytes 327680 | tf_op jit(solution)/shard_map/cond/branch_0_fun/all_to_all | solution.py:21
  22.8 4.7 %collective-permute-start = (bf16[224,2560]{1,0:T(8,128)(2,1)}, bf16[224,2560]{1,0:T(8,128)(2,1)}, u32[]{:S(2)}, u32[]{:S(2)}) collective-permute-start(bf16[224,2560]{1,0:T(8,128)(2,1)} %get-tuple-element.92), channel_id=1, source_target_pairs={{0,20},{1,21},{2,22},{3,23},{4,16},{5,17},{6,18},{7,19},{16,4},{17... | collective-permute-start | bytes 3440648 | tf_op jit(solution)/shard_map/cond/branch_0_fun/ppermute | solution.py:140
  27.5 2.4 %collective-permute-start.1 = (bf16[224,2560]{1,0:T(8,128)(2,1)S(1)}, bf16[224,2560]{1,0:T(8,128)(2,1)S(1)}, u32[]{:S(2)}, u32[]{:S(2)}) collective-permute-start(bf16[224,2560]{1,0:T(8,128)(2,1)S(1)} %copy-done.1), channel_id=1, source_target_pairs={{0,20},{1,21},{2,22},{3,23},{4,16},{5,17},{6,18},{7,19},{16,4},{17... | collective-permute-start | bytes 3440648 | tf_op jit(solution)/shard_map/cond/branch_0_fun/ppermute | solution.py:140
  29.9 4.7 %collective-permute-start.2 = (bf16[80,256]{1,0:T(8,128)(2,1)S(1)}, bf16[80,256]{1,0:T(8,128)(2,1)S(1)}, u32[]{:S(2)}, u32[]{:S(2)}) collective-permute-start(bf16[80,256]{1,0:T(8,128)(2,1)S(1)} %copy-done.14), channel_id=1, source_target_pairs={{0,20},{1,21},{2,22},{3,23},{4,16},{5,17},{6,18},{7,19},{16,4},{17... | collective-permute-start | bytes 122888 | tf_op jit(solution)/shard_map/cond/branch_0_fun/ppermute | solution.py:140
  34.6 1.0 all-to-all-done.1
  35.7 31.2 %collective-permute-done.2 = bf16[80,256]{1,0:T(8,128)(2,1)S(1)} collective-permute-done((bf16[80,256]{1,0:T(8,128)(2,1)S(1)}, bf16[80,256]{1,0:T(8,128)(2,1)S(1)}, u32[]{:S(2)}, u32[]{:S(2)}) %collective-permute-start.2) | collective-permute-done | bytes 40992 | tf_op jit(solution)/shard_map/cond/branch_0_fun/ppermute | solution.py:140
  67.1 1.7 fusion.115
  68.8 1.7 fusion.116
  71.4 0.8 pad_maximum_fusion
  72.2 12.0 %all-to-all-start.2 = ((bf16[16,2,2816]{2,1,0:T(2,128)(2,1)}), bf16[16,2,2816]{2,1,0:T(2,128)(2,1)S(1)}, u32[]{:S(2)}, u32[]{:S(2)}) async-start(bf16[16,2,2816]{2,1,0:T(2,128)(2,1)} %pad_maximum_fusion), calls=%async_computation.2 | async-start | bytes 360448 | tf_op jit(solution)/shard_map/cond/branch_0_fun/all_to_all | solution.py:27
  84.3 12.9 %all-to-all-done.2 = bf16[16,2,2816]{2,1,0:T(2,128)(2,1)S(1)} async-done(((bf16[16,2,2816]{2,1,0:T(2,128)(2,1)}), bf16[16,2,2816]{2,1,0:T(2,128)(2,1)S(1)}, u32[]{:S(2)}, u32[]{:S(2)}) %all-to-all-start.2) | async-done | bytes 180256 | tf_op jit(solution)/shard_map/cond/branch_0_fun/all_to_all | solution.py:27
  97.7 1.3 collective-permute-start.7
  99.1 1.3 fusion.98
  100.4 19.6 %conditional.3 = (f32[32]{0:T(128)S(1)}, f32[32,256]{1,0:T(8,128)S(1)}, f32[32,256]{1,0:T(8,128)S(1)}, f32[32]{0:T(128)S(1)}, bf16[32,160]{1,0:T(8,128)(2,1)S(1)...) conditional(s32[]{:T(128)} %convert_element_type.133, (f32[1,256]{1,0:T(1,128)}, f32[2,256]{1,0:T(2,128)S(1)}, ...), branch_computations={%region_8.9_spmd, %region_9.22_spmd} | conditional | flops 307935200 | bytes 22138064 | solution.py:298
  100.7 0.7 multiply_convert_fusion.1
  101.4 0.6 broadcast_in_dim.66
  102.0 5.3 %all-to-all-start = ((bf16[16,2,640]{2,1,0:T(2,128)(2,1)}), bf16[16,2,640]{2,1,0:T(2,128)(2,1)S(1)}, u32[]{:S(2)}, u32[]{:S(2)}) async-start(bf16[16,2,640]{2,1,0:T(2,128)(2,1)} %broadcast_in_dim.66), calls=%async_computation | async-start | bytes 81920 | tf_op jit(solution)/shard_map/cond/branch_0_fun/all_to_all | solution.py:21
  107.3 12.4 %all-to-all-done = bf16[16,2,640]{2,1,0:T(2,128)(2,1)S(1)} async-done(((bf16[16,2,640]{2,1,0:T(2,128)(2,1)}), bf16[16,2,640]{2,1,0:T(2,128)(2,1)S(1)}, u32[]{:S(2)}, u32[]{:S(2)}) %all-to-all-start) | async-done | bytes 40992 | tf_op jit(solution)/shard_map/cond/branch_0_fun/all_to_all | solution.py:21
  120.0 1.3 collective-permute-start.9
  121.4 26.7 %collective-permute-done.9 = f32[32]{0:T(128)S(1)} collective-permute-done((f32[32]{0:T(128)S(1)}, f32[32]{0:T(128)S(1)}, u32[]{:S(2)}, u32[]{:S(2)}) %collective-permute-start.9) | collective-permute-done | bytes 160 | tf_op jit(solution)/shard_map/ppermute | solution.py:302
  148.5 0.9 copy.118
  149.4 7.7 %all-to-all-start.7 = ((bf16[16,34,384]{2,1,0:T(8,128)(2,1)}), bf16[16,34,384]{2,1,0:T(8,128)(2,1)S(1)}, u32[]{:S(2)}, u32[]{:S(2)}) async-start(bf16[16,34,384]{2,1,0:T(8,128)(2,1)} %copy.118), calls=%async_computation.7 | async-start | bytes 983040 | tf_op jit(solution)/shard_map/all_to_all | solution.py:316
  157.1 1.0 select_select_fusion
  158.1 10.5 %all-to-all-done.7 = bf16[16,34,384]{2,1,0:T(8,128)(2,1)S(1)} async-done(((bf16[16,34,384]{2,1,0:T(8,128)(2,1)}), bf16[16,34,384]{2,1,0:T(8,128)(2,1)S(1)}, u32[]{:S(2)}, u32[]{:S(2)}) %all-to-all-start.7) | async-done | bytes 417824 | tf_op jit(solution)/shard_map/all_to_all | solution.py:316
  168.6 0.8 convolution_bitcast_fusion
  170.0 0.7 copy.119
  170.6 0.6 fusion.95
  (68 shorter events, 4.0 us)
Async XLA Ops:
  0.6 4.4 %copy-start = (f32[1,50,256]{2,0,1:T(1,128)S(1)}, f32[1,50,256]{2,0,1:T(1,128)}, u32[]{:S(2)}) copy-start(f32[1,50,256]{2,0,1:T(1,128)} %param.21) | copy-start | bytes 153604
  0.6 98.4 %collective-permute-start.8 = (bf16[128,2560]{1,0:T(8,128)(2,1)}, bf16[128,2560]{1,0:T(8,128)(2,1)}, u32[]{:S(2)}, u32[]{:S(2)}) collective-permute-start(bf16[128,2560]{1,0:T(8,128)(2,1)} %bitcast.142), channel_id=1, source_target_pairs={{0,8},{1,9},{2,10},{3,11},{4,12},{5,13},{6,14},{7,15},{16,24},{17,... | collective-permute-start | bytes 1966088 | tf_op jit(solution)/shard_map/ppermute | solution.py:121
  5.0 22.5 %copy-start.1 = (bf16[224,2560]{1,0:T(8,128)(2,1)S(1)}, bf16[224,2560]{1,0:T(8,128)(2,1)}, u32[]{:S(2)}) copy-start(bf16[224,2560]{1,0:T(8,128)(2,1)} %get-tuple-element.93) | copy-start | bytes 3440644 | tf_op jit(solution)/shard_map/cond
  5.0 24.9 %copy-start.14 = (bf16[80,256]{1,0:T(8,128)(2,1)S(1)}, bf16[80,256]{1,0:T(8,128)(2,1)}, u32[]{:S(2)}) copy-start(bf16[80,256]{1,0:T(8,128)(2,1)} %get-tuple-element.96) | copy-start | bytes 122884 | tf_op jit(solution)/shard_map/cond
  7.6 28.0 %all-to-all-start.1 = ((bf16[16,2,2560]{2,1,0:T(2,128)(2,1)}), bf16[16,2,2560]{2,1,0:T(2,128)(2,1)S(1)}, u32[]{:S(2)}, u32[]{:S(2)}) async-start(bf16[16,2,2560]{2,1,0:T(2,128)(2,1)} %broadcast_in_dim.63), calls=%async_computation.1 | async-start | bytes 327680 | tf_op jit(solution)/shard_map/cond/branch_0_fun/all_to_all | solution.py:21
  22.8 46.0 %collective-permute-start = (bf16[224,2560]{1,0:T(8,128)(2,1)}, bf16[224,2560]{1,0:T(8,128)(2,1)}, u32[]{:S(2)}, u32[]{:S(2)}) collective-permute-start(bf16[224,2560]{1,0:T(8,128)(2,1)} %get-tuple-element.92), channel_id=1, source_target_pairs={{0,20},{1,21},{2,22},{3,23},{4,16},{5,17},{6,18},{7,19},{16,4},{17... | collective-permute-start | bytes 3440648 | tf_op jit(solution)/shard_map/cond/branch_0_fun/ppermute | solution.py:140
  27.5 43.4 %collective-permute-start.1 = (bf16[224,2560]{1,0:T(8,128)(2,1)S(1)}, bf16[224,2560]{1,0:T(8,128)(2,1)S(1)}, u32[]{:S(2)}, u32[]{:S(2)}) collective-permute-start(bf16[224,2560]{1,0:T(8,128)(2,1)S(1)} %copy-done.1), channel_id=1, source_target_pairs={{0,20},{1,21},{2,22},{3,23},{4,16},{5,17},{6,18},{7,19},{16,4},{17... | collective-permute-start | bytes 3440648 | tf_op jit(solution)/shard_map/cond/branch_0_fun/ppermute | solution.py:140
  29.9 37.0 %collective-permute-start.2 = (bf16[80,256]{1,0:T(8,128)(2,1)S(1)}, bf16[80,256]{1,0:T(8,128)(2,1)S(1)}, u32[]{:S(2)}, u32[]{:S(2)}) collective-permute-start(bf16[80,256]{1,0:T(8,128)(2,1)S(1)} %copy-done.14), channel_id=1, source_target_pairs={{0,20},{1,21},{2,22},{3,23},{4,16},{5,17},{6,18},{7,19},{16,4},{17... | collective-permute-start | bytes 122888 | tf_op jit(solution)/shard_map/cond/branch_0_fun/ppermute | solution.py:140
  70.9 26.4 %copy-start.12 = (f32[1,256]{1,0:T(1,128)S(1)}, f32[1,256]{1,0:T(1,128)}, u32[]{:S(2)}) copy-start(f32[1,256]{1,0:T(1,128)} %get-tuple-element.98) | copy-start | bytes 3076 | tf_op jit(solution)/shard_map/cond
  70.9 26.5 %copy-start.7 = (bf16[128,2560]{1,0:T(8,128)(2,1)S(1)}, bf16[128,2560]{1,0:T(8,128)(2,1)}, u32[]{:S(2)}) copy-start(bf16[128,2560]{1,0:T(8,128)(2,1)} %get-tuple-element.99) | copy-start | bytes 1966084 | tf_op jit(solution)/shard_map/cond
  72.2 24.9 %all-to-all-start.2 = ((bf16[16,2,2816]{2,1,0:T(2,128)(2,1)}), bf16[16,2,2816]{2,1,0:T(2,128)(2,1)S(1)}, u32[]{:S(2)}, u32[]{:S(2)}) async-start(bf16[16,2,2816]{2,1,0:T(2,128)(2,1)} %pad_maximum_fusion), calls=%async_computation.2 | async-start | bytes 360448 | tf_op jit(solution)/shard_map/cond/branch_0_fun/all_to_all | solution.py:27
  97.7 2.7 %collective-permute-start.7 = (f32[2,5248]{1,0:T(2,128)S(1)}, f32[2,5248]{1,0:T(2,128)S(1)}, u32[]{:S(2)}, u32[]{:S(2)}) collective-permute-start(f32[2,5248]{1,0:T(2,128)S(1)} %get-tuple-element.161), channel_id=1, source_target_pairs={{0,8},{1,9},{2,10},{3,11},{4,12},{5,13},{6,14},{7,15},{16,24},{17,... | collective-permute-start | bytes 125960 | tf_op jit(solution)/shard_map/ppermute | solution.py:219
  102.0 17.7 %all-to-all-start = ((bf16[16,2,640]{2,1,0:T(2,128)(2,1)}), bf16[16,2,640]{2,1,0:T(2,128)(2,1)S(1)}, u32[]{:S(2)}, u32[]{:S(2)}) async-start(bf16[16,2,640]{2,1,0:T(2,128)(2,1)} %broadcast_in_dim.66), calls=%async_computation | async-start | bytes 81920 | tf_op jit(solution)/shard_map/cond/branch_0_fun/all_to_all | solution.py:21
  120.0 28.2 %collective-permute-start.9 = (f32[32]{0:T(128)S(1)}, f32[32]{0:T(128)S(1)}, u32[]{:S(2)}, u32[]{:S(2)}) collective-permute-start(f32[32]{0:T(128)S(1)} %get-tuple-element.172), channel_id=1, source_target_pairs={{8,0},{9,1},{10,2},{11,3},{12,4},{13,5},{14,6},{15,7},{24,16},{25,... | collective-permute-start | bytes 392 | tf_op jit(solution)/shard_map/ppermute | solution.py:302
  148.4 8.7 %copy-start.6 = (bf16[1,1,128,2560]{3,2,1,0:T(8,128)(2,1)S(1)}, bf16[1,1,128,2560]{3,2,1,0:T(8,128)(2,1)}, u32[]{:S(2)}) copy-start(bf16[1,1,128,2560]{3,2,1,0:T(8,128)(2,1)} %param.15) | copy-start | bytes 1966084
  149.4 19.2 %all-to-all-start.7 = ((bf16[16,34,384]{2,1,0:T(8,128)(2,1)}), bf16[16,34,384]{2,1,0:T(8,128)(2,1)S(1)}, u32[]{:S(2)}, u32[]{:S(2)}) async-start(bf16[16,34,384]{2,1,0:T(8,128)(2,1)} %copy.118), calls=%async_computation.7 | async-start | bytes 983040 | tf_op jit(solution)/shard_map/all_to_all | solution.py:316

commit v6 on v5

--- a/solution.py
+++ b/solution.py
@@ -102,6 +102,7 @@
     second_section = lax.axis_index("pipe") == 1
     near = lax.axis_index("fsdp_1")
     along = lax.axis_index("fsdp_0")
+    column_slot = lax.axis_index(FSDP)
     cached = cached_out[0, 0]
     w_up = up_weight[0]
     w_down = down_weight[0]
@@ -139,26 +140,6 @@
         ]
         return lax.ppermute(value, ("fsdp_1", "pipe", "dp"), route)
 
-    def halves_from_next(value):
-        half = value.shape[0] // 2
-        far = lax.axis_index("dp") // (dp_count // 2)
-        wanted = lax.dynamic_slice_in_dim(value, (1 - far) * half, half)
-        got = from_next(wanted, 1)
-        route = [(dp_count + dp, dp_count + (dp ^ (dp_count // 2))) for dp in range(dp_count)]
-        shared = lax.ppermute(got, ("pipe", "dp"), route)
-        return jnp.concatenate([got, shared])
-
-    def other_shards(section):
-        swapped = []
-        for value in (w_up, w_down, r_in):
-            swapped.append(from_next(value, section))
-        return tuple(swapped)
-
-    def paired_in(other_in):
-        return jnp.where(
-            near == 0, jnp.concatenate([r_in, other_in]), jnp.concatenate([other_in, r_in])
-        )
-
     def up_both(rows, other_up):
         return jnp.concatenate([contract_last(rows, w_up), contract_last(rows, other_up)], axis=1)
 
@@ -168,16 +149,18 @@
         return times(act[:, :own_units], w_down) + times(act[:, own_units:], other_down)
 
     def first_part():
-        other_up, other_down, other_in = other_shards(0)
         rows_first = rows_at(picked, video_tokens[0])
         rows_cached = rows_at(picked, cached)
         scaled_first, _ = normalize(rows_first)
-        own = from_everyone(scaled_first.astype(jnp.bfloat16), "fsdp_0")
-        act_first, _ = gelu_both(up_both(own, other_up))
-        columns_first = columns_of(own)
-        routed = times(columns_first, paired_in(other_in))
-        sums_first = jnp.concatenate([down_both(act_first, other_down), routed], axis=1)
-        sums_first = summed_on_arrival(sums_first.astype(jnp.bfloat16), "fsdp_0")
+        gathered = from_everyone(scaled_first.astype(jnp.bfloat16), FSDP)
+        act_first, _ = gelu_both(contract_last(gathered, w_up))
+        terms = times(act_first.astype(jnp.bfloat16), w_down)
+        columns = lax.dynamic_slice_in_dim(gathered, column_slot * shard_cols, shard_cols, 1)
+        sums_first = jnp.concatenate([terms, times(columns, r_in)], axis=1)
+        sums_first = summed_on_arrival(sums_first.astype(jnp.bfloat16), FSDP)
+        by_near = gathered.reshape(along_count, near_count, FRESH, features)
+        group_first = lax.dynamic_index_in_dim(by_near, near, 1, keepdims=False)
+        columns_first = columns_of(group_first.reshape(group_rows, features))
         value_first, slope_first, gate_first = gate_of(sums_first[:, features:] + bias_row)
         change_first = rows_first + sums_first[:, :features] - rows_cached
         added_first = live * gate_first * change_first
@@ -201,8 +184,8 @@
         sent = sent.reshape(along_count, FRESH + 1, features)
         group = sent[:, :FRESH].reshape(group_rows, features)
         pieces = sent[:, FRESH].reshape(along_count * piece, hidden)
-        other_up = halves_from_next(w_up)
-        other_down = halves_from_next(w_down)
+        other_up = from_next(w_up, 1)
+        other_down = from_next(w_down, 1)
         whole_in = from_everyone(pieces, PLANE)
         whole_in = whole_in.reshape(near_count, dp_count, along_count, piece, hidden)
         whole_in = whole_in.transpose(2, 0, 1, 3, 4).reshape(features, hidden)

time: 172 us -> 152 us (0.88)
  starting transfers between devices: 57.3 us -> 41.5 us
  waiting for transfers between devices: 94.7 us -> 87.5 us
  local copies, waits for them, and re-layouts: 4.02 us -> 7.4 us
  matrix products: 8.13 us -> 6.02 us
    ppermute x3 -> x0, waiting for transfers between devices: 31.3 us -> none  [from_next(): return lax.ppermute(value, ('fsdp_1', 'pipe', 'dp'), route)]
    all_to_all x2, waiting for transfers between devices: 13.4 us -> 31.7 us  [from_everyone(): lax.all_to_all(copies, axis, split_axis=0, concat_axis=0, tiled=True)]
    ppermute x3 -> x0, starting transfers between devices: 11.7 us -> none  [from_next(): return lax.ppermute(value, ('fsdp_1', 'pipe', 'dp'), route)]
    all_to_all x1, starting transfers between devices: 12 us -> 6.56 us  [summed_on_arrival(): lax.all_to_all(blocks, axis, split_axis=0, concat_axis=0, tiled=True)]
    all_to_all x1, waiting for transfers between devices: 12.9 us -> 17.7 us  [summed_on_arrival(): lax.all_to_all(blocks, axis, split_axis=0, concat_axis=0, tiled=True)]
    dot_general x2 -> x0, matrix products: 3.34 us -> none  [contract_last(): lax.dot_general(left, right, (((1,), (1,)), ((), ())), preferred_element_...]
    all_to_all x2, starting transfers between devices: 20.5 us -> 23.5 us  [from_everyone(): lax.all_to_all(copies, axis, split_axis=0, concat_axis=0, tiled=True)]
    dot_general x7 -> x6, matrix products: 3.94 us -> 5.18 us  [times(): return jnp.dot(left, right, preferred_element_type=jnp.float32)]
  transfers between devices with their start and end apart: 10 -> 7, of which waited for: 6 -> 5; matrix products, arithmetic and copies ran while one was open for 7% -> 9% of each run, Pallas kernels for 0% -> 0%
where the time goes in v6:
time: 152 us; the launch traced here: 151 us
  waiting for transfers between devices  87.5 us (58%)
  starting transfers between devices  41.5 us (27%)
  local copies, waits for them, and re-layouts  7.4 us (5%)
  other arithmetic  6.83 us (4%)
  matrix products  6.02 us (4%)
    all_to_all x2, waiting for transfers between devices, from_everyone(): lax.all_to_all(copies, axis, split_axis=0, concat_axis=0, tiled=True)  31.7 us
    ppermute x1, waiting for transfers between devices, body(): returned = lax.ppermute(returning, 'pipe', [(1, 0)])  27.5 us
    all_to_all x2, starting transfers between devices, from_everyone(): lax.all_to_all(copies, axis, split_axis=0, concat_axis=0, tiled=True)  23.5 us
    all_to_all x1, waiting for transfers between devices, summed_on_arrival(): lax.all_to_all(blocks, axis, split_axis=0, concat_axis=0, tiled=True)  17.7 us
    all_to_all x1, waiting for transfers between devices, body(): lax.all_to_all(message.reshape(plane_count, *message.shape[2:]), PLANE, 0...  10.6 us
    all_to_all x1, starting transfers between devices, summed_on_arrival(): lax.all_to_all(blocks, axis, split_axis=0, concat_axis=0, tiled=True)  6.56 us
    all_to_all x1, starting transfers between devices, body(): lax.all_to_all(message.reshape(plane_count, *message.shape[2:]), PLANE, 0...  6.19 us
    dot_general x6, matrix products, times(): return jnp.dot(left, right, preferred_element_type=jnp.float32)  5.18 us
  transfers between devices with their start and end apart: 7, of which 5 were waited for; matrix products, arithmetic and copies ran while one was open for 9% of the time, Pallas kernels for 0%

profile of v6, /device:TPU:32, one launch (start us, length us, event | category | flops | bytes accessed | tf_op | source)
XLA Modules:
  0.0 150.9 jit_solution(12378039471735660752)
XLA Ops:
  0.6 2.7 %collective-permute-start.3 = (bf16[128,2560]{1,0:T(8,128)(2,1)}, bf16[128,2560]{1,0:T(8,128)(2,1)}, u32[]{:S(2)}, u32[]{:S(2)}) collective-permute-start(bf16[128,2560]{1,0:T(8,128)(2,1)} %bitcast.137), channel_id=1, source_target_pairs={{0,8},{1,9},{2,10},{3,11},{4,12},{5,13},{6,14},{7,15},{16,24},{17,... | collective-permute-start | bytes 1966088 | tf_op jit(solution)/shard_map/ppermute | solution.py:122
  4.0 0.7 fusion.97
  4.8 0.7 fusion.106
  5.5 70.8 %conditional.2 = (f32[2,5248]{1,0:T(2,128)S(1)}, f32[2,256]{1,0:T(2,128)S(1)}, f32[2,256]{1,0:T(2,128)S(1)}, f32[2,1]{0,1:T(1,128)S(1)}, f32[2,2560]{1,0:T(2,128...) conditional(s32[]{:T(128)} %convert_element_type.133, ...), branch_computations={%region_2.7_spmd, %region_7.8_spmd} | conditional | flops 153511936 | bytes 43018764 | solution.py:201
  5.5 1.6 %fusion.109 = (f32[2]{0:T(128)S(1)}, f32[2,2560]{1,0:T(2,128)S(1)}) fusion(bf16[1,128,2560]{2,1,0:T(8,128)(2,1)} %get-tuple-element.183, f32[2,128]{1,0:T(2,128)S(1)} %get-tuple-element.92), kind=kOutput, calls=%fused_computation.216 | convolution fusion | flops 1316094 | bytes 676872 | tf_op jit(solution)/shard_map/cond/branch_0_fun/dot_general | solution.py:61
  7.4 0.9 broadcast_in_dim.63
  8.3 17.8 %all-to-all-start.5 = ((bf16[32,2,2560]{2,1,0:T(2,128)(2,1)}), bf16[32,2,2560]{2,1,0:T(2,128)(2,1)S(1)}, u32[]{:S(2)}, u32[]{:S(2)}) async-start(bf16[32,2,2560]{2,1,0:T(2,128)(2,1)} %broadcast_in_dim.63), calls=%async_computation.5 | async-start | bytes 655360 | tf_op jit(solution)/shard_map/cond/branch_0_fun/all_to_all | solution.py:21
  26.1 19.3 %all-to-all-done.5 = bf16[32,2,2560]{2,1,0:T(2,128)(2,1)S(1)} async-done(((bf16[32,2,2560]{2,1,0:T(2,128)(2,1)}), bf16[32,2,2560]{2,1,0:T(2,128)(2,1)S(1)}, u32[]{:S(2)}, u32[]{:S(2)}) %all-to-all-start.5) | async-done | bytes 327712 | tf_op jit(solution)/shard_map/cond/branch_0_fun/all_to_all | solution.py:21
  45.8 1.7 %convolution_convert_fusion = bf16[64,2560]{1,0:T(8,128)(2,1)} fusion(bf16[224,2560]{1,0:T(8,128)(2,1)S(1)} %copy-done.1, bf16[64,2560]{1,0:T(8,128)(2,1)S(1)} %reshape.257, bf16[224,2560]{1,0:T(8,128)(2,1)S(1)} %copy-done.7), kind=kOutput, calls=%fused_computation | convolution fusion | flops 147093504 | bytes 2949120 | tf_op jit(solution)/shard_map/cond/branch_0_fun/dot_general | solution.py:61
  47.5 1.1 concatenate.34
  48.7 1.1 pad_maximum_fusion
  49.7 6.6 %all-to-all-start.6 = ((bf16[32,2,2816]{2,1,0:T(2,128)(2,1)}), bf16[32,2,2816]{2,1,0:T(2,128)(2,1)S(1)}, u32[]{:S(2)}, u32[]{:S(2)}) async-start(bf16[32,2,2816]{2,1,0:T(2,128)(2,1)} %pad_maximum_fusion), calls=%async_computation.6 | async-start | bytes 720896 | tf_op jit(solution)/shard_map/cond/branch_0_fun/all_to_all | solution.py:27
  56.5 0.7 constant_dynamic-slice_fusion
  57.2 17.7 %all-to-all-done.6 = bf16[32,2,2816]{2,1,0:T(2,128)(2,1)S(1)} async-done(((bf16[32,2,2816]{2,1,0:T(2,128)(2,1)}), bf16[32,2,2816]{2,1,0:T(2,128)(2,1)S(1)}, u32[]{:S(2)}, u32[]{:S(2)}) %all-to-all-start.6) | async-done | bytes 360480 | tf_op jit(solution)/shard_map/cond/branch_0_fun/all_to_all | solution.py:27
  75.4 0.7 multiply_bitcast_fusion
  76.3 1.3 collective-permute-start.2
  77.7 1.3 fusion.98
  79.0 20.6 %conditional.3 = (f32[32]{0:T(128)S(1)}, f32[32,256]{1,0:T(8,128)S(1)}, f32[32,256]{1,0:T(8,128)S(1)}, f32[32]{0:T(128)S(1)}, bf16[32,160]{1,0:T(8,128)(2,1)}, /...) conditional(s32[]{:T(128)} %convert_element_type.133, (f32[1,256]{1,0:T(1,128)}, f32[2,256]{1,0:T(2,128)S(1)}, ...), branch_computations={%region_8.9_spmd, %region_9.22_spmd} | conditional | flops 307935200 | bytes 22138064 | solution.py:281
  79.0 0.7 copy.115
  79.9 0.7 multiply_convert_fusion.1
  80.6 0.6 broadcast_in_dim.66
  81.2 5.7 %all-to-all-start = ((bf16[16,2,640]{2,1,0:T(2,128)(2,1)}), bf16[16,2,640]{2,1,0:T(2,128)(2,1)S(1)}, u32[]{:S(2)}, u32[]{:S(2)}) async-start(bf16[16,2,640]{2,1,0:T(2,128)(2,1)} %broadcast_in_dim.66), calls=%async_computation | async-start | bytes 81920 | tf_op jit(solution)/shard_map/cond/branch_0_fun/all_to_all | solution.py:21
  86.9 12.4 %all-to-all-done = bf16[16,2,640]{2,1,0:T(2,128)(2,1)S(1)} async-done(((bf16[16,2,640]{2,1,0:T(2,128)(2,1)}), bf16[16,2,640]{2,1,0:T(2,128)(2,1)S(1)}, u32[]{:S(2)}, u32[]{:S(2)}) %all-to-all-start) | async-done | bytes 40992 | tf_op jit(solution)/shard_map/cond/branch_0_fun/all_to_all | solution.py:21
  99.6 1.3 collective-permute-start.4
  100.9 0.8 reshape.272
  101.7 27.5 %collective-permute-done.4 = f32[32]{0:T(128)S(1)} collective-permute-done((f32[32]{0:T(128)S(1)}, f32[32]{0:T(128)S(1)}, u32[]{:S(2)}, u32[]{:S(2)}) %collective-permute-start.4) | collective-permute-done | bytes 160 | tf_op jit(solution)/shard_map/ppermute | solution.py:285
  129.6 0.9 copy.118
  130.4 6.2 %all-to-all-start.7 = ((bf16[16,34,384]{2,1,0:T(8,128)(2,1)}), bf16[16,34,384]{2,1,0:T(8,128)(2,1)S(1)}, u32[]{:S(2)}, u32[]{:S(2)}) async-start(bf16[16,34,384]{2,1,0:T(8,128)(2,1)} %copy.118), calls=%async_computation.7 | async-start | bytes 983040 | tf_op jit(solution)/shard_map/all_to_all | solution.py:299
  136.6 1.0 select_select_fusion
  137.6 10.6 %all-to-all-done.7 = bf16[16,34,384]{2,1,0:T(8,128)(2,1)S(1)} async-done(((bf16[16,34,384]{2,1,0:T(8,128)(2,1)}), bf16[16,34,384]{2,1,0:T(8,128)(2,1)S(1)}, u32[]{:S(2)}, u32[]{:S(2)}) %all-to-all-start.7) | async-done | bytes 417824 | tf_op jit(solution)/shard_map/all_to_all | solution.py:299
  148.2 0.8 convolution_bitcast_fusion
  149.6 0.7 copy.119
  (62 shorter events, 3.7 us)
Async XLA Ops:
  0.6 4.9 %copy-start = (f32[1,50,256]{2,0,1:T(1,128)S(1)}, f32[1,50,256]{2,0,1:T(1,128)}, u32[]{:S(2)}) copy-start(f32[1,50,256]{2,0,1:T(1,128)} %param.21) | copy-start | bytes 153604
  0.6 77.0 %collective-permute-start.3 = (bf16[128,2560]{1,0:T(8,128)(2,1)}, bf16[128,2560]{1,0:T(8,128)(2,1)}, u32[]{:S(2)}, u32[]{:S(2)}) collective-permute-start(bf16[128,2560]{1,0:T(8,128)(2,1)} %bitcast.137), channel_id=1, source_target_pairs={{0,8},{1,9},{2,10},{3,11},{4,12},{5,13},{6,14},{7,15},{16,24},{17,... | collective-permute-start | bytes 1966088 | tf_op jit(solution)/shard_map/ppermute | solution.py:122
  5.5 40.0 %copy-start.13 = (bf16[80,256]{1,0:T(8,128)(2,1)S(1)}, bf16[80,256]{1,0:T(8,128)(2,1)}, u32[]{:S(2)}) copy-start(bf16[80,256]{1,0:T(8,128)(2,1)} %get-tuple-element.97) | copy-start | bytes 122884 | tf_op jit(solution)/shard_map/cond
  5.5 40.3 %copy-start.1 = (bf16[224,2560]{1,0:T(8,128)(2,1)S(1)}, bf16[224,2560]{1,0:T(8,128)(2,1)}, u32[]{:S(2)}) copy-start(bf16[224,2560]{1,0:T(8,128)(2,1)} %get-tuple-element.95) | copy-start | bytes 3440644 | tf_op jit(solution)/shard_map/cond
  5.5 40.3 %copy-start.7 = (bf16[224,2560]{1,0:T(8,128)(2,1)S(1)}, bf16[224,2560]{1,0:T(8,128)(2,1)}, u32[]{:S(2)}) copy-start(bf16[224,2560]{1,0:T(8,128)(2,1)} %get-tuple-element.94) | copy-start | bytes 3440644 | tf_op jit(solution)/shard_map/cond
  8.3 37.1 %all-to-all-start.5 = ((bf16[32,2,2560]{2,1,0:T(2,128)(2,1)}), bf16[32,2,2560]{2,1,0:T(2,128)(2,1)S(1)}, u32[]{:S(2)}, u32[]{:S(2)}) async-start(bf16[32,2,2560]{2,1,0:T(2,128)(2,1)} %broadcast_in_dim.63), calls=%async_computation.5 | async-start | bytes 655360 | tf_op jit(solution)/shard_map/cond/branch_0_fun/all_to_all | solution.py:21
  48.6 26.6 %copy-start.14 = (f32[1,256]{1,0:T(1,128)S(1)}, f32[1,256]{1,0:T(1,128)}, u32[]{:S(2)}) copy-start(f32[1,256]{1,0:T(1,128)} %get-tuple-element.99) | copy-start | bytes 3076 | tf_op jit(solution)/shard_map/cond
  48.6 27.4 %copy-start.5 = (bf16[128,2560]{1,0:T(8,128)(2,1)S(1)}, bf16[128,2560]{1,0:T(8,128)(2,1)}, u32[]{:S(2)}) copy-start(bf16[128,2560]{1,0:T(8,128)(2,1)} %get-tuple-element.100) | copy-start | bytes 1966084 | tf_op jit(solution)/shard_map/cond
  49.7 25.2 %all-to-all-start.6 = ((bf16[32,2,2816]{2,1,0:T(2,128)(2,1)}), bf16[32,2,2816]{2,1,0:T(2,128)(2,1)S(1)}, u32[]{:S(2)}, u32[]{:S(2)}) async-start(bf16[32,2,2816]{2,1,0:T(2,128)(2,1)} %pad_maximum_fusion), calls=%async_computation.6 | async-start | bytes 720896 | tf_op jit(solution)/shard_map/cond/branch_0_fun/all_to_all | solution.py:27
  76.3 2.7 %collective-permute-start.2 = (f32[2,5248]{1,0:T(2,128)S(1)}, f32[2,5248]{1,0:T(2,128)S(1)}, u32[]{:S(2)}, u32[]{:S(2)}) collective-permute-start(f32[2,5248]{1,0:T(2,128)S(1)} %get-tuple-element.164), channel_id=1, source_target_pairs={{0,8},{1,9},{2,10},{3,11},{4,12},{5,13},{6,14},{7,15},{16,24},{17,... | collective-permute-start | bytes 125960 | tf_op jit(solution)/shard_map/ppermute | solution.py:202
  81.2 18.1 %all-to-all-start = ((bf16[16,2,640]{2,1,0:T(2,128)(2,1)}), bf16[16,2,640]{2,1,0:T(2,128)(2,1)S(1)}, u32[]{:S(2)}, u32[]{:S(2)}) async-start(bf16[16,2,640]{2,1,0:T(2,128)(2,1)} %broadcast_in_dim.66), calls=%async_computation | async-start | bytes 81920 | tf_op jit(solution)/shard_map/cond/branch_0_fun/all_to_all | solution.py:21
  99.6 29.7 %collective-permute-start.4 = (f32[32]{0:T(128)S(1)}, f32[32]{0:T(128)S(1)}, u32[]{:S(2)}, u32[]{:S(2)}) collective-permute-start(f32[32]{0:T(128)S(1)} %get-tuple-element.175), channel_id=1, source_target_pairs={{8,0},{9,1},{10,2},{11,3},{12,4},{13,5},{14,6},{15,7},{24,16},{25,... | collective-permute-start | bytes 392 | tf_op jit(solution)/shard_map/ppermute | solution.py:285
  129.5 7.1 %copy-start.4 = (bf16[1,1,128,2560]{3,2,1,0:T(8,128)(2,1)S(1)}, bf16[1,1,128,2560]{3,2,1,0:T(8,128)(2,1)}, u32[]{:S(2)}) copy-start(bf16[1,1,128,2560]{3,2,1,0:T(8,128)(2,1)} %param.15) | copy-start | bytes 1966084
  130.4 17.8 %all-to-all-start.7 = ((bf16[16,34,384]{2,1,0:T(8,128)(2,1)}), bf16[16,34,384]{2,1,0:T(8,128)(2,1)S(1)}, u32[]{:S(2)}, u32[]{:S(2)}) async-start(bf16[16,34,384]{2,1,0:T(8,128)(2,1)} %copy.118), calls=%async_computation.7 | async-start | bytes 983040 | tf_op jit(solution)/shard_map/all_to_all | solution.py:299

commit v7 on v6

--- a/solution.py
+++ b/solution.py
@@ -2,6 +2,7 @@
 import jax.numpy as jnp
 from jax import lax
 from jax.experimental import pallas as pl
+from jax.experimental.pallas import tpu as pltpu
 from jax.sharding import Mesh
 from jax.sharding import PartitionSpec as P
 
@@ -72,6 +73,63 @@
         out_shape=[jax.ShapeDtypeStruct(shape, dtype) for shape, dtype in arrays],
         out_specs=[pl.BlockSpec(memory_space=pl.ANY)] * len(arrays),
     )()
+
+
+def final_message(flags, returned, logit, pull, value, shards, plane_count):
+    rows, hidden = pull.shape
+    per_shard = plane_count // shards.shape[0]
+    lanes = shards.shape[2]
+
+    def kernel(flags_ref, returned_ref, logit_ref, pull_ref, value_ref, shards_ref, out_ref):
+        scale = jnp.where(flags_ref[0] > 0, 1.0, returned_ref[...])
+        grads = logit_ref[...] * scale
+        hidden_rows = (grads * pull_ref[...]).astype(jnp.bfloat16)
+        out_row = jnp.sum(grads * value_ref[...], axis=0, keepdims=True)
+        place = lax.broadcasted_iota(jnp.int32, (8, hidden), 0)
+        tail = jnp.where(place == 0, out_row, jnp.where(place == 1, flags_ref[1], 0.0))
+        tail = tail.astype(jnp.bfloat16)
+        for target in range(plane_count):
+            out_ref[target, :rows, :hidden] = hidden_rows
+            out_ref[target, :rows, hidden:] = shards_ref[target // per_shard]
+            out_ref[target, rows:, :hidden] = tail
+            out_ref[target, rows:, hidden:] = jnp.zeros((8, lanes), jnp.bfloat16)
+
+    vmem = pl.BlockSpec(memory_space=pltpu.VMEM)
+    return pl.pallas_call(
+        kernel,
+        out_shape=jax.ShapeDtypeStruct((plane_count, rows + 8, hidden + lanes), jnp.bfloat16),
+        in_specs=[pl.BlockSpec(memory_space=pltpu.SMEM)] + [vmem] * 5,
+        out_specs=vmem,
+    )(flags, returned, logit, pull, value, shards)
+
+
+def final_sums(arrived, rows, hidden, shard_cols, step_count):
+    plane_count = arrived.shape[0]
+
+    def kernel(arrived_ref, in_ref, bias_ref, out_ref):
+        place = lax.broadcasted_iota(jnp.int32, (step_count, hidden), 0).astype(jnp.float32)
+        in_sum = jnp.zeros((arrived.shape[2] - hidden, hidden), jnp.float32)
+        bias_sum = jnp.zeros((step_count, hidden), jnp.float32)
+        out_sum = jnp.zeros((1, hidden), jnp.float32)
+        for source in range(plane_count):
+            hidden_rows = arrived_ref[source, :rows, :hidden]
+            in_sum += contract_first(arrived_ref[source, :rows, hidden:], hidden_rows)
+            tail = arrived_ref[source, rows:, :hidden].astype(jnp.float32)
+            total = jnp.sum(hidden_rows.astype(jnp.float32), axis=0, keepdims=True)
+            bias_sum += jnp.where(place == tail[1:2], total, 0.0)
+            out_sum += tail[:1]
+        in_ref[...] = in_sum[:shard_cols]
+        bias_ref[...] = bias_sum
+        out_ref[...] = out_sum
+
+    vmem = pl.BlockSpec(memory_space=pltpu.VMEM)
+    shapes = [(shard_cols, hidden), (step_count, hidden), (1, hidden)]
+    return pl.pallas_call(
+        kernel,
+        out_shape=[jax.ShapeDtypeStruct(shape, jnp.float32) for shape in shapes],
+        in_specs=[vmem],
+        out_specs=[vmem] * 3,
+    )(arrived)
 
 
 def pick_fresh(mask_row):
@@ -148,6 +206,10 @@
         own_units = w_down.shape[0]
         return times(act[:, :own_units], w_down) + times(act[:, own_units:], other_down)
 
+    def shards_of(columns):
+        shards = jnp.moveaxis(columns.reshape(group_rows, near_count, shard_cols), 1, 0)
+        return jnp.pad(shards, ((0, 0), (0, 0), (0, 128 - shard_cols)))
+
     def first_part():
         rows_first = rows_at(picked, video_tokens[0])
         rows_cached = rows_at(picked, cached)
@@ -187,8 +249,6 @@
         other_up = from_next(w_up, 1)
         other_down = from_next(w_down, 1)
         whole_in = from_everyone(pieces, PLANE)
-        whole_in = whole_in.reshape(near_count, dp_count, along_count, piece, hidden)
-        whole_in = whole_in.transpose(2, 0, 1, 3, 4).reshape(features, hidden)
         act_grad = jnp.concatenate(
             [contract_last(group, w_down), contract_last(group, other_down)], axis=1
         )
@@ -239,6 +299,9 @@
         terms = terms.astype(jnp.bfloat16).reshape(along_count, FRESH, features)
         sums = summed_on_arrival(jnp.concatenate([terms, parts], axis=2), "fsdp_0")
 
+        piece = shard_cols // dp_count
+        whole_in = whole_in.reshape(near_count, dp_count, along_count, piece, hidden)
+        whole_in = whole_in.transpose(2, 0, 1, 3, 4).reshape(features, hidden)
         routed = times(stacked, whole_in)
         value, slope, gate = gate_of(routed[:group_rows] + bias_row)
         pull = r_out[None, :] * slope
@@ -253,14 +316,17 @@
         input_grad = live_group * gate * (
             numbers[:, 5:6] + numbers[:, 6:7] + slope_dot
         ) + logit_grad * pull_tangent
-        returning = (numbers[:, 1:3] * input_grad).reshape(along_count, FRESH, FRESH)
+        by_first = numbers[:, 1:3] * input_grad
+        even = (jnp.arange(group_rows) % FRESH == 0)[:, None]
+        partner = jnp.where(even, jnp.roll(by_first, -1, axis=0), jnp.roll(by_first, 1, axis=0))
+        by_first = by_first + partner
         return (
-            jnp.sum(returning, axis=1).reshape(group_rows),
+            jnp.where(even, by_first[:, :1], by_first[:, 1:]),
             rows_cached + live * gate_own * change,
             value,
             pull,
-            logit_grad[:, 0],
-            columns_of(stacked)[:group_rows],
+            logit_grad,
+            shards_of(columns_of(stacked[:group_rows])),
         )
 
     def first_waits():
@@ -270,48 +336,31 @@
         rows = jnp.concatenate([r_out[None, :] * slope_first, value_first, factors], axis=1)
         rows = from_everyone(rows.astype(jnp.bfloat16), "fsdp_0").astype(jnp.float32)
         return (
-            jnp.zeros((group_rows,), jnp.float32),
+            jnp.zeros((group_rows, 1), jnp.float32),
             rows_cached + passing[:, :features],
             rows[:, hidden : 2 * hidden],
             rows[:, :hidden],
-            rows[:, 2 * hidden] + rows[:, 2 * hidden + 1],
-            columns_first,
-        )
-
-    returning, new_rows, value, pull, logit_grad, pair_columns = lax.cond(
+            rows[:, 2 * hidden : 2 * hidden + 1] + rows[:, 2 * hidden + 1 : 2 * hidden + 2],
+            shards_of(columns_first),
+        )
+
+    returning, new_rows, value, pull, logit_grad, shards = lax.cond(
         second_section, second_part, first_waits
     )
 
     returned = lax.ppermute(returning, "pipe", [(1, 0)])
-    logit_grad = (jnp.where(second_section, 1.0, returned) * logit_grad)[:, None]
-    hidden_rows = (logit_grad * pull).astype(jnp.bfloat16)
-    out_row = jnp.sum(logit_grad * value, axis=0, keepdims=True)
-    step_row = jnp.broadcast_to(timestep[0].astype(jnp.float32), (1, hidden))
-    hidden_part = jnp.concatenate(
-        [hidden_rows, out_row.astype(jnp.bfloat16), step_row.astype(jnp.bfloat16)]
-    )
-    shards = jnp.moveaxis(pair_columns.reshape(group_rows, near_count, shard_cols), 1, 0)
-    shards = jnp.pad(shards, ((0, 0), (0, 2), (0, 128 - shard_cols)))
-    message = jnp.concatenate(
-        [jnp.broadcast_to(hidden_part, (near_count, *hidden_part.shape)), shards], axis=2
-    )
-    message = jnp.broadcast_to(message[:, None], (near_count, dp_count, *message.shape[1:]))
-    arrived = lax.all_to_all(
-        message.reshape(plane_count, *message.shape[2:]), PLANE, 0, 0, tiled=True
-    )
-    plane_rows = arrived[:, :group_rows].reshape(plane_count * group_rows, -1)
-    hidden_rows = plane_rows[:, :hidden]
-    summed_in = contract_first(plane_rows[:, hidden : hidden + shard_cols], hidden_rows)
-    steps = jnp.arange(router_bias.shape[1]).astype(jnp.bfloat16)
-    is_step = (steps[:, None] == arrived[:, group_rows + 1, 0][None, :]).astype(jnp.bfloat16)
-    summed_bias = times(jnp.repeat(is_step, group_rows, axis=1), hidden_rows)
-    summed_out = jnp.sum(arrived[:, group_rows, :hidden].astype(jnp.float32), axis=0)
+    flags = jnp.stack([second_section.astype(jnp.float32), timestep[0].astype(jnp.float32)])
+    message = final_message(flags, returned, logit_grad, pull, value, shards, plane_count)
+    arrived = lax.all_to_all(message, PLANE, split_axis=0, concat_axis=0, tiled=True)
+    summed_in, summed_bias, summed_out = final_sums(
+        arrived, group_rows, hidden, shard_cols, router_bias.shape[1]
+    )
 
     new_rows = new_rows.astype(jnp.bfloat16)
     blended = cached
     for row in range(FRESH):
         blended = jnp.where(picked[row][:, None] > 0, new_rows[row][None, :], blended)
-    return (blended[None, None], summed_in[None], summed_bias[None], summed_out[None])
+    return (blended[None, None], summed_in[None], summed_bias[None], summed_out)
 
 
 def solution(mesh):

time: 152 us -> 153 us (level)
  Pallas kernels: 0.01 us -> 3.81 us
  matrix products: 6.02 us -> 4.24 us
    pallas_call x0 -> x2, Pallas kernels: none -> 3.81 us  [the longest x1 2.14 us: final_sums(): pl.pallas_call(kernel, out_shape=[jax.ShapeDtypeStruct(shape, jnp.float32...]
    unnamed x5 -> x13, local copies, waits for them, and re-layouts: 0.69 us -> 2.88 us
    reshape x3 -> x1, local copies, waits for them, and re-layouts: 1.72 us -> 0.08 us  [shards_of(): columns.reshape(group_rows, near_count, shard_cols)]
    dot_general x6 -> x5, matrix products: 5.18 us -> 4.24 us  [times(): return jnp.dot(left, right, preferred_element_type=jnp.float32)]
  transfers between devices with their start and end apart: 7 -> 7, of which waited for: 5 -> 5; matrix products, arithmetic and copies ran while one was open for 9% -> 7% of each run, Pallas kernels for 0% -> 0%
where the time goes in v7:
time: 153 us; the launch traced here: 152 us
  waiting for transfers between devices  87.3 us (57%)
  starting transfers between devices  40.9 us (27%)
  local copies, waits for them, and re-layouts  7.87 us (5%)
  other arithmetic  6.38 us (4%)
  matrix products  4.24 us (3%)
  Pallas kernels  3.81 us (2%)
    all_to_all x2, waiting for transfers between devices, from_everyone(): lax.all_to_all(copies, axis, split_axis=0, concat_axis=0, tiled=True)  31.5 us
    ppermute x1, waiting for transfers between devices, body(): returned = lax.ppermute(returning, 'pipe', [(1, 0)])  27.1 us
    all_to_all x2, starting transfers between devices, from_everyone(): lax.all_to_all(copies, axis, split_axis=0, concat_axis=0, tiled=True)  23.5 us
    all_to_all x1, waiting for transfers between devices, summed_on_arrival(): lax.all_to_all(blocks, axis, split_axis=0, concat_axis=0, tiled=True)  18.3 us
    all_to_all x1, waiting for transfers between devices, body(): lax.all_to_all(message, PLANE, split_axis=0, concat_axis=0, tiled=True)  10.4 us
    all_to_all x1, starting transfers between devices, summed_on_arrival(): lax.all_to_all(blocks, axis, split_axis=0, concat_axis=0, tiled=True)  6.56 us
    all_to_all x1, starting transfers between devices, body(): lax.all_to_all(message, PLANE, split_axis=0, concat_axis=0, tiled=True)  5.49 us
    dot_general x5, matrix products, times(): return jnp.dot(left, right, preferred_element_type=jnp.float32)  4.24 us
  transfers between devices with their start and end apart: 7, of which 5 were waited for; matrix products, arithmetic and copies ran while one was open for 7% of the time, Pallas kernels for 0%

profile of v7, /device:TPU:32, one launch (start us, length us, event | category | flops | bytes accessed | tf_op | source)
XLA Modules:
  0.0 152.2 jit_solution(11880786124205325299)
XLA Ops:
  0.6 2.7 %collective-permute-start.3 = (bf16[128,2560]{1,0:T(8,128)(2,1)}, bf16[128,2560]{1,0:T(8,128)(2,1)}, u32[]{:S(2)}, u32[]{:S(2)}) collective-permute-start(bf16[128,2560]{1,0:T(8,128)(2,1)} %bitcast.128), channel_id=1, source_target_pairs={{0,8},{1,9},{2,10},{3,11},{4,12},{5,13},{6,14},{7,15},{16,24},{17,... | collective-permute-start | bytes 1966088 | tf_op jit(solution)/shard_map/ppermute | solution.py:180
  3.4 0.7 fusion.92
  5.0 68.4 %conditional.2 = (f32[2,5248]{1,0:T(2,128)S(1)}, f32[2,256]{1,0:T(2,128)S(1)}, f32[2,256]{1,0:T(2,128)S(1)}, f32[2,1]{0,1:T(1,128)S(1)}, f32[2,2560]{1,0:T(2,128...) conditional(s32[]{:T(128)} %convert_element_type.100, ...), branch_computations={%region_2.7_spmd, %region_7.8_spmd} | conditional | flops 153511936 | bytes 32696736 | solution.py:261
  5.1 1.6 %fusion.104 = (f32[2]{0:T(128)S(1)}, f32[2,2560]{1,0:T(2,128)S(1)}) fusion(bf16[1,128,2560]{2,1,0:T(8,128)(2,1)} %get-tuple-element.180, f32[2,128]{1,0:T(2,128)S(1)} %get-tuple-element.85), kind=kOutput, calls=%fused_computation.203 | convolution fusion | flops 1316094 | bytes 676872 | tf_op jit(solution)/shard_map/cond/branch_0_fun/dot_general | solution.py:62
  6.9 0.9 broadcast_in_dim.69
  7.8 17.8 %all-to-all-start.5 = ((bf16[32,2,2560]{2,1,0:T(2,128)(2,1)}), bf16[32,2,2560]{2,1,0:T(2,128)(2,1)S(1)}, u32[]{:S(2)}, u32[]{:S(2)}) async-start(bf16[32,2,2560]{2,1,0:T(2,128)(2,1)} %broadcast_in_dim.69), calls=%async_computation.5 | async-start | bytes 655360 | tf_op jit(solution)/shard_map/cond/branch_0_fun/all_to_all | solution.py:22
  25.7 19.3 %all-to-all-done.5 = bf16[32,2,2560]{2,1,0:T(2,128)(2,1)S(1)} async-done(((bf16[32,2,2560]{2,1,0:T(2,128)(2,1)}), bf16[32,2,2560]{2,1,0:T(2,128)(2,1)S(1)}, u32[]{:S(2)}, u32[]{:S(2)}) %all-to-all-start.5) | async-done | bytes 327712 | tf_op jit(solution)/shard_map/cond/branch_0_fun/all_to_all | solution.py:22
  45.3 1.0 convolution_convert_fusion
  46.5 1.1 pad_maximum_fusion
  47.6 6.6 %all-to-all-start.6 = ((bf16[32,2,2816]{2,1,0:T(2,128)(2,1)}), bf16[32,2,2816]{2,1,0:T(2,128)(2,1)S(1)}, u32[]{:S(2)}, u32[]{:S(2)}) async-start(bf16[32,2,2816]{2,1,0:T(2,128)(2,1)} %pad_maximum_fusion), calls=%async_computation.6 | async-start | bytes 720896 | tf_op jit(solution)/shard_map/cond/branch_0_fun/all_to_all | solution.py:28
  54.4 18.3 %all-to-all-done.6 = bf16[32,2,2816]{2,1,0:T(2,128)(2,1)S(1)} async-done(((bf16[32,2,2816]{2,1,0:T(2,128)(2,1)}), bf16[32,2,2816]{2,1,0:T(2,128)(2,1)S(1)}, u32[]{:S(2)}, u32[]{:S(2)}) %all-to-all-start.6) | async-done | bytes 360480 | tf_op jit(solution)/shard_map/cond/branch_0_fun/all_to_all | solution.py:28
  73.5 1.3 collective-permute-start.2
  74.8 0.6 pad_maximum_fusion.11.flags_ref
  75.9 1.3 fusion.93
  77.2 22.1 %conditional.3 = (f32[32,1]{0,1:T(1,128)}, bf16[2,2560]{1,0:T(2,128)(2,1)S(1)}, f32[32,256]{1,0:T(8,128)}, f32[32,256]{1,0:T(8,128)S(1)}, f32[32,1]{1,0:T(8,128)}, /*index=5*/bf16[2,32,128]{2,1,0:T(8,128)(2,1)}) conditional(s32[]{:T(128)} %convert_element_type.100, (f32[2,5248]{1,0:T(2,128)S(1)}, f32[2,2560]{1,0:T(2,128)S(1)}, f32[1,256]{1,0:T(1,128)}, ...), branch_computations={%region_8.9_spmd, %region_9.21_spmd} | conditional | flops 307925728 | bytes 32406378 | solution.py:347
  77.5 0.7 multiply_convert_fusion.1
  78.2 0.6 broadcast_in_dim.82
  78.8 5.7 %all-to-all-start = ((bf16[16,2,640]{2,1,0:T(2,128)(2,1)}), bf16[16,2,640]{2,1,0:T(2,128)(2,1)S(1)}, u32[]{:S(2)}, u32[]{:S(2)}) async-start(bf16[16,2,640]{2,1,0:T(2,128)(2,1)} %broadcast_in_dim.82), calls=%async_computation | async-start | bytes 81920 | tf_op jit(solution)/shard_map/cond/branch_0_fun/all_to_all | solution.py:22
  84.7 0.6 pad.18.clone
  85.3 12.2 %all-to-all-done = bf16[16,2,640]{2,1,0:T(2,128)(2,1)S(1)} async-done(((bf16[16,2,640]{2,1,0:T(2,128)(2,1)}), bf16[16,2,640]{2,1,0:T(2,128)(2,1)S(1)}, u32[]{:S(2)}, u32[]{:S(2)}) %all-to-all-start) | async-done | bytes 40992 | tf_op jit(solution)/shard_map/cond/branch_0_fun/all_to_all | solution.py:22
  97.5 0.6 fusion.102
  98.2 0.7 slice_add_fusion.3
  99.4 0.8 copy.119
  100.1 1.3 collective-permute-start.4
  101.5 27.1 %collective-permute-done.4.returned_ref = f32[32,1]{1,0:T(8,128)S(1)} collective-permute-done((f32[32,1]{1,0:T(8,128)S(1)}, f32[32,1]{1,0:T(8,128)S(1)}, u32[]{:S(2)}, u32[]{:S(2)}) %collective-permute-start.4) | collective-permute-done | bytes 160 | tf_op jit(solution)/shard_map/ppermute | solution.py:351
  129.1 1.7 %shard_map.131 = bf16[16,40,384]{2,1,0:T(8,128)(2,1)} custom-call(f32[2]{0:T(128)} %pad_maximum_fusion.11.flags_ref, f32[32,1]{1,0:T(8,128)} %copy-done.15, f32[32,1]{1,0:T(8,128)} %get-tuple-element.365.logit_ref, f32[32,256]{1,0:T(8,128)S(1)} %get-tuple-element.171.pull_ref, f32[32,256]{1,0:T(8,128)} %get-tuple-element.172.value_ref, ...), custom_call_target="tpu_custom_call" | custom-call | tf_op jit(solution)/shard_map/pallas_call | solution.py:98
  130.8 5.5 %all-to-all-start.7 = ((bf16[16,40,384]{2,1,0:T(8,128)(2,1)}), bf16[16,40,384]{2,1,0:T(8,128)(2,1)S(1)}, u32[]{:S(2)}, u32[]{:S(2)}) async-start(bf16[16,40,384]{2,1,0:T(8,128)(2,1)} %shard_map.131), calls=%async_computation.7 | async-start | bytes 983040 | tf_op jit(solution)/shard_map/all_to_all | solution.py:354
  136.3 1.0 select_select_fusion
  137.3 10.4 %all-to-all-done.7.arrived_ref = bf16[16,40,384]{2,1,0:T(8,128)(2,1)S(1)} async-done(((bf16[16,40,384]{2,1,0:T(8,128)(2,1)}), bf16[16,40,384]{2,1,0:T(8,128)(2,1)S(1)}, u32[]{:S(2)}, u32[]{:S(2)}) %all-to-all-start.7) | async-done | bytes 491552 | tf_op jit(solution)/shard_map/all_to_all | solution.py:354
  147.8 0.8 copy-done.12
  148.5 2.1 %shard_map.132 = (f32[80,256]{1,0:T(8,128)}, f32[50,256]{1,0:T(8,128)}, f32[1,256]{1,0:T(1,128)}) custom-call(bf16[16,40,384]{2,1,0:T(8,128)(2,1)} %copy-done.12), custom_call_target="tpu_custom_call" | custom-call | tf_op jit(solution)/shard_map/pallas_call | solution.py:127
  150.7 1.5 copy.122
  (58 shorter events, 4.2 us)
Async XLA Ops:
  0.6 4.4 %copy-start = (f32[1,50,256]{2,0,1:T(1,128)S(1)}, f32[1,50,256]{2,0,1:T(1,128)}, u32[]{:S(2)}) copy-start(f32[1,50,256]{2,0,1:T(1,128)} %param.21) | copy-start | bytes 153604
  0.6 75.3 %collective-permute-start.3 = (bf16[128,2560]{1,0:T(8,128)(2,1)}, bf16[128,2560]{1,0:T(8,128)(2,1)}, u32[]{:S(2)}, u32[]{:S(2)}) collective-permute-start(bf16[128,2560]{1,0:T(8,128)(2,1)} %bitcast.128), channel_id=1, source_target_pairs={{0,8},{1,9},{2,10},{3,11},{4,12},{5,13},{6,14},{7,15},{16,24},{17,... | collective-permute-start | bytes 1966088 | tf_op jit(solution)/shard_map/ppermute | solution.py:180
  5.0 40.0 %copy-start.14 = (bf16[80,256]{1,0:T(8,128)(2,1)S(1)}, bf16[80,256]{1,0:T(8,128)(2,1)}, u32[]{:S(2)}) copy-start(bf16[80,256]{1,0:T(8,128)(2,1)} %get-tuple-element.90) | copy-start | bytes 122884 | tf_op jit(solution)/shard_map/cond
  5.0 40.3 %copy-start.1 = (bf16[224,2560]{1,0:T(8,128)(2,1)S(1)}, bf16[224,2560]{1,0:T(8,128)(2,1)}, u32[]{:S(2)}) copy-start(bf16[224,2560]{1,0:T(8,128)(2,1)} %get-tuple-element.88) | copy-start | bytes 3440644 | tf_op jit(solution)/shard_map/cond
  5.1 40.3 %copy-start.7 = (bf16[224,2560]{1,0:T(8,128)(2,1)S(1)}, bf16[224,2560]{1,0:T(8,128)(2,1)}, u32[]{:S(2)}) copy-start(bf16[224,2560]{1,0:T(8,128)(2,1)} %get-tuple-element.87) | copy-start | bytes 3440644 | tf_op jit(solution)/shard_map/cond
  7.8 37.1 %all-to-all-start.5 = ((bf16[32,2,2560]{2,1,0:T(2,128)(2,1)}), bf16[32,2,2560]{2,1,0:T(2,128)(2,1)S(1)}, u32[]{:S(2)}, u32[]{:S(2)}) async-start(bf16[32,2,2560]{2,1,0:T(2,128)(2,1)} %broadcast_in_dim.69), calls=%async_computation.5 | async-start | bytes 655360 | tf_op jit(solution)/shard_map/cond/branch_0_fun/all_to_all | solution.py:22
  46.5 26.6 %copy-start.16 = (f32[1,256]{1,0:T(1,128)S(1)}, f32[1,256]{1,0:T(1,128)}, u32[]{:S(2)}) copy-start(f32[1,256]{1,0:T(1,128)} %get-tuple-element.92) | copy-start | bytes 3076 | tf_op jit(solution)/shard_map/cond
  46.5 26.7 %copy-start.5 = (bf16[128,2560]{1,0:T(8,128)(2,1)S(1)}, bf16[128,2560]{1,0:T(8,128)(2,1)}, u32[]{:S(2)}) copy-start(bf16[128,2560]{1,0:T(8,128)(2,1)} %get-tuple-element.93) | copy-start | bytes 1966084 | tf_op jit(solution)/shard_map/cond
  47.6 25.2 %all-to-all-start.6 = ((bf16[32,2,2816]{2,1,0:T(2,128)(2,1)}), bf16[32,2,2816]{2,1,0:T(2,128)(2,1)S(1)}, u32[]{:S(2)}, u32[]{:S(2)}) async-start(bf16[32,2,2816]{2,1,0:T(2,128)(2,1)} %pad_maximum_fusion), calls=%async_computation.6 | async-start | bytes 720896 | tf_op jit(solution)/shard_map/cond/branch_0_fun/all_to_all | solution.py:28
  73.5 3.7 %collective-permute-start.2 = (f32[2,5248]{1,0:T(2,128)S(1)}, f32[2,5248]{1,0:T(2,128)S(1)}, u32[]{:S(2)}, u32[]{:S(2)}) collective-permute-start(f32[2,5248]{1,0:T(2,128)S(1)} %get-tuple-element.156), channel_id=1, source_target_pairs={{0,8},{1,9},{2,10},{3,11},{4,12},{5,13},{6,14},{7,15},{16,24},{17,... | collective-permute-start | bytes 125960 | tf_op jit(solution)/shard_map/ppermute | solution.py:262
  78.8 18.7 %all-to-all-start = ((bf16[16,2,640]{2,1,0:T(2,128)(2,1)}), bf16[16,2,640]{2,1,0:T(2,128)(2,1)S(1)}, u32[]{:S(2)}, u32[]{:S(2)}) async-start(bf16[16,2,640]{2,1,0:T(2,128)(2,1)} %broadcast_in_dim.82), calls=%async_computation | async-start | bytes 81920 | tf_op jit(solution)/shard_map/cond/branch_0_fun/all_to_all | solution.py:22
  99.4 36.9 %copy-start.4 = (bf16[1,1,128,2560]{3,2,1,0:T(8,128)(2,1)S(1)}, bf16[1,1,128,2560]{3,2,1,0:T(8,128)(2,1)}, u32[]{:S(2)}) copy-start(bf16[1,1,128,2560]{3,2,1,0:T(8,128)(2,1)} %param.15) | copy-start | bytes 1966084
  99.4 36.9 %copy-start.20 = (pred[128]{0:T(512)(128)(4,1)S(1)}, pred[128]{0:T(512)(128)(4,1)}, u32[]{:S(2)}) copy-start(pred[128]{0:T(512)(128)(4,1)} %get-tuple-element.430) | copy-start | bytes 388
  99.4 37.0 %copy-start.21 = (pred[128]{0:T(512)(128)(4,1)S(1)}, pred[128]{0:T(512)(128)(4,1)}, u32[]{:S(2)}) copy-start(pred[128]{0:T(512)(128)(4,1)} %get-tuple-element.431) | copy-start | bytes 388
  100.1 28.4 %collective-permute-start.4 = (f32[32,1]{1,0:T(8,128)S(1)}, f32[32,1]{1,0:T(8,128)S(1)}, u32[]{:S(2)}, u32[]{:S(2)}) collective-permute-start(f32[32,1]{1,0:T(8,128)S(1)} %copy.119), channel_id=1, source_target_pairs={{8,0},{9,1},{10,2},{11,3},{12,4},{13,5},{14,6},{15,7},{24,16},{25,... | collective-permute-start | bytes 392 | tf_op jit(solution)/shard_map/ppermute | solution.py:351
  128.5 0.6 copy-start.15
  130.8 17.0 %all-to-all-start.7 = ((bf16[16,40,384]{2,1,0:T(8,128)(2,1)}), bf16[16,40,384]{2,1,0:T(8,128)(2,1)S(1)}, u32[]{:S(2)}, u32[]{:S(2)}) async-start(bf16[16,40,384]{2,1,0:T(8,128)(2,1)} %shard_map.131), calls=%async_computation.7 | async-start | bytes 983040 | tf_op jit(solution)/shard_map/all_to_all | solution.py:354
  147.8 0.8 copy-start.12

commit v8 on v7

--- a/solution.py
+++ b/solution.py
@@ -82,7 +82,9 @@
 
     def kernel(flags_ref, returned_ref, logit_ref, pull_ref, value_ref, shards_ref, out_ref):
         scale = jnp.where(flags_ref[0] > 0, 1.0, returned_ref[...])
-        grads = logit_ref[...] * scale
+        square = [lax.broadcasted_iota(jnp.int32, (rows, rows), axis) for axis in (0, 1)]
+        spread = jnp.where(square[0] == square[1], logit_ref[...] * scale, 0.0)
+        grads = jnp.sum(spread, axis=1, keepdims=True)
         hidden_rows = (grads * pull_ref[...]).astype(jnp.bfloat16)
         out_row = jnp.sum(grads * value_ref[...], axis=0, keepdims=True)
         place = lax.broadcasted_iota(jnp.int32, (8, hidden), 0)
@@ -100,36 +102,7 @@
         out_shape=jax.ShapeDtypeStruct((plane_count, rows + 8, hidden + lanes), jnp.bfloat16),
         in_specs=[pl.BlockSpec(memory_space=pltpu.SMEM)] + [vmem] * 5,
         out_specs=vmem,
-    )(flags, returned, logit, pull, value, shards)
-
-
-def final_sums(arrived, rows, hidden, shard_cols, step_count):
-    plane_count = arrived.shape[0]
-
-    def kernel(arrived_ref, in_ref, bias_ref, out_ref):
-        place = lax.broadcasted_iota(jnp.int32, (step_count, hidden), 0).astype(jnp.float32)
-        in_sum = jnp.zeros((arrived.shape[2] - hidden, hidden), jnp.float32)
-        bias_sum = jnp.zeros((step_count, hidden), jnp.float32)
-        out_sum = jnp.zeros((1, hidden), jnp.float32)
-        for source in range(plane_count):
-            hidden_rows = arrived_ref[source, :rows, :hidden]
-            in_sum += contract_first(arrived_ref[source, :rows, hidden:], hidden_rows)
-            tail = arrived_ref[source, rows:, :hidden].astype(jnp.float32)
-            total = jnp.sum(hidden_rows.astype(jnp.float32), axis=0, keepdims=True)
-            bias_sum += jnp.where(place == tail[1:2], total, 0.0)
-            out_sum += tail[:1]
-        in_ref[...] = in_sum[:shard_cols]
-        bias_ref[...] = bias_sum
-        out_ref[...] = out_sum
-
-    vmem = pl.BlockSpec(memory_space=pltpu.VMEM)
-    shapes = [(shard_cols, hidden), (step_count, hidden), (1, hidden)]
-    return pl.pallas_call(
-        kernel,
-        out_shape=[jax.ShapeDtypeStruct(shape, jnp.float32) for shape in shapes],
-        in_specs=[vmem],
-        out_specs=[vmem] * 3,
-    )(arrived)
+    )(flags, returned[None], logit[None], pull, value, shards)
 
 
 def pick_fresh(mask_row):
@@ -246,7 +219,9 @@
         sent = sent.reshape(along_count, FRESH + 1, features)
         group = sent[:, :FRESH].reshape(group_rows, features)
         pieces = sent[:, FRESH].reshape(along_count * piece, hidden)
-        other_up = from_next(w_up, 1)
+        half = w_up.shape[0] // 2
+        other_up = from_next(w_up[:half], 1)
+        other_up = jnp.concatenate([other_up, from_next(w_up[half:], 1)])
         other_down = from_next(w_down, 1)
         whole_in = from_everyone(pieces, PLANE)
         act_grad = jnp.concatenate(
@@ -288,7 +263,7 @@
         both = jnp.concatenate([scaled, tangent, numbers], axis=1).astype(jnp.bfloat16)
         both = from_everyone(both, "fsdp_0")
         stacked = jnp.concatenate([both[:, :features], both[:, features : 2 * features]])
-        numbers = both[:, 2 * features :].astype(jnp.float32)
+        numbers = both[:, 2 * features : 2 * features + 8].astype(jnp.float32).T
         pre_both = up_both(stacked, other_up)
         act, act_slope = gelu_both(pre_both[:group_rows])
         terms = down_both(act, other_down)
@@ -305,23 +280,24 @@
         routed = times(stacked, whole_in)
         value, slope, gate = gate_of(routed[:group_rows] + bias_row)
         pull = r_out[None, :] * slope
-        pull_tangent = jnp.sum(pull * routed[group_rows:], axis=1, keepdims=True)
+        pull_tangent = jnp.sum(pull * routed[group_rows:], axis=1)
         gate_own = lax.dynamic_slice_in_dim(gate, along * FRESH, FRESH)
         change = rows_second + sums[:, :features] - rows_cached
-        live_group = numbers[:, :1]
-        block_dot = sums[0, features : features + group_rows][:, None]
-        slope_dot = sums[1, features : features + group_rows][:, None]
-        gate_grad = live_group * (numbers[:, 3:4] + numbers[:, 4:5] + block_dot)
+        gate = gate[:, 0]
+        block_dot = sums[0, features : features + group_rows]
+        slope_dot = sums[1, features : features + group_rows]
+        gate_grad = numbers[0] * (numbers[3] + numbers[4] + block_dot)
         logit_grad = gate_grad * gate * (1.0 - gate)
-        input_grad = live_group * gate * (
-            numbers[:, 5:6] + numbers[:, 6:7] + slope_dot
-        ) + logit_grad * pull_tangent
-        by_first = numbers[:, 1:3] * input_grad
-        even = (jnp.arange(group_rows) % FRESH == 0)[:, None]
-        partner = jnp.where(even, jnp.roll(by_first, -1, axis=0), jnp.roll(by_first, 1, axis=0))
-        by_first = by_first + partner
+        input_grad = (
+            numbers[0] * gate * (numbers[5] + numbers[6] + slope_dot) + logit_grad * pull_tangent
+        )
+        even = jnp.arange(group_rows) % FRESH == 0
+        by_first = [numbers[1 + place] * input_grad for place in range(FRESH)]
+        by_first = [
+            part + jnp.where(even, jnp.roll(part, -1), jnp.roll(part, 1)) for part in by_first
+        ]
         return (
-            jnp.where(even, by_first[:, :1], by_first[:, 1:]),
+            jnp.where(even, by_first[0], by_first[1]),
             rows_cached + live * gate_own * change,
             value,
             pull,
@@ -336,11 +312,11 @@
         rows = jnp.concatenate([r_out[None, :] * slope_first, value_first, factors], axis=1)
         rows = from_everyone(rows.astype(jnp.bfloat16), "fsdp_0").astype(jnp.float32)
         return (
-            jnp.zeros((group_rows, 1), jnp.float32),
+            jnp.zeros((group_rows,), jnp.float32),
             rows_cached + passing[:, :features],
             rows[:, hidden : 2 * hidden],
             rows[:, :hidden],
-            rows[:, 2 * hidden : 2 * hidden + 1] + rows[:, 2 * hidden + 1 : 2 * hidden + 2],
+            rows[:, 2 * hidden] + rows[:, 2 * hidden + 1],
             shards_of(columns_first),
         )
 
@@ -352,15 +328,19 @@
     flags = jnp.stack([second_section.astype(jnp.float32), timestep[0].astype(jnp.float32)])
     message = final_message(flags, returned, logit_grad, pull, value, shards, plane_count)
     arrived = lax.all_to_all(message, PLANE, split_axis=0, concat_axis=0, tiled=True)
-    summed_in, summed_bias, summed_out = final_sums(
-        arrived, group_rows, hidden, shard_cols, router_bias.shape[1]
-    )
+    plane_rows = arrived[:, :group_rows].reshape(plane_count * group_rows, -1)
+    hidden_rows = plane_rows[:, :hidden]
+    summed_in = contract_first(plane_rows[:, hidden : hidden + shard_cols], hidden_rows)
+    steps = jnp.arange(router_bias.shape[1]).astype(jnp.bfloat16)
+    is_step = (steps[:, None] == arrived[:, group_rows + 1, 0][None, :]).astype(jnp.bfloat16)
+    summed_bias = times(jnp.repeat(is_step, group_rows, axis=1), hidden_rows)
+    summed_out = jnp.sum(arrived[:, group_rows, :hidden].astype(jnp.float32), axis=0)
 
     new_rows = new_rows.astype(jnp.bfloat16)
     blended = cached
     for row in range(FRESH):
         blended = jnp.where(picked[row][:, None] > 0, new_rows[row][None, :], blended)
-    return (blended[None, None], summed_in[None], summed_bias[None], summed_out)
+    return (blended[None, None], summed_in[None], summed_bias[None], summed_out[None])
 
 
 def solution(mesh):

time: 153 us -> 157 us (1.026)
  waiting for transfers between devices: 87.3 us -> 91.1 us
  local copies, waits for them, and re-layouts: 7.87 us -> 5.71 us
  Pallas kernels: 3.81 us -> 1.68 us
  starting transfers between devices: 40.9 us -> 43 us
    ppermute x1, waiting for transfers between devices: 27.1 us -> 30.8 us  [body(): returned = lax.ppermute(returning, 'pipe', [(1, 0)])]
    pallas_call x1 -> x0, Pallas kernels: 2.14 us -> none  [final_sums(): pl.pallas_call(kernel, out_shape=[jax.ShapeDtypeStruct(shape, jnp.float32...]
    all_to_all x1, starting transfers between devices: 5.49 us -> 7.44 us  [body(): lax.all_to_all(message, PLANE, split_axis=0, concat_axis=0, tiled=True)]
    unnamed x13 -> x11, local copies, waits for them, and re-layouts: 2.88 us -> 1.21 us
    dot_general x5 -> x6, matrix products: 4.24 us -> 4.44 us  [times(): return jnp.dot(left, right, preferred_element_type=jnp.float32)]
  transfers between devices with their start and end apart: 7 -> 7, of which waited for: 5 -> 5; matrix products, arithmetic and copies ran while one was open for 7% -> 8% of each run, Pallas kernels for 0% -> 0%
where the time goes in v8:
time: 157 us; the launch traced here: 156 us
  waiting for transfers between devices  91.1 us (58%)
  starting transfers between devices  43 us (27%)
  other arithmetic  7.12 us (5%)
  local copies, waits for them, and re-layouts  5.71 us (4%)
  matrix products  5.29 us (3%)
  Pallas kernels  1.68 us (1%)
    all_to_all x2, waiting for transfers between devices, from_everyone(): lax.all_to_all(copies, axis, split_axis=0, concat_axis=0, tiled=True)  31.5 us
    ppermute x1, waiting for transfers between devices, body(): returned = lax.ppermute(returning, 'pipe', [(1, 0)])  30.8 us
    all_to_all x2, starting transfers between devices, from_everyone(): lax.all_to_all(copies, axis, split_axis=0, concat_axis=0, tiled=True)  23.5 us
    all_to_all x1, waiting for transfers between devices, summed_on_arrival(): lax.all_to_all(blocks, axis, split_axis=0, concat_axis=0, tiled=True)  18.3 us
    all_to_all x1, waiting for transfers between devices, body(): lax.all_to_all(message, PLANE, split_axis=0, concat_axis=0, tiled=True)  10.4 us
    all_to_all x1, starting transfers between devices, body(): lax.all_to_all(message, PLANE, split_axis=0, concat_axis=0, tiled=True)  7.44 us
    all_to_all x1, starting transfers between devices, summed_on_arrival(): lax.all_to_all(blocks, axis, split_axis=0, concat_axis=0, tiled=True)  6.66 us
    dot_general x6, matrix products, times(): return jnp.dot(left, right, preferred_element_type=jnp.float32)  4.44 us
  transfers between devices with their start and end apart: 7, of which 5 were waited for; matrix products, arithmetic and copies ran while one was open for 8% of the time, Pallas kernels for 0%

profile of v8, /device:TPU:32, one launch (start us, length us, event | category | flops | bytes accessed | tf_op | source)
XLA Modules:
  0.0 155.6 jit_solution(1606314342385850034)
XLA Ops:
  0.6 2.7 %collective-permute-start.4 = (bf16[128,2560]{1,0:T(8,128)(2,1)}, bf16[128,2560]{1,0:T(8,128)(2,1)}, u32[]{:S(2)}, u32[]{:S(2)}) collective-permute-start(bf16[128,2560]{1,0:T(8,128)(2,1)} %bitcast.134), channel_id=1, source_target_pairs={{0,8},{1,9},{2,10},{3,11},{4,12},{5,13},{6,14},{7,15},{16,24},{17,... | collective-permute-start | bytes 1966088 | tf_op jit(solution)/shard_map/ppermute | solution.py:153
  3.4 0.7 fusion.98
  5.0 68.5 %conditional.2 = (f32[2,5248]{1,0:T(2,128)S(1)}, f32[2,256]{1,0:T(2,128)S(1)}, f32[2,256]{1,0:T(2,128)S(1)}, f32[2,1]{0,1:T(1,128)S(1)}, f32[2,2560]{1,0:T(2,128...) conditional(s32[]{:T(128)} %convert_element_type.112, ...), branch_computations={%region_2.7_spmd, %region_7.8_spmd} | conditional | flops 153511936 | bytes 37284296 | solution.py:236
  5.1 1.6 fusion.111
  6.9 0.9 broadcast_in_dim.56
  7.8 17.8 %all-to-all-start.5 = ((bf16[32,2,2560]{2,1,0:T(2,128)(2,1)}), bf16[32,2,2560]{2,1,0:T(2,128)(2,1)S(1)}, u32[]{:S(2)}, u32[]{:S(2)}) async-start(bf16[32,2,2560]{2,1,0:T(2,128)(2,1)} %broadcast_in_dim.56), calls=%async_computation.5 | async-start | bytes 655360 | tf_op jit(solution)/shard_map/cond/branch_0_fun/all_to_all | solution.py:22
  25.7 19.3 %all-to-all-done.5 = bf16[32,2,2560]{2,1,0:T(2,128)(2,1)S(1)} async-done(((bf16[32,2,2560]{2,1,0:T(2,128)(2,1)}), bf16[32,2,2560]{2,1,0:T(2,128)(2,1)S(1)}, u32[]{:S(2)}, u32[]{:S(2)}) %all-to-all-start.5) | async-done | bytes 327712 | tf_op jit(solution)/shard_map/cond/branch_0_fun/all_to_all | solution.py:22
  45.3 1.0 convolution_convert_fusion
  46.5 1.1 pad_maximum_fusion
  47.6 6.7 %all-to-all-start.6 = ((bf16[32,2,2816]{2,1,0:T(2,128)(2,1)}), bf16[32,2,2816]{2,1,0:T(2,128)(2,1)S(1)}, u32[]{:S(2)}, u32[]{:S(2)}) async-start(bf16[32,2,2816]{2,1,0:T(2,128)(2,1)} %pad_maximum_fusion), calls=%async_computation.6 | async-start | bytes 720896 | tf_op jit(solution)/shard_map/cond/branch_0_fun/all_to_all | solution.py:28
  54.5 18.3 %all-to-all-done.6 = bf16[32,2,2816]{2,1,0:T(2,128)(2,1)S(1)} async-done(((bf16[32,2,2816]{2,1,0:T(2,128)(2,1)}), bf16[32,2,2816]{2,1,0:T(2,128)(2,1)S(1)}, u32[]{:S(2)}, u32[]{:S(2)}) %all-to-all-start.6) | async-done | bytes 360480 | tf_op jit(solution)/shard_map/cond/branch_0_fun/all_to_all | solution.py:28
  73.6 1.3 collective-permute-start.3
  74.9 0.6 iota_convert_fusion
  75.5 0.6 pad_maximum_fusion.12.flags_ref
  76.6 1.3 fusion.99
  77.9 21.6 %conditional.3 = (f32[32]{0:T(128)}, bf16[2,2560]{1,0:T(2,128)(2,1)S(1)}, f32[32,256]{1,0:T(8,128)}, f32[32,256]{1,0:T(8,128)S(1)}, f32[1,32]{1,0:T(1,128)S(1)}, /*index=5*/bf16[2,32,128]{2,1,0:T(8,128)(2,1)}) conditional(s32[]{:T(128)} %convert_element_type.112, (f32[2,5248]{1,0:T(2,128)S(1)}, f32[2,2560]{1,0:T(2,128)S(1)}, f32[1,256]{1,0:T(1,128)}, ...), branch_computations={%region_8.9_spmd, %region_9.21_spmd} | conditional | flops 307921792 | bytes 30484502 | solution.py:323
  78.1 0.7 multiply_convert_fusion.1
  78.8 0.6 broadcast_in_dim.65
  79.5 5.7 %all-to-all-start = ((bf16[16,2,640]{2,1,0:T(2,128)(2,1)}), bf16[16,2,640]{2,1,0:T(2,128)(2,1)S(1)}, u32[]{:S(2)}, u32[]{:S(2)}) async-start(bf16[16,2,640]{2,1,0:T(2,128)(2,1)} %broadcast_in_dim.65), calls=%async_computation | async-start | bytes 81920 | tf_op jit(solution)/shard_map/cond/branch_0_fun/all_to_all | solution.py:22
  85.3 0.6 pad.18.clone
  85.9 12.2 %all-to-all-done = bf16[16,2,640]{2,1,0:T(2,128)(2,1)S(1)} async-done(((bf16[16,2,640]{2,1,0:T(2,128)(2,1)}), bf16[16,2,640]{2,1,0:T(2,128)(2,1)S(1)}, u32[]{:S(2)}, u32[]{:S(2)}) %all-to-all-start) | async-done | bytes 40992 | tf_op jit(solution)/shard_map/cond/branch_0_fun/all_to_all | solution.py:22
  98.1 0.6 fusion.110
  98.9 0.5 broadcast.242
  99.4 1.4 collective-permute-start.5
  100.9 30.8 %collective-permute-done.5 = f32[32]{0:T(128)S(1)} collective-permute-done((f32[32]{0:T(128)}, f32[32]{0:T(128)S(1)}, u32[]{:S(2)}, u32[]{:S(2)}) %collective-permute-start.5) | collective-permute-done | bytes 160 | tf_op jit(solution)/shard_map/ppermute | solution.py:327
  132.3 1.7 %shard_map.131 = bf16[16,40,384]{2,1,0:T(8,128)(2,1)} custom-call(f32[2]{0:T(128)} %pad_maximum_fusion.12.flags_ref, f32[1,32]{1,0:T(1,128)} %bitcast.159, f32[1,32]{1,0:T(1,128)S(1)} %get-tuple-element.168.logit_ref, f32[32,256]{1,0:T(8,128)S(1)} %get-tuple-element.169.pull_ref, f32[32,256]{1,0:T(8,128)} %get-tuple-element.170.value_ref, ...), custom_call_target="tpu_custom_call" | custom-call | tf_op jit(solution)/shard_map/pallas_call | solution.py:100
  134.0 7.4 %all-to-all-start.7 = ((bf16[16,40,384]{2,1,0:T(8,128)(2,1)}), bf16[16,40,384]{2,1,0:T(8,128)(2,1)S(1)}, u32[]{:S(2)}, u32[]{:S(2)}) async-start(bf16[16,40,384]{2,1,0:T(8,128)(2,1)} %shard_map.131), calls=%async_computation.7 | async-start | bytes 983040 | tf_op jit(solution)/shard_map/all_to_all | solution.py:330
  141.4 1.0 select_select_fusion
  142.4 10.4 %all-to-all-done.7 = bf16[16,40,384]{2,1,0:T(8,128)(2,1)S(1)} async-done(((bf16[16,40,384]{2,1,0:T(8,128)(2,1)}), bf16[16,40,384]{2,1,0:T(8,128)(2,1)S(1)}, u32[]{:S(2)}, u32[]{:S(2)}) %all-to-all-start.7) | async-done | bytes 491552 | tf_op jit(solution)/shard_map/all_to_all | solution.py:330
  152.9 0.8 convolution_bitcast_fusion
  154.3 0.7 copy.97
  155.0 0.6 fusion.97
  (62 shorter events, 4.3 us)
Async XLA Ops:
  0.6 4.4 %copy-start = (f32[1,50,256]{2,0,1:T(1,128)S(1)}, f32[1,50,256]{2,0,1:T(1,128)}, u32[]{:S(2)}) copy-start(f32[1,50,256]{2,0,1:T(1,128)} %param.21) | copy-start | bytes 153604
  0.6 75.9 %collective-permute-start.4 = (bf16[128,2560]{1,0:T(8,128)(2,1)}, bf16[128,2560]{1,0:T(8,128)(2,1)}, u32[]{:S(2)}, u32[]{:S(2)}) collective-permute-start(bf16[128,2560]{1,0:T(8,128)(2,1)} %bitcast.134), channel_id=1, source_target_pairs={{0,8},{1,9},{2,10},{3,11},{4,12},{5,13},{6,14},{7,15},{16,24},{17,... | collective-permute-start | bytes 1966088 | tf_op jit(solution)/shard_map/ppermute | solution.py:153
  5.0 40.0 %copy-start.12 = (bf16[80,256]{1,0:T(8,128)(2,1)S(1)}, bf16[80,256]{1,0:T(8,128)(2,1)}, u32[]{:S(2)}) copy-start(bf16[80,256]{1,0:T(8,128)(2,1)} %get-tuple-element.91) | copy-start | bytes 122884 | tf_op jit(solution)/shard_map/cond
  5.1 40.2 %copy-start.1 = (bf16[224,2560]{1,0:T(8,128)(2,1)S(1)}, bf16[224,2560]{1,0:T(8,128)(2,1)}, u32[]{:S(2)}) copy-start(bf16[224,2560]{1,0:T(8,128)(2,1)} %get-tuple-element.88) | copy-start | bytes 3440644 | tf_op jit(solution)/shard_map/cond
  5.1 40.2 %copy-start.4 = (bf16[224,2560]{1,0:T(8,128)(2,1)S(1)}, bf16[224,2560]{1,0:T(8,128)(2,1)}, u32[]{:S(2)}) copy-start(bf16[224,2560]{1,0:T(8,128)(2,1)} %get-tuple-element.89) | copy-start | bytes 3440644 | tf_op jit(solution)/shard_map/cond
  7.8 37.1 %all-to-all-start.5 = ((bf16[32,2,2560]{2,1,0:T(2,128)(2,1)}), bf16[32,2,2560]{2,1,0:T(2,128)(2,1)S(1)}, u32[]{:S(2)}, u32[]{:S(2)}) async-start(bf16[32,2,2560]{2,1,0:T(2,128)(2,1)} %broadcast_in_dim.56), calls=%async_computation.5 | async-start | bytes 655360 | tf_op jit(solution)/shard_map/cond/branch_0_fun/all_to_all | solution.py:22
  46.5 26.7 %copy-start.13 = (f32[1,256]{1,0:T(1,128)S(1)}, f32[1,256]{1,0:T(1,128)}, u32[]{:S(2)}) copy-start(f32[1,256]{1,0:T(1,128)} %get-tuple-element.93) | copy-start | bytes 3076 | tf_op jit(solution)/shard_map/cond
  46.5 26.8 %copy-start.8 = (bf16[128,2560]{1,0:T(8,128)(2,1)S(1)}, bf16[128,2560]{1,0:T(8,128)(2,1)}, u32[]{:S(2)}) copy-start(bf16[128,2560]{1,0:T(8,128)(2,1)} %get-tuple-element.94) | copy-start | bytes 1966084 | tf_op jit(solution)/shard_map/cond
  47.6 25.3 %all-to-all-start.6 = ((bf16[32,2,2816]{2,1,0:T(2,128)(2,1)}), bf16[32,2,2816]{2,1,0:T(2,128)(2,1)S(1)}, u32[]{:S(2)}, u32[]{:S(2)}) async-start(bf16[32,2,2816]{2,1,0:T(2,128)(2,1)} %pad_maximum_fusion), calls=%async_computation.6 | async-start | bytes 720896 | tf_op jit(solution)/shard_map/cond/branch_0_fun/all_to_all | solution.py:28
  73.6 4.3 %collective-permute-start.3 = (f32[2,5248]{1,0:T(2,128)S(1)}, f32[2,5248]{1,0:T(2,128)S(1)}, u32[]{:S(2)}, u32[]{:S(2)}) collective-permute-start(f32[2,5248]{1,0:T(2,128)S(1)} %get-tuple-element.154), channel_id=1, source_target_pairs={{0,8},{1,9},{2,10},{3,11},{4,12},{5,13},{6,14},{7,15},{16,24},{17,... | collective-permute-start | bytes 125960 | tf_op jit(solution)/shard_map/ppermute | solution.py:237
  79.5 18.6 %all-to-all-start = ((bf16[16,2,640]{2,1,0:T(2,128)(2,1)}), bf16[16,2,640]{2,1,0:T(2,128)(2,1)S(1)}, u32[]{:S(2)}, u32[]{:S(2)}) async-start(bf16[16,2,640]{2,1,0:T(2,128)(2,1)} %broadcast_in_dim.65), calls=%async_computation | async-start | bytes 81920 | tf_op jit(solution)/shard_map/cond/branch_0_fun/all_to_all | solution.py:22
  99.4 42.0 %copy-start.7 = (bf16[1,1,128,2560]{3,2,1,0:T(8,128)(2,1)S(1)}, bf16[1,1,128,2560]{3,2,1,0:T(8,128)(2,1)}, u32[]{:S(2)}) copy-start(bf16[1,1,128,2560]{3,2,1,0:T(8,128)(2,1)} %param.15) | copy-start | bytes 1966084
  99.4 42.0 %copy-start.17 = (pred[128]{0:T(512)(128)(4,1)S(1)}, pred[128]{0:T(512)(128)(4,1)}, u32[]{:S(2)}) copy-start(pred[128]{0:T(512)(128)(4,1)} %get-tuple-element.404) | copy-start | bytes 388
  99.4 32.3 %collective-permute-start.5 = (f32[32]{0:T(128)}, f32[32]{0:T(128)S(1)}, u32[]{:S(2)}, u32[]{:S(2)}) collective-permute-start(f32[32]{0:T(128)} %get-tuple-element.167), channel_id=1, source_target_pairs={{8,0},{9,1},{10,2},{11,3},{12,4},{13,5},{14,6},{15,7},{24,16},{25,... | collective-permute-start | bytes 392 | tf_op jit(solution)/shard_map/ppermute | solution.py:327
  131.8 0.5 copy-start.19
  134.0 18.9 %all-to-all-start.7 = ((bf16[16,40,384]{2,1,0:T(8,128)(2,1)}), bf16[16,40,384]{2,1,0:T(8,128)(2,1)S(1)}, u32[]{:S(2)}, u32[]{:S(2)}) async-start(bf16[16,40,384]{2,1,0:T(8,128)(2,1)} %shard_map.131), calls=%async_computation.7 | async-start | bytes 983040 | tf_op jit(solution)/shard_map/all_to_all | solution.py:330
  141.4 12.6 %copy-start.18 = (bf16[50]{0:T(256)(128)(2,1)S(1)}, bf16[50]{0:T(256)(128)(2,1)}, u32[]{:S(2)}) copy-start(bf16[50]{0:T(256)(128)(2,1)} %iota_convert_fusion) | copy-start | bytes 304

commit v9 on v8

--- a/solution.py
+++ b/solution.py
@@ -81,10 +81,10 @@
     lanes = shards.shape[2]
 
     def kernel(flags_ref, returned_ref, logit_ref, pull_ref, value_ref, shards_ref, out_ref):
-        scale = jnp.where(flags_ref[0] > 0, 1.0, returned_ref[...])
         square = [lax.broadcasted_iota(jnp.int32, (rows, rows), axis) for axis in (0, 1)]
-        spread = jnp.where(square[0] == square[1], logit_ref[...] * scale, 0.0)
-        grads = jnp.sum(spread, axis=1, keepdims=True)
+        scale = jnp.where(square[0] == square[1], returned_ref[...], 0.0)
+        scale = jnp.sum(scale, axis=1, keepdims=True)
+        grads = logit_ref[...] * jnp.where(flags_ref[0] > 0, 1.0, scale)
         hidden_rows = (grads * pull_ref[...]).astype(jnp.bfloat16)
         out_row = jnp.sum(grads * value_ref[...], axis=0, keepdims=True)
         place = lax.broadcasted_iota(jnp.int32, (8, hidden), 0)
@@ -102,7 +102,7 @@
         out_shape=jax.ShapeDtypeStruct((plane_count, rows + 8, hidden + lanes), jnp.bfloat16),
         in_specs=[pl.BlockSpec(memory_space=pltpu.SMEM)] + [vmem] * 5,
         out_specs=vmem,
-    )(flags, returned[None], logit[None], pull, value, shards)
+    )(flags, returned[None], logit, pull, value, shards)
 
 
 def pick_fresh(mask_row):
@@ -219,9 +219,7 @@
         sent = sent.reshape(along_count, FRESH + 1, features)
         group = sent[:, :FRESH].reshape(group_rows, features)
         pieces = sent[:, FRESH].reshape(along_count * piece, hidden)
-        half = w_up.shape[0] // 2
-        other_up = from_next(w_up[:half], 1)
-        other_up = jnp.concatenate([other_up, from_next(w_up[half:], 1)])
+        other_up = from_next(w_up, 1)
         other_down = from_next(w_down, 1)
         whole_in = from_everyone(pieces, PLANE)
         act_grad = jnp.concatenate(
@@ -263,7 +261,7 @@
         both = jnp.concatenate([scaled, tangent, numbers], axis=1).astype(jnp.bfloat16)
         both = from_everyone(both, "fsdp_0")
         stacked = jnp.concatenate([both[:, :features], both[:, features : 2 * features]])
-        numbers = both[:, 2 * features : 2 * features + 8].astype(jnp.float32).T
+        numbers = both[:, 2 * features :].astype(jnp.float32)
         pre_both = up_both(stacked, other_up)
         act, act_slope = gelu_both(pre_both[:group_rows])
         terms = down_both(act, other_down)
@@ -280,24 +278,20 @@
         routed = times(stacked, whole_in)
         value, slope, gate = gate_of(routed[:group_rows] + bias_row)
         pull = r_out[None, :] * slope
-        pull_tangent = jnp.sum(pull * routed[group_rows:], axis=1)
+        pull_tangent = jnp.sum(pull * routed[group_rows:], axis=1, keepdims=True)
         gate_own = lax.dynamic_slice_in_dim(gate, along * FRESH, FRESH)
         change = rows_second + sums[:, :features] - rows_cached
-        gate = gate[:, 0]
-        block_dot = sums[0, features : features + group_rows]
-        slope_dot = sums[1, features : features + group_rows]
-        gate_grad = numbers[0] * (numbers[3] + numbers[4] + block_dot)
+        live_group = numbers[:, :1]
+        block_dot = sums[0, features : features + group_rows][:, None]
+        slope_dot = sums[1, features : features + group_rows][:, None]
+        gate_grad = live_group * (numbers[:, 3:4] + numbers[:, 4:5] + block_dot)
         logit_grad = gate_grad * gate * (1.0 - gate)
-        input_grad = (
-            numbers[0] * gate * (numbers[5] + numbers[6] + slope_dot) + logit_grad * pull_tangent
-        )
-        even = jnp.arange(group_rows) % FRESH == 0
-        by_first = [numbers[1 + place] * input_grad for place in range(FRESH)]
-        by_first = [
-            part + jnp.where(even, jnp.roll(part, -1), jnp.roll(part, 1)) for part in by_first
-        ]
+        input_grad = live_group * gate * (
+            numbers[:, 5:6] + numbers[:, 6:7] + slope_dot
+        ) + logit_grad * pull_tangent
+        returning = (numbers[:, 1:3] * input_grad).reshape(along_count, FRESH, FRESH)
         return (
-            jnp.where(even, by_first[0], by_first[1]),
+            jnp.sum(returning, axis=1).reshape(group_rows),
             rows_cached + live * gate_own * change,
             value,
             pull,
@@ -316,7 +310,7 @@
             rows_cached + passing[:, :features],
             rows[:, hidden : 2 * hidden],
             rows[:, :hidden],
-            rows[:, 2 * hidden] + rows[:, 2 * hidden + 1],
+            rows[:, 2 * hidden : 2 * hidden + 1] + rows[:, 2 * hidden + 1 : 2 * hidden + 2],
             shards_of(columns_first),
         )
 

time: 157 us -> 151 us (0.962)
  waiting for transfers between devices: 91.1 us -> 87.6 us
  starting transfers between devices: 43 us -> 40.5 us
    ppermute x1, waiting for transfers between devices: 30.8 us -> 27.4 us  [body(): returned = lax.ppermute(returning, 'pipe', [(1, 0)])]
    all_to_all x1, starting transfers between devices: 7.44 us -> 4.95 us  [body(): lax.all_to_all(message, PLANE, split_axis=0, concat_axis=0, tiled=True)]
where the time goes in v9:
time: 151 us; the launch traced here: 150 us
  waiting for transfers between devices  87.6 us (58%)
  starting transfers between devices  40.5 us (27%)
  other arithmetic  7.57 us (5%)
  local copies, waits for them, and re-layouts  5.74 us (4%)
  matrix products  5.28 us (3%)
  Pallas kernels  1.76 us (1%)
    all_to_all x2, waiting for transfers between devices, from_everyone(): lax.all_to_all(copies, axis, split_axis=0, concat_axis=0, tiled=True)  31.5 us
    ppermute x1, waiting for transfers between devices, body(): returned = lax.ppermute(returning, 'pipe', [(1, 0)])  27.4 us
    all_to_all x2, starting transfers between devices, from_everyone(): lax.all_to_all(copies, axis, split_axis=0, concat_axis=0, tiled=True)  23.6 us
    all_to_all x1, waiting for transfers between devices, summed_on_arrival(): lax.all_to_all(blocks, axis, split_axis=0, concat_axis=0, tiled=True)  18.3 us
    all_to_all x1, waiting for transfers between devices, body(): lax.all_to_all(message, PLANE, split_axis=0, concat_axis=0, tiled=True)  10.4 us
    all_to_all x1, starting transfers between devices, summed_on_arrival(): lax.all_to_all(blocks, axis, split_axis=0, concat_axis=0, tiled=True)  6.56 us
    all_to_all x1, starting transfers between devices, body(): lax.all_to_all(message, PLANE, split_axis=0, concat_axis=0, tiled=True)  4.95 us
    dot_general x6, matrix products, times(): return jnp.dot(left, right, preferred_element_type=jnp.float32)  4.43 us
  transfers between devices with their start and end apart: 7, of which 5 were waited for; matrix products, arithmetic and copies ran while one was open for 8% of the time, Pallas kernels for 0%

profile of v9, /device:TPU:32, one launch (start us, length us, event | category | flops | bytes accessed | tf_op | source)
XLA Modules:
  0.0 150.2 jit_solution(16275000536493043061)
XLA Ops:
  0.6 2.7 %collective-permute-start.3 = (bf16[128,2560]{1,0:T(8,128)(2,1)}, bf16[128,2560]{1,0:T(8,128)(2,1)}, u32[]{:S(2)}, u32[]{:S(2)}) collective-permute-start(bf16[128,2560]{1,0:T(8,128)(2,1)} %bitcast.137), channel_id=1, source_target_pairs={{0,8},{1,9},{2,10},{3,11},{4,12},{5,13},{6,14},{7,15},{16,24},{17,... | collective-permute-start | bytes 1966088 | tf_op jit(solution)/shard_map/ppermute | solution.py:153
  3.4 0.7 fusion.94
  5.0 68.4 %conditional.2 = (f32[2,5248]{1,0:T(2,128)S(1)}, f32[2,256]{1,0:T(2,128)S(1)}, f32[2,256]{1,0:T(2,128)S(1)}, f32[2,1]{0,1:T(1,128)S(1)}, f32[2,2560]{1,0:T(2,128...) conditional(s32[]{:T(128)} %convert_element_type.114, ...), branch_computations={%region_2.7_spmd, %region_7.8_spmd} | conditional | flops 153511936 | bytes 32696736 | solution.py:234
  5.1 1.6 %fusion.106 = (f32[2]{0:T(128)S(1)}, f32[2,2560]{1,0:T(2,128)S(1)}) fusion(bf16[1,128,2560]{2,1,0:T(8,128)(2,1)} %get-tuple-element.174, f32[2,128]{1,0:T(2,128)S(1)} %get-tuple-element.85), kind=kOutput, calls=%fused_computation.207 | convolution fusion | flops 1316094 | bytes 676872 | tf_op jit(solution)/shard_map/cond/branch_0_fun/dot_general | solution.py:62
  7.0 0.9 broadcast_in_dim.64
  7.8 17.8 %all-to-all-start.5 = ((bf16[32,2,2560]{2,1,0:T(2,128)(2,1)}), bf16[32,2,2560]{2,1,0:T(2,128)(2,1)S(1)}, u32[]{:S(2)}, u32[]{:S(2)}) async-start(bf16[32,2,2560]{2,1,0:T(2,128)(2,1)} %broadcast_in_dim.64), calls=%async_computation.5 | async-start | bytes 655360 | tf_op jit(solution)/shard_map/cond/branch_0_fun/all_to_all | solution.py:22
  25.7 19.3 %all-to-all-done.5 = bf16[32,2,2560]{2,1,0:T(2,128)(2,1)S(1)} async-done(((bf16[32,2,2560]{2,1,0:T(2,128)(2,1)}), bf16[32,2,2560]{2,1,0:T(2,128)(2,1)S(1)}, u32[]{:S(2)}, u32[]{:S(2)}) %all-to-all-start.5) | async-done | bytes 327712 | tf_op jit(solution)/shard_map/cond/branch_0_fun/all_to_all | solution.py:22
  45.3 1.0 convolution_convert_fusion
  46.5 1.1 pad_maximum_fusion
  47.6 6.6 %all-to-all-start.6 = ((bf16[32,2,2816]{2,1,0:T(2,128)(2,1)}), bf16[32,2,2816]{2,1,0:T(2,128)(2,1)S(1)}, u32[]{:S(2)}, u32[]{:S(2)}) async-start(bf16[32,2,2816]{2,1,0:T(2,128)(2,1)} %pad_maximum_fusion), calls=%async_computation.6 | async-start | bytes 720896 | tf_op jit(solution)/shard_map/cond/branch_0_fun/all_to_all | solution.py:28
  54.4 18.3 %all-to-all-done.6 = bf16[32,2,2816]{2,1,0:T(2,128)(2,1)S(1)} async-done(((bf16[32,2,2816]{2,1,0:T(2,128)(2,1)}), bf16[32,2,2816]{2,1,0:T(2,128)(2,1)S(1)}, u32[]{:S(2)}, u32[]{:S(2)}) %all-to-all-start.6) | async-done | bytes 360480 | tf_op jit(solution)/shard_map/cond/branch_0_fun/all_to_all | solution.py:28
  73.5 1.3 collective-permute-start.2
  75.3 0.6 pad_maximum_fusion.11.flags_ref
  75.9 0.5 compare_bitcast_fusion.1
  76.4 1.3 fusion.95
  77.7 22.2 %conditional.3 = (f32[32]{0:T(128)}, bf16[2,2560]{1,0:T(2,128)(2,1)S(1)}, f32[32,256]{1,0:T(8,128)}, f32[32,256]{1,0:T(8,128)S(1)}, f32[32,1]{1,0:T(8,128)}, /*index=5*/bf16[2,32,128]{2,1,0:T(8,128)(2,1)}) conditional(s32[]{:T(128)} %convert_element_type.114, (f32[2,5248]{1,0:T(2,128)S(1)}, f32[2,2560]{1,0:T(2,128)S(1)}, f32[1,256]{1,0:T(1,128)}, ...), branch_computations={%region_8.9_spmd, %region_9.22_spmd} | conditional | flops 307924960 | bytes 32405166 | solution.py:317
  78.0 0.7 multiply_convert_fusion.1
  78.7 0.6 broadcast_in_dim.67
  79.4 5.8 %all-to-all-start = ((bf16[16,2,640]{2,1,0:T(2,128)(2,1)}), bf16[16,2,640]{2,1,0:T(2,128)(2,1)S(1)}, u32[]{:S(2)}, u32[]{:S(2)}) async-start(bf16[16,2,640]{2,1,0:T(2,128)(2,1)} %broadcast_in_dim.67), calls=%async_computation | async-start | bytes 81920 | tf_op jit(solution)/shard_map/cond/branch_0_fun/all_to_all | solution.py:22
  85.2 0.6 pad.18.clone
  85.8 12.2 %all-to-all-done = bf16[16,2,640]{2,1,0:T(2,128)(2,1)S(1)} async-done(((bf16[16,2,640]{2,1,0:T(2,128)(2,1)}), bf16[16,2,640]{2,1,0:T(2,128)(2,1)S(1)}, u32[]{:S(2)}, u32[]{:S(2)}) %all-to-all-start) | async-done | bytes 40992 | tf_op jit(solution)/shard_map/cond/branch_0_fun/all_to_all | solution.py:22
  98.1 0.6 fusion.104
  98.7 0.7 slice_add_fusion.3
  99.9 1.4 collective-permute-start.4
  101.4 27.4 %collective-permute-done.4 = f32[32]{0:T(128)S(1)} collective-permute-done((f32[32]{0:T(128)}, f32[32]{0:T(128)S(1)}, u32[]{:S(2)}, u32[]{:S(2)}) %collective-permute-start.4) | collective-permute-done | bytes 160 | tf_op jit(solution)/shard_map/ppermute | solution.py:321
  129.3 1.8 %shard_map.131 = bf16[16,40,384]{2,1,0:T(8,128)(2,1)} custom-call(f32[2]{0:T(128)} %pad_maximum_fusion.11.flags_ref, f32[1,32]{1,0:T(1,128)} %bitcast.161, f32[32,1]{1,0:T(8,128)} %get-tuple-element.359.logit_ref, f32[32,256]{1,0:T(8,128)S(1)} %get-tuple-element.168.pull_ref, f32[32,256]{1,0:T(8,128)} %get-tuple-element.169.value_ref, ...), custom_call_target="tpu_custom_call" | custom-call | tf_op jit(solution)/shard_map/pallas_call | solution.py:100
  131.1 4.9 %all-to-all-start.7 = ((bf16[16,40,384]{2,1,0:T(8,128)(2,1)}), bf16[16,40,384]{2,1,0:T(8,128)(2,1)S(1)}, u32[]{:S(2)}, u32[]{:S(2)}) async-start(bf16[16,40,384]{2,1,0:T(8,128)(2,1)} %shard_map.131), calls=%async_computation.7 | async-start | bytes 983040 | tf_op jit(solution)/shard_map/all_to_all | solution.py:324
  136.0 1.0 select_select_fusion
  137.0 10.4 %all-to-all-done.7 = bf16[16,40,384]{2,1,0:T(8,128)(2,1)S(1)} async-done(((bf16[16,40,384]{2,1,0:T(8,128)(2,1)}), bf16[16,40,384]{2,1,0:T(8,128)(2,1)S(1)}, u32[]{:S(2)}, u32[]{:S(2)}) %all-to-all-start.7) | async-done | bytes 491552 | tf_op jit(solution)/shard_map/all_to_all | solution.py:324
  147.5 0.8 convolution_bitcast_fusion
  148.9 0.7 copy.121
  149.6 0.6 fusion.93
  (64 shorter events, 4.7 us)
Async XLA Ops:
  0.6 4.4 %copy-start = (f32[1,50,256]{2,0,1:T(1,128)S(1)}, f32[1,50,256]{2,0,1:T(1,128)}, u32[]{:S(2)}) copy-start(f32[1,50,256]{2,0,1:T(1,128)} %param.21) | copy-start | bytes 153604
  0.6 75.8 %collective-permute-start.3 = (bf16[128,2560]{1,0:T(8,128)(2,1)}, bf16[128,2560]{1,0:T(8,128)(2,1)}, u32[]{:S(2)}, u32[]{:S(2)}) collective-permute-start(bf16[128,2560]{1,0:T(8,128)(2,1)} %bitcast.137), channel_id=1, source_target_pairs={{0,8},{1,9},{2,10},{3,11},{4,12},{5,13},{6,14},{7,15},{16,24},{17,... | collective-permute-start | bytes 1966088 | tf_op jit(solution)/shard_map/ppermute | solution.py:153
  5.0 40.0 %copy-start.13 = (bf16[80,256]{1,0:T(8,128)(2,1)S(1)}, bf16[80,256]{1,0:T(8,128)(2,1)}, u32[]{:S(2)}) copy-start(bf16[80,256]{1,0:T(8,128)(2,1)} %get-tuple-element.90) | copy-start | bytes 122884 | tf_op jit(solution)/shard_map/cond
  5.1 40.3 %copy-start.1 = (bf16[224,2560]{1,0:T(8,128)(2,1)S(1)}, bf16[224,2560]{1,0:T(8,128)(2,1)}, u32[]{:S(2)}) copy-start(bf16[224,2560]{1,0:T(8,128)(2,1)} %get-tuple-element.88) | copy-start | bytes 3440644 | tf_op jit(solution)/shard_map/cond
  5.1 40.3 %copy-start.7 = (bf16[224,2560]{1,0:T(8,128)(2,1)S(1)}, bf16[224,2560]{1,0:T(8,128)(2,1)}, u32[]{:S(2)}) copy-start(bf16[224,2560]{1,0:T(8,128)(2,1)} %get-tuple-element.87) | copy-start | bytes 3440644 | tf_op jit(solution)/shard_map/cond
  7.8 37.1 %all-to-all-start.5 = ((bf16[32,2,2560]{2,1,0:T(2,128)(2,1)}), bf16[32,2,2560]{2,1,0:T(2,128)(2,1)S(1)}, u32[]{:S(2)}, u32[]{:S(2)}) async-start(bf16[32,2,2560]{2,1,0:T(2,128)(2,1)} %broadcast_in_dim.64), calls=%async_computation.5 | async-start | bytes 655360 | tf_op jit(solution)/shard_map/cond/branch_0_fun/all_to_all | solution.py:22
  46.5 26.6 %copy-start.14 = (f32[1,256]{1,0:T(1,128)S(1)}, f32[1,256]{1,0:T(1,128)}, u32[]{:S(2)}) copy-start(f32[1,256]{1,0:T(1,128)} %get-tuple-element.92) | copy-start | bytes 3076 | tf_op jit(solution)/shard_map/cond
  46.5 26.7 %copy-start.5 = (bf16[128,2560]{1,0:T(8,128)(2,1)S(1)}, bf16[128,2560]{1,0:T(8,128)(2,1)}, u32[]{:S(2)}) copy-start(bf16[128,2560]{1,0:T(8,128)(2,1)} %get-tuple-element.93) | copy-start | bytes 1966084 | tf_op jit(solution)/shard_map/cond
  47.6 25.2 %all-to-all-start.6 = ((bf16[32,2,2816]{2,1,0:T(2,128)(2,1)}), bf16[32,2,2816]{2,1,0:T(2,128)(2,1)S(1)}, u32[]{:S(2)}, u32[]{:S(2)}) async-start(bf16[32,2,2816]{2,1,0:T(2,128)(2,1)} %pad_maximum_fusion), calls=%async_computation.6 | async-start | bytes 720896 | tf_op jit(solution)/shard_map/cond/branch_0_fun/all_to_all | solution.py:28
  73.5 4.2 %collective-permute-start.2 = (f32[2,5248]{1,0:T(2,128)S(1)}, f32[2,5248]{1,0:T(2,128)S(1)}, u32[]{:S(2)}, u32[]{:S(2)}) collective-permute-start(f32[2,5248]{1,0:T(2,128)S(1)} %get-tuple-element.153), channel_id=1, source_target_pairs={{0,8},{1,9},{2,10},{3,11},{4,12},{5,13},{6,14},{7,15},{16,24},{17,... | collective-permute-start | bytes 125960 | tf_op jit(solution)/shard_map/ppermute | solution.py:235
  79.4 18.7 %all-to-all-start = ((bf16[16,2,640]{2,1,0:T(2,128)(2,1)}), bf16[16,2,640]{2,1,0:T(2,128)(2,1)S(1)}, u32[]{:S(2)}, u32[]{:S(2)}) async-start(bf16[16,2,640]{2,1,0:T(2,128)(2,1)} %broadcast_in_dim.67), calls=%async_computation | async-start | bytes 81920 | tf_op jit(solution)/shard_map/cond/branch_0_fun/all_to_all | solution.py:22
  99.9 36.1 %copy-start.4 = (bf16[1,1,128,2560]{3,2,1,0:T(8,128)(2,1)S(1)}, bf16[1,1,128,2560]{3,2,1,0:T(8,128)(2,1)}, u32[]{:S(2)}) copy-start(bf16[1,1,128,2560]{3,2,1,0:T(8,128)(2,1)} %param.15) | copy-start | bytes 1966084
  99.9 36.1 %copy-start.18 = (pred[128]{0:T(512)(128)(4,1)S(1)}, pred[128]{0:T(512)(128)(4,1)}, u32[]{:S(2)}) copy-start(pred[128]{0:T(512)(128)(4,1)} %get-tuple-element.420) | copy-start | bytes 388
  99.9 36.1 %copy-start.19 = (pred[128]{0:T(512)(128)(4,1)S(1)}, pred[128]{0:T(512)(128)(4,1)}, u32[]{:S(2)}) copy-start(pred[128]{0:T(512)(128)(4,1)} %get-tuple-element.421) | copy-start | bytes 388
  99.9 28.9 %collective-permute-start.4 = (f32[32]{0:T(128)}, f32[32]{0:T(128)S(1)}, u32[]{:S(2)}, u32[]{:S(2)}) collective-permute-start(f32[32]{0:T(128)} %get-tuple-element.166), channel_id=1, source_target_pairs={{8,0},{9,1},{10,2},{11,3},{12,4},{13,5},{14,6},{15,7},{24,16},{25,... | collective-permute-start | bytes 392 | tf_op jit(solution)/shard_map/ppermute | solution.py:321
  128.8 0.5 copy-start.20
  131.1 16.4 %all-to-all-start.7 = ((bf16[16,40,384]{2,1,0:T(8,128)(2,1)}), bf16[16,40,384]{2,1,0:T(8,128)(2,1)S(1)}, u32[]{:S(2)}, u32[]{:S(2)}) async-start(bf16[16,40,384]{2,1,0:T(8,128)(2,1)} %shard_map.131), calls=%async_computation.7 | async-start | bytes 983040 | tf_op jit(solution)/shard_map/all_to_all | solution.py:324
  136.0 12.5 %copy-start.21 = (bf16[50]{0:T(256)(128)(2,1)S(1)}, bf16[50]{0:T(256)(128)(2,1)}, u32[]{:S(2)}) copy-start(bf16[50]{0:T(256)(128)(2,1)} %iota_convert_fusion) | copy-start | bytes 304

commit v10 on v9

--- a/solution.py
+++ b/solution.py
@@ -82,9 +82,9 @@
 
     def kernel(flags_ref, returned_ref, logit_ref, pull_ref, value_ref, shards_ref, out_ref):
         square = [lax.broadcasted_iota(jnp.int32, (rows, rows), axis) for axis in (0, 1)]
-        scale = jnp.where(square[0] == square[1], returned_ref[...], 0.0)
-        scale = jnp.sum(scale, axis=1, keepdims=True)
-        grads = logit_ref[...] * jnp.where(flags_ref[0] > 0, 1.0, scale)
+        grads = logit_ref[...] * jnp.where(flags_ref[0] > 0, 1.0, returned_ref[...])
+        grads = jnp.where(square[0] == square[1], grads, 0.0)
+        grads = jnp.sum(grads, axis=1, keepdims=True)
         hidden_rows = (grads * pull_ref[...]).astype(jnp.bfloat16)
         out_row = jnp.sum(grads * value_ref[...], axis=0, keepdims=True)
         place = lax.broadcasted_iota(jnp.int32, (8, hidden), 0)
@@ -102,7 +102,7 @@
         out_shape=jax.ShapeDtypeStruct((plane_count, rows + 8, hidden + lanes), jnp.bfloat16),
         in_specs=[pl.BlockSpec(memory_space=pltpu.SMEM)] + [vmem] * 5,
         out_specs=vmem,
-    )(flags, returned[None], logit, pull, value, shards)
+    )(flags, returned[None], logit[None], pull, value, shards)
 
 
 def pick_fresh(mask_row):
@@ -214,11 +214,9 @@
         cot_rows = rows_at(picked, out_cotangent[0])
         piece = shard_cols // dp_count
         own_piece = lax.dynamic_slice_in_dim(r_in, lax.axis_index("dp") * piece, piece)
-        sent = jnp.concatenate([cot_rows.astype(jnp.bfloat16), own_piece.reshape(1, features)])
-        sent = from_everyone(sent, "fsdp_0")
-        sent = sent.reshape(along_count, FRESH + 1, features)
-        group = sent[:, :FRESH].reshape(group_rows, features)
-        pieces = sent[:, FRESH].reshape(along_count * piece, hidden)
+        pieces = from_everyone(own_piece.reshape(1, features), "fsdp_0")
+        pieces = pieces.reshape(along_count * piece, hidden)
+        group = from_everyone(cot_rows.astype(jnp.bfloat16), "fsdp_0")
         other_up = from_next(w_up, 1)
         other_down = from_next(w_down, 1)
         whole_in = from_everyone(pieces, PLANE)
@@ -295,7 +293,7 @@
             rows_cached + live * gate_own * change,
             value,
             pull,
-            logit_grad,
+            logit_grad[:, 0],
             shards_of(columns_of(stacked[:group_rows])),
         )
 
@@ -310,7 +308,7 @@
             rows_cached + passing[:, :features],
             rows[:, hidden : 2 * hidden],
             rows[:, :hidden],
-            rows[:, 2 * hidden : 2 * hidden + 1] + rows[:, 2 * hidden + 1 : 2 * hidden + 2],
+            rows[:, 2 * hidden] + rows[:, 2 * hidden + 1],
             shards_of(columns_first),
         )
 

time: 151 us -> 163 us (1.079)
  starting transfers between devices: 40.5 us -> 53.8 us
    ppermute x1, starting transfers between devices: 1.29 us -> 12.6 us  [body(): passed = lax.ppermute(passing, 'pipe', [(0, 1)])]
    all_to_all x1, starting transfers between devices: 4.95 us -> 6.72 us  [body(): lax.all_to_all(message, PLANE, split_axis=0, concat_axis=0, tiled=True)]
  transfers between devices with their start and end apart: 7 -> 7, of which waited for: 5 -> 5; matrix products, arithmetic and copies ran while one was open for 8% -> 7% of each run, Pallas kernels for 0% -> 0%
where the time goes in v10:
time: 163 us; the launch traced here: 162 us
  waiting for transfers between devices  86.1 us (53%)
  starting transfers between devices  53.8 us (33%)
  other arithmetic  7.6 us (5%)
  local copies, waits for them, and re-layouts  5.7 us (3%)
  matrix products  5.29 us (3%)
  Pallas kernels  1.68 us (1%)
    all_to_all x2, waiting for transfers between devices, from_everyone(): lax.all_to_all(copies, axis, split_axis=0, concat_axis=0, tiled=True)  30.2 us
    ppermute x1, waiting for transfers between devices, body(): returned = lax.ppermute(returning, 'pipe', [(1, 0)])  27.1 us
    all_to_all x2, starting transfers between devices, from_everyone(): lax.all_to_all(copies, axis, split_axis=0, concat_axis=0, tiled=True)  24.4 us
    all_to_all x1, waiting for transfers between devices, summed_on_arrival(): lax.all_to_all(blocks, axis, split_axis=0, concat_axis=0, tiled=True)  18.3 us
    ppermute x1, starting transfers between devices, body(): passed = lax.ppermute(passing, 'pipe', [(0, 1)])  12.6 us
    all_to_all x1, waiting for transfers between devices, body(): lax.all_to_all(message, PLANE, split_axis=0, concat_axis=0, tiled=True)  10.4 us
    all_to_all x1, starting transfers between devices, body(): lax.all_to_all(message, PLANE, split_axis=0, concat_axis=0, tiled=True)  6.72 us
    all_to_all x1, starting transfers between devices, summed_on_arrival(): lax.all_to_all(blocks, axis, split_axis=0, concat_axis=0, tiled=True)  5.9 us
  transfers between devices with their start and end apart: 7, of which 5 were waited for; matrix products, arithmetic and copies ran while one was open for 7% of the time, Pallas kernels for 0%

profile of v10, /device:TPU:32, one launch (start us, length us, event | category | flops | bytes accessed | tf_op | source)
XLA Modules:
  0.0 161.7 jit_solution(6279956485794033675)
XLA Ops:
  0.6 2.7 %collective-permute-start.3 = (bf16[128,2560]{1,0:T(8,128)(2,1)}, bf16[128,2560]{1,0:T(8,128)(2,1)}, u32[]{:S(2)}, u32[]{:S(2)}) collective-permute-start(bf16[128,2560]{1,0:T(8,128)(2,1)} %bitcast.135), channel_id=1, source_target_pairs={{0,8},{1,9},{2,10},{3,11},{4,12},{5,13},{6,14},{7,15},{16,24},{17,... | collective-permute-start | bytes 1966088 | tf_op jit(solution)/shard_map/ppermute | solution.py:153
  3.4 0.7 fusion.95
  5.0 66.5 %conditional.2 = (f32[2,5248]{1,0:T(2,128)S(1)}, f32[2,256]{1,0:T(2,128)S(1)}, f32[2,256]{1,0:T(2,128)S(1)}, f32[2,1]{0,1:T(1,128)S(1)}, f32[2,2560]{1,0:T(2,128...) conditional(s32[]{:T(128)} %convert_element_type.114, ...), branch_computations={%region_2.7_spmd, %region_7.8_spmd} | conditional | flops 153511936 | bytes 32666056 | solution.py:232
  5.1 1.6 fusion.107
  7.0 0.9 broadcast_in_dim.67
  7.8 17.8 %all-to-all-start.3 = ((bf16[32,2,2560]{2,1,0:T(2,128)(2,1)}), bf16[32,2,2560]{2,1,0:T(2,128)(2,1)S(1)}, u32[]{:S(2)}, u32[]{:S(2)}) async-start(bf16[32,2,2560]{2,1,0:T(2,128)(2,1)} %broadcast_in_dim.67), calls=%async_computation.3 | async-start | bytes 655360 | tf_op jit(solution)/shard_map/cond/branch_0_fun/all_to_all | solution.py:22
  25.7 17.9 %all-to-all-done.3 = bf16[32,2,2560]{2,1,0:T(2,128)(2,1)S(1)} async-done(((bf16[32,2,2560]{2,1,0:T(2,128)(2,1)}), bf16[32,2,2560]{2,1,0:T(2,128)(2,1)S(1)}, u32[]{:S(2)}, u32[]{:S(2)}) %all-to-all-start.3) | async-done | bytes 327712 | tf_op jit(solution)/shard_map/cond/branch_0_fun/all_to_all | solution.py:22
  44.0 1.0 convolution_convert_fusion
  45.2 1.1 pad_maximum_fusion
  46.2 5.9 %all-to-all-start.4 = ((bf16[32,2,2816]{2,1,0:T(2,128)(2,1)}), bf16[32,2,2816]{2,1,0:T(2,128)(2,1)S(1)}, u32[]{:S(2)}, u32[]{:S(2)}) async-start(bf16[32,2,2816]{2,1,0:T(2,128)(2,1)} %pad_maximum_fusion), calls=%async_computation.4 | async-start | bytes 720896 | tf_op jit(solution)/shard_map/cond/branch_0_fun/all_to_all | solution.py:28
  52.5 18.3 %all-to-all-done.4 = bf16[32,2,2816]{2,1,0:T(2,128)(2,1)S(1)} async-done(((bf16[32,2,2816]{2,1,0:T(2,128)(2,1)}), bf16[32,2,2816]{2,1,0:T(2,128)(2,1)S(1)}, u32[]{:S(2)}, u32[]{:S(2)}) %all-to-all-start.4) | async-done | bytes 360480 | tf_op jit(solution)/shard_map/cond/branch_0_fun/all_to_all | solution.py:28
  71.5 12.6 %collective-permute-start.2 = (f32[2,5248]{1,0:T(2,128)S(1)}, f32[2,5248]{1,0:T(2,128)S(1)}, u32[]{:S(2)}, u32[]{:S(2)}) collective-permute-start(f32[2,5248]{1,0:T(2,128)S(1)} %get-tuple-element.154), channel_id=1, source_target_pairs={{0,8},{1,9},{2,10},{3,11},{4,12},{5,13},{6,14},{7,15},{16,24},{17,... | collective-permute-start | bytes 125960 | tf_op jit(solution)/shard_map/ppermute | solution.py:233
  84.6 0.6 pad_maximum_fusion.10.flags_ref
  85.2 0.5 compare_bitcast_fusion.1
  85.8 1.3 fusion.96
  87.1 23.0 %conditional.3 = (f32[32]{0:T(128)}, bf16[2,2560]{1,0:T(2,128)(2,1)S(1)}, f32[32,256]{1,0:T(8,128)}, f32[32,256]{1,0:T(8,128)S(1)}, f32[1,32]{1,0:T(1,128)}, /*index=5*/bf16[2,32,128]{2,1,0:T(8,128)(2,1)}) conditional(s32[]{:T(128)} %convert_element_type.114, (f32[2,5248]{1,0:T(2,128)S(1)}, f32[2,2560]{1,0:T(2,128)S(1)}, f32[1,256]{1,0:T(1,128)}, ...), branch_computations={%region_8.9_spmd, %region_9.22_spmd} | conditional | flops 307924960 | bytes 32404910 | solution.py:315
  87.4 0.7 multiply_convert_fusion.1
  88.0 0.6 broadcast_in_dim.86
  88.7 6.5 %all-to-all-start = ((bf16[16,2,640]{2,1,0:T(2,128)(2,1)}), bf16[16,2,640]{2,1,0:T(2,128)(2,1)S(1)}, u32[]{:S(2)}, u32[]{:S(2)}) async-start(bf16[16,2,640]{2,1,0:T(2,128)(2,1)} %broadcast_in_dim.86), calls=%async_computation | async-start | bytes 81920 | tf_op jit(solution)/shard_map/cond/branch_0_fun/all_to_all | solution.py:22
  95.3 0.6 pad.18.clone
  96.0 12.2 %all-to-all-done = bf16[16,2,640]{2,1,0:T(2,128)(2,1)S(1)} async-done(((bf16[16,2,640]{2,1,0:T(2,128)(2,1)}), bf16[16,2,640]{2,1,0:T(2,128)(2,1)S(1)}, u32[]{:S(2)}, u32[]{:S(2)}) %all-to-all-start) | async-done | bytes 40992 | tf_op jit(solution)/shard_map/cond/branch_0_fun/all_to_all | solution.py:22
  108.2 0.6 fusion.106
  108.8 0.7 fusion.34
  110.0 1.4 collective-permute-start.4
  111.5 27.1 %collective-permute-done.4 = f32[32]{0:T(128)S(1)} collective-permute-done((f32[32]{0:T(128)}, f32[32]{0:T(128)S(1)}, u32[]{:S(2)}, u32[]{:S(2)}) %collective-permute-start.4) | collective-permute-done | bytes 160 | tf_op jit(solution)/shard_map/ppermute | solution.py:319
  139.2 1.7 %shard_map.131 = bf16[16,40,384]{2,1,0:T(8,128)(2,1)} custom-call(f32[2]{0:T(128)} %pad_maximum_fusion.10.flags_ref, f32[1,32]{1,0:T(1,128)} %bitcast.161, f32[1,32]{1,0:T(1,128)} %get-tuple-element.168.logit_ref, f32[32,256]{1,0:T(8,128)S(1)} %get-tuple-element.169.pull_ref, f32[32,256]{1,0:T(8,128)} %get-tuple-element.170.value_ref, ...), custom_call_target="tpu_custom_call" | custom-call | tf_op jit(solution)/shard_map/pallas_call | solution.py:100
  140.9 6.7 %all-to-all-start.8 = ((bf16[16,40,384]{2,1,0:T(8,128)(2,1)}), bf16[16,40,384]{2,1,0:T(8,128)(2,1)S(1)}, u32[]{:S(2)}, u32[]{:S(2)}) async-start(bf16[16,40,384]{2,1,0:T(8,128)(2,1)} %shard_map.131), calls=%async_computation.8 | async-start | bytes 983040 | tf_op jit(solution)/shard_map/all_to_all | solution.py:322
  147.6 1.0 select_select_fusion
  148.6 10.4 %all-to-all-done.8 = bf16[16,40,384]{2,1,0:T(8,128)(2,1)S(1)} async-done(((bf16[16,40,384]{2,1,0:T(8,128)(2,1)}), bf16[16,40,384]{2,1,0:T(8,128)(2,1)S(1)}, u32[]{:S(2)}, u32[]{:S(2)}) %all-to-all-start.8) | async-done | bytes 491552 | tf_op jit(solution)/shard_map/all_to_all | solution.py:322
  159.1 0.8 convolution_bitcast_fusion
  160.5 0.7 copy.133
  161.1 0.6 fusion.94
  (64 shorter events, 4.6 us)
Async XLA Ops:
  0.6 4.4 %copy-start = (f32[1,50,256]{2,0,1:T(1,128)S(1)}, f32[1,50,256]{2,0,1:T(1,128)}, u32[]{:S(2)}) copy-start(f32[1,50,256]{2,0,1:T(1,128)} %param.21) | copy-start | bytes 153604
  0.6 85.1 %collective-permute-start.3 = (bf16[128,2560]{1,0:T(8,128)(2,1)}, bf16[128,2560]{1,0:T(8,128)(2,1)}, u32[]{:S(2)}, u32[]{:S(2)}) collective-permute-start(bf16[128,2560]{1,0:T(8,128)(2,1)} %bitcast.135), channel_id=1, source_target_pairs={{0,8},{1,9},{2,10},{3,11},{4,12},{5,13},{6,14},{7,15},{16,24},{17,... | collective-permute-start | bytes 1966088 | tf_op jit(solution)/shard_map/ppermute | solution.py:153
  5.0 38.7 %copy-start.13 = (bf16[80,256]{1,0:T(8,128)(2,1)S(1)}, bf16[80,256]{1,0:T(8,128)(2,1)}, u32[]{:S(2)}) copy-start(bf16[80,256]{1,0:T(8,128)(2,1)} %get-tuple-element.91) | copy-start | bytes 122884 | tf_op jit(solution)/shard_map/cond
  5.1 38.9 %copy-start.1 = (bf16[224,2560]{1,0:T(8,128)(2,1)S(1)}, bf16[224,2560]{1,0:T(8,128)(2,1)}, u32[]{:S(2)}) copy-start(bf16[224,2560]{1,0:T(8,128)(2,1)} %get-tuple-element.89) | copy-start | bytes 3440644 | tf_op jit(solution)/shard_map/cond
  5.1 38.9 %copy-start.7 = (bf16[224,2560]{1,0:T(8,128)(2,1)S(1)}, bf16[224,2560]{1,0:T(8,128)(2,1)}, u32[]{:S(2)}) copy-start(bf16[224,2560]{1,0:T(8,128)(2,1)} %get-tuple-element.88) | copy-start | bytes 3440644 | tf_op jit(solution)/shard_map/cond
  7.8 35.8 %all-to-all-start.3 = ((bf16[32,2,2560]{2,1,0:T(2,128)(2,1)}), bf16[32,2,2560]{2,1,0:T(2,128)(2,1)S(1)}, u32[]{:S(2)}, u32[]{:S(2)}) async-start(bf16[32,2,2560]{2,1,0:T(2,128)(2,1)} %broadcast_in_dim.67), calls=%async_computation.3 | async-start | bytes 655360 | tf_op jit(solution)/shard_map/cond/branch_0_fun/all_to_all | solution.py:22
  45.2 25.9 %copy-start.14 = (f32[1,256]{1,0:T(1,128)S(1)}, f32[1,256]{1,0:T(1,128)}, u32[]{:S(2)}) copy-start(f32[1,256]{1,0:T(1,128)} %get-tuple-element.93) | copy-start | bytes 3076 | tf_op jit(solution)/shard_map/cond
  45.2 26.1 %copy-start.5 = (bf16[128,2560]{1,0:T(8,128)(2,1)S(1)}, bf16[128,2560]{1,0:T(8,128)(2,1)}, u32[]{:S(2)}) copy-start(bf16[128,2560]{1,0:T(8,128)(2,1)} %get-tuple-element.94) | copy-start | bytes 1966084 | tf_op jit(solution)/shard_map/cond
  46.2 24.6 %all-to-all-start.4 = ((bf16[32,2,2816]{2,1,0:T(2,128)(2,1)}), bf16[32,2,2816]{2,1,0:T(2,128)(2,1)S(1)}, u32[]{:S(2)}, u32[]{:S(2)}) async-start(bf16[32,2,2816]{2,1,0:T(2,128)(2,1)} %pad_maximum_fusion), calls=%async_computation.4 | async-start | bytes 720896 | tf_op jit(solution)/shard_map/cond/branch_0_fun/all_to_all | solution.py:28
  71.5 15.6 %collective-permute-start.2 = (f32[2,5248]{1,0:T(2,128)S(1)}, f32[2,5248]{1,0:T(2,128)S(1)}, u32[]{:S(2)}, u32[]{:S(2)}) collective-permute-start(f32[2,5248]{1,0:T(2,128)S(1)} %get-tuple-element.154), channel_id=1, source_target_pairs={{0,8},{1,9},{2,10},{3,11},{4,12},{5,13},{6,14},{7,15},{16,24},{17,... | collective-permute-start | bytes 125960 | tf_op jit(solution)/shard_map/ppermute | solution.py:233
  88.7 19.5 %all-to-all-start = ((bf16[16,2,640]{2,1,0:T(2,128)(2,1)}), bf16[16,2,640]{2,1,0:T(2,128)(2,1)S(1)}, u32[]{:S(2)}, u32[]{:S(2)}) async-start(bf16[16,2,640]{2,1,0:T(2,128)(2,1)} %broadcast_in_dim.86), calls=%async_computation | async-start | bytes 81920 | tf_op jit(solution)/shard_map/cond/branch_0_fun/all_to_all | solution.py:22
  110.0 37.5 %copy-start.4 = (bf16[1,1,128,2560]{3,2,1,0:T(8,128)(2,1)S(1)}, bf16[1,1,128,2560]{3,2,1,0:T(8,128)(2,1)}, u32[]{:S(2)}) copy-start(bf16[1,1,128,2560]{3,2,1,0:T(8,128)(2,1)} %param.15) | copy-start | bytes 1966084
  110.0 37.6 %copy-start.18 = (pred[128]{0:T(512)(128)(4,1)S(1)}, pred[128]{0:T(512)(128)(4,1)}, u32[]{:S(2)}) copy-start(pred[128]{0:T(512)(128)(4,1)} %get-tuple-element.436) | copy-start | bytes 388
  110.0 37.6 %copy-start.19 = (pred[128]{0:T(512)(128)(4,1)S(1)}, pred[128]{0:T(512)(128)(4,1)}, u32[]{:S(2)}) copy-start(pred[128]{0:T(512)(128)(4,1)} %get-tuple-element.437) | copy-start | bytes 388
  110.0 28.6 %collective-permute-start.4 = (f32[32]{0:T(128)}, f32[32]{0:T(128)S(1)}, u32[]{:S(2)}, u32[]{:S(2)}) collective-permute-start(f32[32]{0:T(128)} %get-tuple-element.167), channel_id=1, source_target_pairs={{8,0},{9,1},{10,2},{11,3},{12,4},{13,5},{14,6},{15,7},{24,16},{25,... | collective-permute-start | bytes 392 | tf_op jit(solution)/shard_map/ppermute | solution.py:319
  138.7 0.5 copy-start.21
  140.9 18.2 %all-to-all-start.8 = ((bf16[16,40,384]{2,1,0:T(8,128)(2,1)}), bf16[16,40,384]{2,1,0:T(8,128)(2,1)S(1)}, u32[]{:S(2)}, u32[]{:S(2)}) async-start(bf16[16,40,384]{2,1,0:T(8,128)(2,1)} %shard_map.131), calls=%async_computation.8 | async-start | bytes 983040 | tf_op jit(solution)/shard_map/all_to_all | solution.py:322
  147.6 12.5 %copy-start.20 = (bf16[50]{0:T(256)(128)(2,1)S(1)}, bf16[50]{0:T(256)(128)(2,1)}, u32[]{:S(2)}) copy-start(bf16[50]{0:T(256)(128)(2,1)} %iota_convert_fusion) | copy-start | bytes 304
